TPU v7x, 256 devices: a whole 4x4x8 slice. The times are simulated.
256 devices in a mesh: dp: 8 (over z), expert: 16 (over y, x), tensor: 2 (over core).
Axes of the slice: x: 4, y: 4, z: 8, core: 2. Of those that a mesh axis runs over, the one named last changes fastest.
Arguments:
- tokens: bfloat16 [1536, 7168], P(('dp', 'expert')), may hold values from -6 to 6
- expert_ids: int32 [1536, 8], P(('dp', 'expert')), may hold values from 0 to 15, all different within a row; in each aligned block of 12 rows (0 to 11, 12 to 23, ...) at most 8 rows name the same one
- route_weights: float32 [1536, 8], P(('dp', 'expert')), may hold values from 0.1 to 1
- gate_weights: bfloat16 [16, 7168, 2048], P('expert', 'dp', 'tensor'), may hold values from -0.0625 to 0.0625
- up_weights: bfloat16 [16, 7168, 2048], P('expert', 'dp', 'tensor'), may hold values from -0.0625 to 0.0625
- down_weights: bfloat16 [16, 2048, 7168], P('expert', 'tensor', 'dp'), may hold values from -0.125 to 0.125
- shared_gate: bfloat16 [7168, 2048], P('dp', 'tensor'), may hold values from -0.0625 to 0.0625
- shared_up: bfloat16 [7168, 2048], P('dp', 'tensor'), may hold values from -0.0625 to 0.0625
- shared_down: bfloat16 [2048, 7168], P('tensor', 'dp'), may hold values from -0.125 to 0.125
Outputs:
- mixed: bfloat16 [1536, 7168], P(('dp', 'expert'))
Inputs may be any that keep to these rules, and one draw needn't show every extreme that they name: `expert_ids`: each token names 8 different experts. In the rows of one device no expert is named by more than 8 tokens, and in some device's rows some expert is named by exactly 8.
All inputs are finite; a program needn't handle non-finite values.
Results may differ from a plain program's by a relative error of at most 0.005.
Values may be sent and summed in bfloat16 or wider, within the bound.
No kernel may reach another device: no remote copies, remote signals or barrier semaphores. Data moves between devices by JAX's collectives and lax.ppermute only.
A program may use at most 128 MiB of HBM per device.

v0:
```python
import functools

import jax
import jax.numpy as jnp
from jax import lax
from jax.experimental import pallas as pl
from jax.experimental.pallas import tpu as pltpu
from jax.sharding import PartitionSpec as P

EXPERTS = 16
CAP = 8
TOP = 8
ZN = 8
TOK = 12
PADT = 16
BLOCK = 896
ROWS = EXPERTS * CAP
CHUNK = ROWS + PADT
FFH = 1024
CUT = FFH // 2
NT = 256
EXT = 128
HELD = ((0, 7, 6, 5), (4, 1, 2, 3))
EARLY = (3, 4, 5)
LATE = (6, 7, 0, 1, 2)
SCALE = 16.0
LINK = jnp.float16

PARAMS = pltpu.CompilerParams(vmem_limit_bytes=16 * 1024 * 1024)
VMEM = pl.BlockSpec(memory_space=pltpu.VMEM)
SMEM = pl.BlockSpec(memory_space=pltpu.SMEM)
SWAP = [(0, 1), (1, 0)]


def shifted(k):
    return [(i, (i + k) % ZN) for i in range(ZN)]


def paired(up, down):
    out = []
    for i in range(ZN):
        out.append((i * 2, ((i + up) % ZN) * 2))
        out.append((i * 2 + 1, ((i - down) % ZN) * 2 + 1))
    return out


def fdot(a, b):
    return jnp.dot(a, b, preferred_element_type=jnp.float32)


def prep_kernel(s_ref, x_hbm, ids_hbm, w_hbm, *refs):
    outs, (x_ref, ids_ref, w_ref, sems) = refs[:4], refs[4:]
    z, c = s_ref[0], s_ref[1]
    pairs = ((ids_hbm, ids_ref), (w_hbm, w_ref), (x_hbm, x_ref))
    copies = [pltpu.make_async_copy(a, b, sems.at[i]) for i, (a, b) in enumerate(pairs)]
    for copy in copies:
        copy.start()
    for copy in copies:
        copy.wait()
    w = w_ref[...]
    hi = w.astype(jnp.bfloat16)
    rest = w - hi.astype(jnp.float32)
    mid = rest.astype(jnp.bfloat16)
    low = (rest - mid.astype(jnp.float32)).astype(jnp.bfloat16)
    lane = lax.broadcasted_iota(jnp.int32, (TOP, EXT), 1)
    part = lax.broadcasted_iota(jnp.int32, (TOP, EXT), 0)
    ext = jnp.zeros((TOK, EXT), jnp.float32)
    for i, v in enumerate((ids_ref[...].astype(jnp.float32).astype(jnp.bfloat16), hi, mid, low)):
        spread = (lane == TOP * i + part).astype(jnp.bfloat16)
        ext = ext + lax.dot_general(v, spread, (((0,), (0,)), ((), ())), preferred_element_type=jnp.float32)
    ext = ext.astype(jnp.bfloat16)
    for j, out_ref in enumerate(outs):
        block = (z + 4 * c) % ZN if j == 0 else (z + ZN + jnp.where(c == 0, -j, j)) % ZN
        out_ref[...] = jnp.zeros((PADT, BLOCK + EXT), jnp.bfloat16)
        out_ref[:TOK, :BLOCK] = x_ref[:, pl.ds(pl.multiple_of(block * BLOCK, 128), BLOCK)]
        out_ref[:TOK, BLOCK:] = ext


def prep(s, x, ids, w):
    return pl.pallas_call(
        prep_kernel,
        out_shape=(jax.ShapeDtypeStruct((PADT, BLOCK + EXT), jnp.bfloat16),) * 4,
        in_specs=[SMEM] + [pl.BlockSpec(memory_space=pltpu.HBM)] * 3,
        out_specs=(VMEM,) * 4,
        scratch_shapes=[
            pltpu.VMEM((TOK, ZN * BLOCK), jnp.bfloat16),
            pltpu.VMEM((TOP, TOK), jnp.int32),
            pltpu.VMEM((TOP, TOK), jnp.float32),
            pltpu.SemaphoreType.DMA((3,)),
        ],
        compiler_params=PARAMS,
        name="prep",
    )(s, x, ids, w)


def pack_kernel(*refs):
    xs, (packed_ref, shared_ref, ext_ref) = refs[:4], refs[4:]
    n = 4 * PADT
    for i, x in enumerate(xs):
        shared_ref[i * PADT : (i + 1) * PADT] = x[:, :BLOCK]
        ext_ref[i * PADT : (i + 1) * PADT] = x[:, BLOCK:]
    x = shared_ref[...]
    ids = jnp.transpose(ext_ref[...].astype(jnp.float32))[:TOP, :].astype(jnp.int32)
    experts = lax.broadcasted_iota(jnp.int32, (EXPERTS, n), 0)
    row = lax.broadcasted_iota(jnp.int32, (EXPERTS, n), 1)
    member = jnp.zeros((EXPERTS, n), jnp.float32)
    for k in range(TOP):
        member = member + ((experts == ids[k : k + 1, :]) & (row % PADT < TOK)).astype(jnp.float32)
    r0 = lax.broadcasted_iota(jnp.int32, (n, n), 0)
    r1 = lax.broadcasted_iota(jnp.int32, (n, n), 1)
    before = ((r0 // PADT == r1 // PADT) & (r0 < r1)).astype(jnp.bfloat16)
    pos = fdot(member.astype(jnp.bfloat16), before).astype(jnp.int32)
    target = jnp.where(member > 0.5, row // PADT * CAP + pos, -1)
    wanted = lax.broadcasted_iota(jnp.int32, (4 * CAP, n), 0)
    for e in range(EXPERTS):
        pick = (wanted == target[e : e + 1, :]).astype(jnp.bfloat16)
        packed_ref[e] = fdot(pick, x).astype(jnp.bfloat16)


def pack(*xs):
    return pl.pallas_call(
        pack_kernel,
        out_shape=(
            jax.ShapeDtypeStruct((EXPERTS, 4 * CAP, BLOCK), jnp.bfloat16),
            jax.ShapeDtypeStruct((4 * PADT, BLOCK), jnp.bfloat16),
            jax.ShapeDtypeStruct((4 * PADT, EXT), jnp.bfloat16),
        ),
        in_specs=[VMEM] * 4,
        out_specs=(VMEM, VMEM, VMEM),
        compiler_params=PARAMS,
        name="pack",
    )(*xs)


def up_kernel(ks, c_ref, own_ref, oth_ref, so_ref, st_ref, wg_ref, wu_ref, sg_ref, su_ref, *refs):
    count = len(ks)
    out_refs, (x_ref, s_ref, full_ref) = refs[:-3], refs[-3:]

    def gather(sides):
        for at, k in enumerate(ks):
            side = 0 if k in HELD[0] else 1
            i = HELD[side].index(k)
            full, shared = sides[side]
            x_ref[at] = full[i]
            s_ref[at * PADT : (at + 1) * PADT] = shared[i * PADT : (i + 1) * PADT]

    own, oth = (own_ref, so_ref), (oth_ref, st_ref)
    start = pl.program_id(0) == 0

    @pl.when(start & (c_ref[0] == 0))
    def _():
        gather((own, oth))

    @pl.when(start & (c_ref[0] != 0))
    def _():
        gather((oth, own))

    for w_ref, v_ref, o_refs in ((wg_ref, sg_ref, out_refs[:count]), (wu_ref, su_ref, out_refs[count:])):
        shared = fdot(s_ref[...], v_ref[...]) * SCALE

        def chunk(i, carry):
            full_ref[i] = fdot(x_ref[i], w_ref[0]) * SCALE
            return carry

        lax.fori_loop(0, count, chunk, 0)
        for i in range(count):
            o_refs[i][:ROWS, :] = full_ref[i]
            o_refs[i][ROWS:, :] = shared[i * PADT : (i + 1) * PADT]


def up_dots(ks, c, own, oth, so, st, wg, wu, sg, su):
    whole = lambda *shape: pl.BlockSpec(shape, lambda n: (0,) * len(shape))
    count = len(ks)
    return pl.pallas_call(
        functools.partial(up_kernel, ks),
        grid=(FFH // NT,),
        out_shape=(jax.ShapeDtypeStruct((CHUNK, FFH), jnp.float32),) * (2 * count),
        in_specs=[
            SMEM,
            whole(4, ROWS, BLOCK),
            whole(4, ROWS, BLOCK),
            whole(4 * PADT, BLOCK),
            whole(4 * PADT, BLOCK),
            pl.BlockSpec((1, BLOCK, NT), lambda n: (0, 0, n)),
            pl.BlockSpec((1, BLOCK, NT), lambda n: (0, 0, n)),
            pl.BlockSpec((BLOCK, NT), lambda n: (0, n)),
            pl.BlockSpec((BLOCK, NT), lambda n: (0, n)),
        ],
        out_specs=(pl.BlockSpec((CHUNK, NT), lambda n: (0, n)),) * (2 * count),
        scratch_shapes=[
            pltpu.VMEM((count, ROWS, BLOCK), jnp.bfloat16),
            pltpu.VMEM((count * PADT, BLOCK), jnp.bfloat16),
            pltpu.VMEM((count, ROWS, NT), jnp.float32),
        ],
        compiler_params=PARAMS,
        cost_estimate=pl.CostEstimate(
            flops=2 * 2 * count * CHUNK * BLOCK * FFH, bytes_accessed=4 * BLOCK * FFH * 2, transcendentals=0
        ),
    )(c, own, oth, so, st, wg, wu, sg, su)


def down_kernel(c_ref, *refs):
    xs, (wd_ref, sd_ref, keep_ref, send_ref, x_ref, s_ref, full_ref) = refs[:-7], refs[-7:]
    n = len(xs) // 4
    for i in range(2 * n):
        for x, cols in zip(xs[2 * i : 2 * i + 2], (slice(0, CUT), slice(CUT, FFH))):
            x_ref[i, :, cols] = x[:ROWS]
            s_ref[i * PADT : (i + 1) * PADT, cols] = x[ROWS:]

    def chunk(i, carry):
        full_ref[i, :ROWS] = fdot(x_ref[i], wd_ref[0])
        return carry

    lax.fori_loop(0, 2 * n, chunk, 0)
    shared = fdot(s_ref[...], sd_ref[...])
    for i in range(2 * n):
        full_ref[i, ROWS:] = shared[i * PADT : (i + 1) * PADT]
    c = c_ref[0]
    for i in range(n):
        keep_ref[i] = full_ref[c * n + i]
        send_ref[i] = full_ref[(1 - c) * n + i]


def down_dots(c, xs, wd, sd):
    n = len(xs) // 4
    return pl.pallas_call(
        down_kernel,
        out_shape=(
            jax.ShapeDtypeStruct((n, CHUNK, BLOCK), jnp.float32),
            jax.ShapeDtypeStruct((n, CHUNK, BLOCK), jnp.float32),
        ),
        in_specs=[SMEM] + [VMEM] * (len(xs) + 2),
        out_specs=(VMEM, VMEM),
        scratch_shapes=[
            pltpu.VMEM((2 * n, ROWS, FFH), jnp.bfloat16),
            pltpu.VMEM((2 * n * PADT, FFH), jnp.bfloat16),
            pltpu.VMEM((2 * n, CHUNK, BLOCK), jnp.float32),
        ],
        compiler_params=PARAMS,
        cost_estimate=pl.CostEstimate(
            flops=2 * 2 * n * CHUNK * BLOCK * FFH, bytes_accessed=2 * BLOCK * FFH * 2, transcendentals=0
        ),
        name="down_dots",
    )(c, *xs, wd, sd)


def settle_kernel(keep_ref, came_ref, *refs):
    before, (rows_ref, shared_ref) = refs[:-2], refs[-2:]
    at = 0
    if before:
        at = 2 * CAP
        rows_ref[:, :at, :] = before[0][...]
    for i in range(2):
        total = keep_ref[i, :ROWS] + came_ref[i, :ROWS]
        rows_ref[:, at + i * CAP : at + (i + 1) * CAP, :] = total.reshape(EXPERTS, CAP, BLOCK).astype(jnp.bfloat16)
        shared_ref[i * PADT : (i + 1) * PADT] = keep_ref[i, ROWS:] + came_ref[i, ROWS:]


def settle(keep, came, *before):
    return pl.pallas_call(
        settle_kernel,
        out_shape=(
            jax.ShapeDtypeStruct((EXPERTS, (2 + 2 * len(before)) * CAP, BLOCK), jnp.bfloat16),
            jax.ShapeDtypeStruct((2 * PADT, BLOCK), jnp.float32),
        ),
        in_specs=[VMEM] * (2 + len(before)),
        out_specs=(VMEM, VMEM),
        compiler_params=PARAMS,
        name="settle",
    )(keep, came, *before)


def combine_kernel(ext_ref, back_ref, near_ref, far_ref, out_ref, terms_ref, total_ref):
    rows = 4 * PADT
    cols = 4 * ROWS
    ext = jnp.concatenate([ext_ref[PADT:], ext_ref[:PADT]], axis=0).astype(jnp.float32)
    weight = (ext[:, TOP : 2 * TOP] + ext[:, 2 * TOP : 3 * TOP]) + ext[:, 3 * TOP : 4 * TOP]
    column = lax.broadcasted_iota(jnp.int32, (rows, cols), 1)
    row = lax.broadcasted_iota(jnp.int32, (rows, cols), 0)
    live = (row % PADT < TOK) & (row // PADT == (column // CAP) % 4)
    owner = (column // (4 * CAP)).astype(jnp.float32)
    slot = (column % CAP).astype(jnp.float32)
    member = jnp.zeros((rows, cols), jnp.float32)
    scale = jnp.zeros((rows, cols), jnp.float32)
    for k in range(TOP):
        hit = (ext[:, k : k + 1] == owner) & live
        member = jnp.where(hit, 1.0, member)
        scale = jnp.where(hit, weight[:, k : k + 1], scale)
    i0 = lax.broadcasted_iota(jnp.int32, (rows, rows), 0)
    i1 = lax.broadcasted_iota(jnp.int32, (rows, rows), 1)
    before = ((i1 < i0) & (i0 // PADT == i1 // PADT)).astype(jnp.bfloat16)
    pos = fdot(before, member.astype(jnp.bfloat16))
    scale = jnp.where((pos == slot) & (member > 0.5), scale, 0.0)
    hi = scale.astype(jnp.bfloat16)
    rest = scale - hi.astype(jnp.float32)
    mid = rest.astype(jnp.bfloat16)
    low = (rest - mid.astype(jnp.float32)).astype(jnp.bfloat16)
    for i, term in enumerate((low, mid, hi)):
        terms_ref[i] = term
    total_ref[: 2 * PADT] = near_ref[...]
    total_ref[2 * PADT :] = far_ref[...]

    def add(i, carry):
        total_ref[...] += fdot(terms_ref[i], back_ref[...])
        return carry

    lax.fori_loop(0, 3, add, 0)
    out_ref[...] = total_ref[...].astype(jnp.bfloat16)


def combine(ext, back, near, far):
    return pl.pallas_call(
        combine_kernel,
        out_shape=jax.ShapeDtypeStruct((4 * PADT, BLOCK), jnp.bfloat16),
        in_specs=[VMEM, VMEM, VMEM, VMEM],
        out_specs=VMEM,
        scratch_shapes=[
            pltpu.VMEM((3, 4 * PADT, 4 * ROWS), jnp.bfloat16),
            pltpu.VMEM((4 * PADT, BLOCK), jnp.float32),
        ],
        compiler_params=PARAMS,
        name="combine",
    )(ext, back, near, far)


def assemble_kernel(s_ref, *refs):
    out_ref = refs[-1]
    z = s_ref[0]
    held_ref, came_ref = refs[:-1]
    a1, a2, b3, b0 = [held_ref[i * PADT : i * PADT + TOK] for i in range(4)]
    o1, o2, o3, o0 = [came_ref[i * PADT : i * PADT + TOK] for i in range(4)]

    def put(parts):
        for i, part in enumerate(parts):
            at = pl.multiple_of(((z + i) % ZN) * BLOCK, 128)
            out_ref[:, pl.ds(at, BLOCK)] = part

    @pl.when(s_ref[1] == 0)
    def _():
        put((b0, o1, o2, o3, o0, b3, a2, a1))

    @pl.when(s_ref[1] != 0)
    def _():
        put((o0, a1, a2, b3, b0, o3, o2, o1))


def assemble(s, *parts):
    return pl.pallas_call(
        assemble_kernel,
        out_shape=jax.ShapeDtypeStruct((TOK, ZN * BLOCK), jnp.bfloat16),
        in_specs=[SMEM] + [VMEM] * len(parts),
        out_specs=VMEM,
        compiler_params=PARAMS,
        name="assemble",
    )(s, *parts)


def ring(parts, shift):
    total = None
    for mine in parts:
        total = mine if total is None else mine + total.astype(jnp.float32)
        total = lax.ppermute(total.astype(LINK), "dp", shifted(shift))
    return total.astype(jnp.float32)


def layer(tokens, ids, weights, wg, wu, wd, sg, su, sd):
    z = lax.axis_index("dp")
    c = lax.axis_index("tensor")
    c1, zc = c.reshape(1), jnp.stack([z, c])
    sent = prep(zc, tokens, ids.T, weights.T)
    came = []
    for j, piece in enumerate(sent):
        came.append(lax.ppermute(piece, ("dp", "tensor"), paired(-j, -j) if j else paired(0, 4)))
    packed, shared_own, ext = pack(*came)
    arrived = lax.all_to_all(packed, "expert", 0, 0, tiled=True)
    both = jnp.concatenate([arrived.reshape(4 * ROWS, BLOCK), shared_own])
    both = lax.ppermute(both, "tensor", SWAP)
    shared_oth = both[4 * ROWS :]
    own, oth = [
        jnp.moveaxis(a.reshape(EXPERTS, 4, CAP, BLOCK), 1, 0).reshape(4, ROWS, BLOCK)
        for a in (arrived, both[: 4 * ROWS])
    ]
    args = (c1, own, oth, shared_own, shared_oth, wg, wu, sg, su)
    early = up_dots(EARLY, *args)
    late = up_dots(LATE, *args)
    gate = dict(zip(EARLY + LATE, early[: len(EARLY)] + late[: len(LATE)]))
    up = dict(zip(EARLY + LATE, early[len(EARLY) :] + late[len(LATE) :]))
    g_down = ring([gate[k] for k in (4, 3, 2, 1)], -1)
    u_up = ring([up[k] for k in (4, 5, 6, 7)], 1)
    u_down = ring([up[k] for k in (3, 2, 1)], -1)
    g_up = ring([gate[k] for k in (5, 6, 7)], 1)
    g = (gate[0] + (g_down + g_up)) * (1.0 / SCALE)
    u = (up[0] + (u_down + u_up)) * (1.0 / SCALE)
    hidden = (jax.nn.silu(g) * u).astype(jnp.bfloat16)
    top, tail = hidden[:, :CUT], hidden[:, CUT:]
    got = {0: (top, tail)}
    pd, pu, qd, qu = top, top, tail, tail
    for j in range(1, 5):
        pd = lax.ppermute(pd, "dp", shifted(-1))
        qu = lax.ppermute(qu, "dp", shifted(1))
        if j < 4:
            qd = lax.ppermute(qd, "dp", shifted(-1))
            pu = lax.ppermute(pu, "dp", shifted(1))
            got[ZN - j], got[j] = (pd, qd), (pu, qu)
        else:
            got[4] = (pd, qu)
    rows, shares = (), []
    for a, b in (((7, 6), (1, 2)), ((5, 0), (3, 4))):
        keep, send = down_dots(c1, [p for k in a + b for p in got[k]], wd, sd)
        came = lax.ppermute(send, "tensor", SWAP)
        *rows, shared = settle(keep, came, *rows)
        shares.append(shared)
    back = lax.all_to_all(rows[0], "expert", 0, 0, tiled=True).reshape(4 * ROWS, BLOCK)
    mixed = combine(ext, back, *shares)
    held = []
    for i, (to, fro) in enumerate(((1, 1), (2, 2), (3, 3), (0, 4))):
        held.append(lax.ppermute(mixed[i * PADT : (i + 1) * PADT], ("dp", "tensor"), paired(to, fro)))
    held = jnp.concatenate(held)
    others = lax.ppermute(held, "tensor", SWAP)
    return assemble(zc, held, others)


def solution(mesh):
    placed = (
        P(("dp", "expert"), None),
        P(("dp", "expert"), None),
        P(("dp", "expert"), None),
        P("expert", "dp", "tensor"),
        P("expert", "dp", "tensor"),
        P("expert", "tensor", "dp"),
        P("dp", "tensor"),
        P("dp", "tensor"),
        P("tensor", "dp"),
    )
    return jax.shard_map(layer, mesh=mesh, in_specs=placed, out_specs=P(("dp", "expert"), None), check_vma=False)
```

profile of v0, /device:TPU:1, one launch (start us, length us, event | category | flops | bytes accessed | tf_op | source)
XLA Modules:
  0.0 188.9 jit_solution(10292235578823229495)
XLA Ops:
  0.1 0.9 copy-done.6
  1.0 0.7 copy-done.7
  1.7 0.7 copy-done.8
  2.4 1.1 prep.1
  3.5 9.6 %collective-permute-start = (bf16[16,1024]{1,0:T(8,128)(2,1)S(1)}, bf16[16,1024]{1,0:T(8,128)(2,1)S(1)}, u32[]{:S(2)}, u32[]{:S(2)}) collective-permute-start(bf16[16,1024]{1,0:T(8,128)(2,1)S(1)} %get-tuple-element.36), channel_id=1, source_target_pairs={{0,0},{1,129},{32,32},{33,161},{64,64},{65,193},{96,96},{97,225},{... | collective-permute-start | bytes 98312 | tf_op jit(solution)/shard_map/ppermute | solution.py:373
  13.1 0.8 collective-permute-start.1
  13.9 1.2 collective-permute-start.2
  15.1 2.0 %collective-permute-done.1.refs_1_ = bf16[16,1024]{1,0:T(8,128)(2,1)S(1)} collective-permute-done((bf16[16,1024]{1,0:T(8,128)(2,1)S(1)}, bf16[16,1024]{1,0:T(8,128)(2,1)S(1)}, u32[]{:S(2)}, u32[]{:S(2)}) %collective-permute-start.1) | collective-permute-done | bytes 32800 | tf_op jit(solution)/shard_map/ppermute | solution.py:373
  17.2 1.7 collective-permute-done.2.refs_2_
  18.8 2.1 %collective-permute-done.3.refs_3_ = bf16[16,1024]{1,0:T(8,128)(2,1)S(1)} collective-permute-done((bf16[16,1024]{1,0:T(8,128)(2,1)S(1)}, bf16[16,1024]{1,0:T(8,128)(2,1)S(1)}, u32[]{:S(2)}, u32[]{:S(2)}) %collective-permute-start.3) | collective-permute-done | bytes 32800 | tf_op jit(solution)/shard_map/ppermute | solution.py:373
  20.9 0.6 pack.1
  21.5 21.1 %all_to_all.10 = bf16[16,32,896]{2,1,0:T(8,128)(2,1)S(1)} all-to-all(bf16[16,32,896]{2,1,0:T(8,128)(2,1)S(1)} %get-tuple-element.41), channel_id=1, replica_groups=mesh['dp'=8,'expert'=16,'tensor'=2] {'expert'}, dimensions={0} | all-to-all | bytes 1835008 | tf_op jit(solution)/shard_map/all_to_all | solution.py:375
  43.0 2.5 %collective-permute-done.4 = bf16[576,896]{1,0:T(8,128)(2,1)S(1)} collective-permute-done((bf16[576,896]{1,0:T(8,128)(2,1)S(1)}, bf16[576,896]{1,0:T(8,128)(2,1)S(1)}, u32[]{:S(2)}, u32[]{:S(2)}) %collective-permute-start.4) | collective-permute-done | bytes 1032224 | tf_op jit(solution)/shard_map/ppermute | solution.py:377
  45.7 0.2 copy-done.3
  45.9 9.0 %shard_map.92 = (f32[144,1024]{1,0:T(8,128)S(1)}, f32[144,1024]{1,0:T(8,128)S(1)}, f32[144,1024]{1,0:T(8,128)S(1)}, f32[144,1024]{1,0:T(8,128)S(1)}, f32[144,1024]{1,0:T(8,128)S(1)}, /*index=5*/f32[144,1024]{1,0:T(8,128)S(1)}) custom-call(s32[1]{0:T(128)} %bitcast.1.c_ref, bf16[4,128,896]{2,1,0:T(8,128)(2,1)S(1)} %copy_bitcast_fusion.1.own_ref, ...), custom_call_target="tpu_custom_call" | custom-call | flops 1585446912 | bytes 7340032 | tf_op jit(solution)/shard_map/pallas_call | solution.py:174
  54.9 1.9 %collective-permute-start.15 = (f16[144,1024]{1,0:T(8,128)(2,1)S(1)}, f16[144,1024]{1,0:T(8,128)(2,1)S(1)}, u32[]{:S(2)}, u32[]{:S(2)}) collective-permute-start(f16[144,1024]{1,0:T(8,128)(2,1)S(1)} %convert_element_type.107), channel_id=1, source_target_pairs={{0,32},{32,64},{64,96},{96,128},{128,160},{160,192},{192,224},{224... | collective-permute-start | bytes 884744 | tf_op jit(solution)/shard_map/ppermute | solution.py:362
  56.9 0.9 collective-permute-start.5
  57.8 13.3 %shard_map.91 = (f32[144,1024]{1,0:T(8,128)S(1)}, f32[144,1024]{1,0:T(8,128)S(1)}, f32[144,1024]{1,0:T(8,128)S(1)}, f32[144,1024]{1,0:T(8,128)S(1)}, f32[144,102...) custom-call(s32[1]{0:T(128)} %bitcast.1.c_ref, ...), custom_call_target="tpu_custom_call" | custom-call | flops 2642411520 | bytes 7340032 | tf_op jit(solution)/shard_map/pallas_call | solution.py:174
  71.1 1.2 collective-permute-start.12
  72.3 0.4 collective-permute-start.9
  72.8 0.7 collective-permute-start.16
  73.6 2.1 %collective-permute-start.6 = (f16[144,1024]{1,0:T(8,128)(2,1)S(1)}, f16[144,1024]{1,0:T(8,128)(2,1)S(1)}, u32[]{:S(2)}, u32[]{:S(2)}) collective-permute-start(f16[144,1024]{1,0:T(8,128)(2,1)S(1)} %add_convert_fusion.9), channel_id=1, source_target_pairs={{0,224},{32,0},{64,32},{96,64},{128,96},{160,128},{192,160},{224,1... | collective-permute-start | bytes 884744 | tf_op jit(solution)/shard_map/ppermute | solution.py:362
  75.7 5.2 %collective-permute-done.9 = f16[144,1024]{1,0:T(8,128)(2,1)S(1)} collective-permute-done((f16[144,1024]{1,0:T(8,128)(2,1)S(1)}, f16[144,1024]{1,0:T(8,128)(2,1)S(1)}, u32[]{:S(2)}, u32[]{:S(2)}) %collective-permute-start.9) | collective-permute-done | bytes 294944 | tf_op jit(solution)/shard_map/ppermute | solution.py:362
  81.2 2.9 %collective-permute-start.13 = (f16[144,1024]{1,0:T(8,128)(2,1)S(1)}, f16[144,1024]{1,0:T(8,128)(2,1)S(1)}, u32[]{:S(2)}, u32[]{:S(2)}) collective-permute-start(f16[144,1024]{1,0:T(8,128)(2,1)S(1)} %add_convert_fusion.4), channel_id=1, source_target_pairs={{0,224},{32,0},{64,32},{96,64},{128,96},{160,128},{192,160},{224,1... | collective-permute-start | bytes 884744 | tf_op jit(solution)/shard_map/ppermute | solution.py:362
  84.1 1.4 collective-permute-done.6
  85.5 2.1 %collective-permute-start.7 = (f16[144,1024]{1,0:T(8,128)(2,1)S(1)}, f16[144,1024]{1,0:T(8,128)(2,1)S(1)}, u32[]{:S(2)}, u32[]{:S(2)}) collective-permute-start(f16[144,1024]{1,0:T(8,128)(2,1)S(1)} %add_convert_fusion.8), channel_id=1, source_target_pairs={{0,224},{32,0},{64,32},{96,64},{128,96},{160,128},{192,160},{224,1... | collective-permute-start | bytes 884744 | tf_op jit(solution)/shard_map/ppermute | solution.py:362
  87.7 5.9 %collective-permute-done.10 = f16[144,1024]{1,0:T(8,128)(2,1)S(1)} collective-permute-done((f16[144,1024]{1,0:T(8,128)(2,1)S(1)}, f16[144,1024]{1,0:T(8,128)(2,1)S(1)}, u32[]{:S(2)}, u32[]{:S(2)}) %collective-permute-start.10) | collective-permute-done | bytes 294944 | tf_op jit(solution)/shard_map/ppermute | solution.py:362
  94.0 2.7 %collective-permute-start.14 = (f16[144,1024]{1,0:T(8,128)(2,1)S(1)}, f16[144,1024]{1,0:T(8,128)(2,1)S(1)}, u32[]{:S(2)}, u32[]{:S(2)}) collective-permute-start(f16[144,1024]{1,0:T(8,128)(2,1)S(1)} %add_convert_fusion.3), channel_id=1, source_target_pairs={{0,224},{32,0},{64,32},{96,64},{128,96},{160,128},{192,160},{224,1... | collective-permute-start | bytes 884744 | tf_op jit(solution)/shard_map/ppermute | solution.py:362
  96.7 0.8 collective-permute-done.7
  97.6 0.8 collective-permute-start.8
  98.3 9.4 %collective-permute-done.17 = f16[144,1024]{1,0:T(8,128)(2,1)S(1)} collective-permute-done((f16[144,1024]{1,0:T(8,128)(2,1)S(1)}, f16[144,1024]{1,0:T(8,128)(2,1)S(1)}, u32[]{:S(2)}, u32[]{:S(2)}) %collective-permute-start.17) | collective-permute-done | bytes 294944 | tf_op jit(solution)/shard_map/ppermute | solution.py:362
  108.0 2.2 %collective-permute-done.8 = f16[144,1024]{1,0:T(8,128)(2,1)S(1)} collective-permute-done((f16[144,1024]{1,0:T(8,128)(2,1)S(1)}, f16[144,1024]{1,0:T(8,128)(2,1)S(1)}, u32[]{:S(2)}, u32[]{:S(2)}) %collective-permute-start.8) | collective-permute-done | bytes 294944 | tf_op jit(solution)/shard_map/ppermute | solution.py:362
  110.1 4.6 %collective-permute-done.18 = f16[144,1024]{1,0:T(8,128)(2,1)S(1)} collective-permute-done((f16[144,1024]{1,0:T(8,128)(2,1)S(1)}, f16[144,1024]{1,0:T(8,128)(2,1)S(1)}, u32[]{:S(2)}, u32[]{:S(2)}) %collective-permute-start.18) | collective-permute-done | bytes 294944 | tf_op jit(solution)/shard_map/ppermute | solution.py:362
  114.7 0.4 multiply_convert_fusion
  115.2 2.7 %collective-permute-start.19 = (bf16[144,512]{1,0:T(8,128)(2,1)S(1)}, bf16[144,512]{1,0:T(8,128)(2,1)S(1)}, u32[]{:S(2)}, u32[]{:S(2)}) collective-permute-start(bf16[144,512]{1,0:T(8,128)(2,1)S(1)} %get-tuple-element.68.refs_2_), channel_id=1, source_target_pairs={{0,224},{32,0},{64,32},{96,64},{128,96},{160,128},{192,160},{224,1... | collective-permute-start | bytes 442376 | tf_op jit(solution)/shard_map/ppermute | solution.py:399
  117.9 1.4 collective-permute-start.25
  119.3 1.1 collective-permute-done.28.refs_5_
  120.4 2.7 %collective-permute-start.20 = (bf16[144,512]{1,0:T(8,128)(2,1)S(1)}, bf16[144,512]{1,0:T(8,128)(2,1)S(1)}, u32[]{:S(2)}, u32[]{:S(2)}) collective-permute-start(bf16[144,512]{1,0:T(8,128)(2,1)S(1)} %collective-permute-done.19.refs_0_), channel_id=1, source_target_pairs={{0,224},{32,0},{64,32},{96,64},{128,96},{160,128},{192,160},{224,1... | collective-permute-start | bytes 442376 | tf_op jit(solution)/shard_map/ppermute | solution.py:399
  123.1 1.6 collective-permute-start.23
  124.7 0.5 collective-permute-start.26
  125.1 1.4 collective-permute-done.29.refs_7_
  126.5 0.3 collective-permute-start.30
  126.8 3.4 %collective-permute-start.21 = (bf16[144,512]{1,0:T(8,128)(2,1)S(1)}, bf16[144,512]{1,0:T(8,128)(2,1)S(1)}, u32[]{:S(2)}, u32[]{:S(2)}) collective-permute-start(bf16[144,512]{1,0:T(8,128)(2,1)S(1)} %collective-permute-done.20.refs_2_), channel_id=1, source_target_pairs={{0,224},{32,0},{64,32},{96,64},{128,96},{160,128},{192,160},{224,1... | collective-permute-start | bytes 442376 | tf_op jit(solution)/shard_map/ppermute | solution.py:399
  130.2 2.4 %collective-permute-start.24 = (bf16[144,512]{1,0:T(8,128)(2,1)S(1)}, bf16[144,512]{1,0:T(8,128)(2,1)S(1)}, u32[]{:S(2)}, u32[]{:S(2)}) collective-permute-start(bf16[144,512]{1,0:T(8,128)(2,1)S(1)} %collective-permute-done.23.refs_3_), channel_id=1, source_target_pairs={{0,224},{32,0},{64,32},{96,64},{128,96},{160,128},{192,160},{224,1... | collective-permute-start | bytes 442376 | tf_op jit(solution)/shard_map/ppermute | solution.py:402
  132.6 0.5 collective-permute-done.30.refs_5_
  133.1 0.6 collective-permute-start.32
  133.7 0.1 collective-permute-done.21.refs_0_
  133.8 3.4 %collective-permute-start.31 = (bf16[144,512]{1,0:T(8,128)(2,1)S(1)}, bf16[144,512]{1,0:T(8,128)(2,1)S(1)}, u32[]{:S(2)}, u32[]{:S(2)}) collective-permute-start(bf16[144,512]{1,0:T(8,128)(2,1)S(1)} %collective-permute-done.21.refs_0_), channel_id=1, source_target_pairs={{0,224},{32,0},{64,32},{96,64},{128,96},{160,128},{192,160},{224,1... | collective-permute-start | bytes 442376 | tf_op jit(solution)/shard_map/ppermute | solution.py:399
  137.2 2.4 %down_dots.3 = (f32[2,144,896]{2,1,0:T(8,128)S(1)}, f32[2,144,896]{2,1,0:T(8,128)S(1)}) custom-call(s32[1]{0:T(128)} %bitcast.1.c_ref, bf16[144,512]{1,0:T(8,128)(2,1)S(1)} %collective-permute-done.19.refs_0_, bf16[144,512]{1,0:T(8,128)(2,1)S(1)} %collective-permute-done.22.refs_1_, bf16[144,512]{1,0:T(8,128)(2,1)S(1)} %collective-permute-done.20.refs_2_, ...), custom_call_target="tpu_custom_call" | custom-call | flops 1056964608 | bytes 3670016 | tf_op jit(solution)/shard_map/down_dots/pallas_call | solution.py:226
  139.7 9.3 %collective-permute-start.34 = (f32[2,144,896]{2,1,0:T(8,128)S(1)}, f32[2,144,896]{2,1,0:T(8,128)S(1)}, u32[]{:S(2)}, u32[]{:S(2)}) collective-permute-start(f32[2,144,896]{2,1,0:T(8,128)S(1)} %get-tuple-element.62), channel_id=1, source_target_pairs={{0,1},{1,0},{2,3},{3,2},{4,5},{5,4},{6,7},{7,6},{8,9},{9,8},{10,11... | collective-permute-start | bytes 3096584 | tf_op jit(solution)/shard_map/ppermute | solution.py:410
  149.0 2.4 %down_dots.2 = (f32[2,144,896]{2,1,0:T(8,128)S(1)}, f32[2,144,896]{2,1,0:T(8,128)S(1)}) custom-call(s32[1]{0:T(128)} %bitcast.1.c_ref, bf16[144,512]{1,0:T(8,128)(2,1)S(1)} %collective-permute-done.21.refs_0_, bf16[144,512]{1,0:T(8,128)(2,1)S(1)} %collective-permute-done.24.refs_1_, bf16[144,512]{1,0:T(8,128)(2,1)S(1)} %get-tuple-element.68.refs_2_, ...), custom_call_target="tpu_custom_call" | custom-call | flops 1056964608 | bytes 3670016 | tf_op jit(solution)/shard_map/down_dots/pallas_call | solution.py:226
  151.5 0.7 collective-permute-start.33
  152.1 0.1 settle.2
  152.2 2.2 %collective-permute-done.33.came_ref = f32[2,144,896]{2,1,0:T(8,128)S(1)} collective-permute-done((f32[2,144,896]{2,1,0:T(8,128)S(1)}, f32[2,144,896]{2,1,0:T(8,128)S(1)}, u32[]{:S(2)}, u32[]{:S(2)}) %collective-permute-start.33) | collective-permute-done | bytes 1032224 | tf_op jit(solution)/shard_map/ppermute | solution.py:410
  154.4 0.1 settle.3
  154.5 18.0 %all_to_all.11 = bf16[16,32,896]{2,1,0:T(8,128)(2,1)S(1)} all-to-all(bf16[16,32,896]{2,1,0:T(8,128)(2,1)S(1)} %get-tuple-element.64), channel_id=1, replica_groups=mesh['dp'=8,'expert'=16,'tensor'=2] {'expert'}, dimensions={0} | all-to-all | bytes 1835008 | tf_op jit(solution)/shard_map/all_to_all | solution.py:413
  172.5 1.3 combine.1
  173.9 3.0 %collective-permute-start.35 = (bf16[16,896]{1,0:T(8,128)(2,1)S(1)}, bf16[16,896]{1,0:T(8,128)(2,1)S(1)}, u32[]{:S(2)}, u32[]{:S(2)}) collective-permute-start(bf16[16,896]{1,0:T(8,128)(2,1)S(1)} %get-tuple-element.72), channel_id=1, source_target_pairs={{0,32},{1,225},{32,64},{33,1},{64,96},{65,33},{96,128},{97,65},{12... | collective-permute-start | bytes 86024 | tf_op jit(solution)/shard_map/ppermute | solution.py:417
  176.9 3.8 %collective-permute-start.38 = (bf16[16,896]{1,0:T(8,128)(2,1)S(1)}, bf16[16,896]{1,0:T(8,128)(2,1)S(1)}, u32[]{:S(2)}, u32[]{:S(2)}) collective-permute-start(bf16[16,896]{1,0:T(8,128)(2,1)S(1)} %get-tuple-element.69), channel_id=1, source_target_pairs={{0,0},{1,129},{32,32},{33,161},{64,64},{65,193},{96,96},{97,225},{... | collective-permute-start | bytes 86024 | tf_op jit(solution)/shard_map/ppermute | solution.py:417
  180.7 0.9 collective-permute-start.37
  181.6 2.7 %collective-permute-start.36 = (bf16[16,896]{1,0:T(8,128)(2,1)S(1)}, bf16[16,896]{1,0:T(8,128)(2,1)S(1)}, u32[]{:S(2)}, u32[]{:S(2)}) collective-permute-start(bf16[16,896]{1,0:T(8,128)(2,1)S(1)} %get-tuple-element.71), channel_id=1, source_target_pairs={{0,64},{1,193},{32,96},{33,225},{64,128},{65,1},{96,160},{97,33},{... | collective-permute-start | bytes 86024 | tf_op jit(solution)/shard_map/ppermute | solution.py:417
  184.3 1.8 collective-permute-done.36
  186.3 1.3 collective-permute-done.39.refs_1_
  187.6 1.3 assemble.1
  (73 shorter events, 2.2 us)
Async XLA Ops:
  0.1 0.9 copy-start.6
  1.0 0.7 copy-start.7
  1.7 0.7 copy-start.8
  3.5 11.7 %collective-permute-start = (bf16[16,1024]{1,0:T(8,128)(2,1)S(1)}, bf16[16,1024]{1,0:T(8,128)(2,1)S(1)}, u32[]{:S(2)}, u32[]{:S(2)}) collective-permute-start(bf16[16,1024]{1,0:T(8,128)(2,1)S(1)} %get-tuple-element.36), channel_id=1, source_target_pairs={{0,0},{1,129},{32,32},{33,161},{64,64},{65,193},{96,96},{97,225},{... | collective-permute-start | bytes 98312 | tf_op jit(solution)/shard_map/ppermute | solution.py:373
  13.1 4.1 %collective-permute-start.1 = (bf16[16,1024]{1,0:T(8,128)(2,1)S(1)}, bf16[16,1024]{1,0:T(8,128)(2,1)S(1)}, u32[]{:S(2)}, u32[]{:S(2)}) collective-permute-start(bf16[16,1024]{1,0:T(8,128)(2,1)S(1)} %get-tuple-element.37), channel_id=1, source_target_pairs={{0,224},{1,33},{32,0},{33,65},{64,32},{65,97},{96,64},{97,129},{12... | collective-permute-start | bytes 98312 | tf_op jit(solution)/shard_map/ppermute | solution.py:373
  13.9 4.9 %collective-permute-start.2 = (bf16[16,1024]{1,0:T(8,128)(2,1)S(1)}, bf16[16,1024]{1,0:T(8,128)(2,1)S(1)}, u32[]{:S(2)}, u32[]{:S(2)}) collective-permute-start(bf16[16,1024]{1,0:T(8,128)(2,1)S(1)} %get-tuple-element.38), channel_id=1, source_target_pairs={{0,192},{1,65},{32,224},{33,97},{64,0},{65,129},{96,32},{97,161},{... | collective-permute-start | bytes 98312 | tf_op jit(solution)/shard_map/ppermute | solution.py:373
  15.1 5.8 %collective-permute-start.3 = (bf16[16,1024]{1,0:T(8,128)(2,1)S(1)}, bf16[16,1024]{1,0:T(8,128)(2,1)S(1)}, u32[]{:S(2)}, u32[]{:S(2)}) collective-permute-start(bf16[16,1024]{1,0:T(8,128)(2,1)S(1)} %get-tuple-element.39), channel_id=1, source_target_pairs={{0,160},{1,97},{32,192},{33,129},{64,224},{65,161},{96,0},{97,193}... | collective-permute-start | bytes 98312 | tf_op jit(solution)/shard_map/ppermute | solution.py:373
  42.6 3.0 %copy-start.5 = (bf16[896,1024]{1,0:T(8,128)(2,1)S(1)}, bf16[896,1024]{1,0:T(8,128)(2,1)}, u32[]{:S(2)}) copy-start(bf16[896,1024]{1,0:T(8,128)(2,1)} %su_ref.3) | copy-start | bytes 5505028
  42.7 2.7 %collective-permute-start.4 = (bf16[576,896]{1,0:T(8,128)(2,1)S(1)}, bf16[576,896]{1,0:T(8,128)(2,1)S(1)}, u32[]{:S(2)}, u32[]{:S(2)}) collective-permute-start(bf16[576,896]{1,0:T(8,128)(2,1)S(1)} %pad_maximum_fusion), channel_id=1, source_target_pairs={{0,1},{1,0},{2,3},{3,2},{4,5},{5,4},{6,7},{7,6},{8,9},{9,8},{10,11... | collective-permute-start | bytes 3096584 | tf_op jit(solution)/shard_map/ppermute | solution.py:377
  42.8 2.8 %copy-start.4 = (bf16[896,1024]{1,0:T(8,128)(2,1)S(1)}, bf16[896,1024]{1,0:T(8,128)(2,1)}, u32[]{:S(2)}) copy-start(bf16[896,1024]{1,0:T(8,128)(2,1)} %sg_ref.3) | copy-start | bytes 5505028
  42.9 2.7 %copy-start.2 = (bf16[1,896,1024]{2,1,0:T(8,128)(2,1)S(1)}, bf16[1,896,1024]{2,1,0:T(8,128)(2,1)}, u32[]{:S(2)}) copy-start(bf16[1,896,1024]{2,1,0:T(8,128)(2,1)} %wg_ref.3) | copy-start | bytes 5505028
  42.9 2.9 %copy-start.3 = (bf16[1,896,1024]{2,1,0:T(8,128)(2,1)S(1)}, bf16[1,896,1024]{2,1,0:T(8,128)(2,1)}, u32[]{:S(2)}) copy-start(bf16[1,896,1024]{2,1,0:T(8,128)(2,1)} %wu_ref.3) | copy-start | bytes 5505028
  54.9 17.8 %collective-permute-start.15 = (f16[144,1024]{1,0:T(8,128)(2,1)S(1)}, f16[144,1024]{1,0:T(8,128)(2,1)S(1)}, u32[]{:S(2)}, u32[]{:S(2)}) collective-permute-start(f16[144,1024]{1,0:T(8,128)(2,1)S(1)} %convert_element_type.107), channel_id=1, source_target_pairs={{0,32},{32,64},{64,96},{96,128},{128,160},{160,192},{192,224},{224... | collective-permute-start | bytes 884744 | tf_op jit(solution)/shard_map/ppermute | solution.py:362
  56.9 16.6 %collective-permute-start.5 = (f16[144,1024]{1,0:T(8,128)(2,1)S(1)}, f16[144,1024]{1,0:T(8,128)(2,1)S(1)}, u32[]{:S(2)}, u32[]{:S(2)}) collective-permute-start(f16[144,1024]{1,0:T(8,128)(2,1)S(1)} %convert_element_type.87), channel_id=1, source_target_pairs={{0,224},{32,0},{64,32},{96,64},{128,96},{160,128},{192,160},{224,1... | collective-permute-start | bytes 884744 | tf_op jit(solution)/shard_map/ppermute | solution.py:362
  71.1 9.9 %collective-permute-start.12 = (f16[144,1024]{1,0:T(8,128)(2,1)S(1)}, f16[144,1024]{1,0:T(8,128)(2,1)S(1)}, u32[]{:S(2)}, u32[]{:S(2)}) collective-permute-start(f16[144,1024]{1,0:T(8,128)(2,1)S(1)} %convert_element_type.101), channel_id=1, source_target_pairs={{0,224},{32,0},{64,32},{96,64},{128,96},{160,128},{192,160},{224,1... | collective-permute-start | bytes 884744 | tf_op jit(solution)/shard_map/ppermute | solution.py:362
  72.3 8.6 %collective-permute-start.9 = (f16[144,1024]{1,0:T(8,128)(2,1)S(1)}, f16[144,1024]{1,0:T(8,128)(2,1)S(1)}, u32[]{:S(2)}, u32[]{:S(2)}) collective-permute-start(f16[144,1024]{1,0:T(8,128)(2,1)S(1)} %convert_element_type.95), channel_id=1, source_target_pairs={{0,32},{32,64},{64,96},{96,128},{128,160},{160,192},{192,224},{224... | collective-permute-start | bytes 884744 | tf_op jit(solution)/shard_map/ppermute | solution.py:362
  72.8 20.9 %collective-permute-start.16 = (f16[144,1024]{1,0:T(8,128)(2,1)S(1)}, f16[144,1024]{1,0:T(8,128)(2,1)S(1)}, u32[]{:S(2)}, u32[]{:S(2)}) collective-permute-start(f16[144,1024]{1,0:T(8,128)(2,1)S(1)} %add_convert_fusion.2), channel_id=1, source_target_pairs={{0,32},{32,64},{64,96},{96,128},{128,160},{160,192},{192,224},{224... | collective-permute-start | bytes 884744 | tf_op jit(solution)/shard_map/ppermute | solution.py:362
  73.6 11.8 %collective-permute-start.6 = (f16[144,1024]{1,0:T(8,128)(2,1)S(1)}, f16[144,1024]{1,0:T(8,128)(2,1)S(1)}, u32[]{:S(2)}, u32[]{:S(2)}) collective-permute-start(f16[144,1024]{1,0:T(8,128)(2,1)S(1)} %add_convert_fusion.9), channel_id=1, source_target_pairs={{0,224},{32,0},{64,32},{96,64},{128,96},{160,128},{192,160},{224,1... | collective-permute-start | bytes 884744 | tf_op jit(solution)/shard_map/ppermute | solution.py:362
  81.0 12.6 %collective-permute-start.10 = (f16[144,1024]{1,0:T(8,128)(2,1)S(1)}, f16[144,1024]{1,0:T(8,128)(2,1)S(1)}, u32[]{:S(2)}, u32[]{:S(2)}) collective-permute-start(f16[144,1024]{1,0:T(8,128)(2,1)S(1)} %add_convert_fusion.6), channel_id=1, source_target_pairs={{0,32},{32,64},{64,96},{96,128},{128,160},{160,192},{192,224},{224... | collective-permute-start | bytes 884744 | tf_op jit(solution)/shard_map/ppermute | solution.py:362
  81.2 12.7 %collective-permute-start.13 = (f16[144,1024]{1,0:T(8,128)(2,1)S(1)}, f16[144,1024]{1,0:T(8,128)(2,1)S(1)}, u32[]{:S(2)}, u32[]{:S(2)}) collective-permute-start(f16[144,1024]{1,0:T(8,128)(2,1)S(1)} %add_convert_fusion.4), channel_id=1, source_target_pairs={{0,224},{32,0},{64,32},{96,64},{128,96},{160,128},{192,160},{224,1... | collective-permute-start | bytes 884744 | tf_op jit(solution)/shard_map/ppermute | solution.py:362
  85.5 12.0 %collective-permute-start.7 = (f16[144,1024]{1,0:T(8,128)(2,1)S(1)}, f16[144,1024]{1,0:T(8,128)(2,1)S(1)}, u32[]{:S(2)}, u32[]{:S(2)}) collective-permute-start(f16[144,1024]{1,0:T(8,128)(2,1)S(1)} %add_convert_fusion.8), channel_id=1, source_target_pairs={{0,224},{32,0},{64,32},{96,64},{128,96},{160,128},{192,160},{224,1... | collective-permute-start | bytes 884744 | tf_op jit(solution)/shard_map/ppermute | solution.py:362
  93.6 14.3 %collective-permute-start.11 = (f16[144,1024]{1,0:T(8,128)(2,1)S(1)}, f16[144,1024]{1,0:T(8,128)(2,1)S(1)}, u32[]{:S(2)}, u32[]{:S(2)}) collective-permute-start(f16[144,1024]{1,0:T(8,128)(2,1)S(1)} %add_convert_fusion.5), channel_id=1, source_target_pairs={{0,32},{32,64},{64,96},{96,128},{128,160},{160,192},{192,224},{224... | collective-permute-start | bytes 884744 | tf_op jit(solution)/shard_map/ppermute | solution.py:362
  93.8 13.9 %collective-permute-start.17 = (f16[144,1024]{1,0:T(8,128)(2,1)S(1)}, f16[144,1024]{1,0:T(8,128)(2,1)S(1)}, u32[]{:S(2)}, u32[]{:S(2)}) collective-permute-start(f16[144,1024]{1,0:T(8,128)(2,1)S(1)} %add_convert_fusion.1), channel_id=1, source_target_pairs={{0,32},{32,64},{64,96},{96,128},{128,160},{160,192},{192,224},{224... | collective-permute-start | bytes 884744 | tf_op jit(solution)/shard_map/ppermute | solution.py:362
  94.0 14.0 %collective-permute-start.14 = (f16[144,1024]{1,0:T(8,128)(2,1)S(1)}, f16[144,1024]{1,0:T(8,128)(2,1)S(1)}, u32[]{:S(2)}, u32[]{:S(2)}) collective-permute-start(f16[144,1024]{1,0:T(8,128)(2,1)S(1)} %add_convert_fusion.3), channel_id=1, source_target_pairs={{0,224},{32,0},{64,32},{96,64},{128,96},{160,128},{192,160},{224,1... | collective-permute-start | bytes 884744 | tf_op jit(solution)/shard_map/ppermute | solution.py:362
  97.6 12.6 %collective-permute-start.8 = (f16[144,1024]{1,0:T(8,128)(2,1)S(1)}, f16[144,1024]{1,0:T(8,128)(2,1)S(1)}, u32[]{:S(2)}, u32[]{:S(2)}) collective-permute-start(f16[144,1024]{1,0:T(8,128)(2,1)S(1)} %add_convert_fusion.7), channel_id=1, source_target_pairs={{0,224},{32,0},{64,32},{96,64},{128,96},{160,128},{192,160},{224,1... | collective-permute-start | bytes 884744 | tf_op jit(solution)/shard_map/ppermute | solution.py:362
  107.8 29.5 %copy-start.1 = (bf16[1024,896]{1,0:T(8,128)(2,1)S(1)}, bf16[1024,896]{1,0:T(8,128)(2,1)}, u32[]{:S(2)}) copy-start(bf16[1024,896]{1,0:T(8,128)(2,1)} %refs_9_.3) | copy-start | bytes 5505028
  107.8 29.4 %copy-start = (bf16[1,1024,896]{2,1,0:T(8,128)(2,1)S(1)}, bf16[1,1024,896]{2,1,0:T(8,128)(2,1)}, u32[]{:S(2)}) copy-start(bf16[1,1024,896]{2,1,0:T(8,128)(2,1)} %refs_8_.3) | copy-start | bytes 5505028
  107.9 6.9 %collective-permute-start.18 = (f16[144,1024]{1,0:T(8,128)(2,1)S(1)}, f16[144,1024]{1,0:T(8,128)(2,1)S(1)}, u32[]{:S(2)}, u32[]{:S(2)}) collective-permute-start(f16[144,1024]{1,0:T(8,128)(2,1)S(1)} %add_convert_fusion), channel_id=1, source_target_pairs={{0,32},{32,64},{64,96},{96,128},{128,160},{160,192},{192,224},{224... | collective-permute-start | bytes 884744 | tf_op jit(solution)/shard_map/ppermute | solution.py:362
  115.1 5.3 %collective-permute-start.28 = (bf16[144,512]{1,0:T(8,128)(2,1)S(1)}, bf16[144,512]{1,0:T(8,128)(2,1)S(1)}, u32[]{:S(2)}, u32[]{:S(2)}) collective-permute-start(bf16[144,512]{1,0:T(8,128)(2,1)S(1)} %get-tuple-element.67.refs_3_), channel_id=1, source_target_pairs={{0,32},{32,64},{64,96},{96,128},{128,160},{160,192},{192,224},{224... | collective-permute-start | bytes 442376 | tf_op jit(solution)/shard_map/ppermute | solution.py:400
  115.2 5.2 %collective-permute-start.19 = (bf16[144,512]{1,0:T(8,128)(2,1)S(1)}, bf16[144,512]{1,0:T(8,128)(2,1)S(1)}, u32[]{:S(2)}, u32[]{:S(2)}) collective-permute-start(bf16[144,512]{1,0:T(8,128)(2,1)S(1)} %get-tuple-element.68.refs_2_), channel_id=1, source_target_pairs={{0,224},{32,0},{64,32},{96,64},{128,96},{160,128},{192,160},{224,1... | collective-permute-start | bytes 442376 | tf_op jit(solution)/shard_map/ppermute | solution.py:399
  117.9 5.2 %collective-permute-start.22 = (bf16[144,512]{1,0:T(8,128)(2,1)S(1)}, bf16[144,512]{1,0:T(8,128)(2,1)S(1)}, u32[]{:S(2)}, u32[]{:S(2)}) collective-permute-start(bf16[144,512]{1,0:T(8,128)(2,1)S(1)} %get-tuple-element.67.refs_3_), channel_id=1, source_target_pairs={{0,224},{32,0},{64,32},{96,64},{128,96},{160,128},{192,160},{224,1... | collective-permute-start | bytes 442376 | tf_op jit(solution)/shard_map/ppermute | solution.py:402
  117.9 6.8 %collective-permute-start.25 = (bf16[144,512]{1,0:T(8,128)(2,1)S(1)}, bf16[144,512]{1,0:T(8,128)(2,1)S(1)}, u32[]{:S(2)}, u32[]{:S(2)}) collective-permute-start(bf16[144,512]{1,0:T(8,128)(2,1)S(1)} %get-tuple-element.68.refs_2_), channel_id=1, source_target_pairs={{0,32},{32,64},{64,96},{96,128},{128,160},{160,192},{192,224},{224... | collective-permute-start | bytes 442376 | tf_op jit(solution)/shard_map/ppermute | solution.py:403
  120.4 6.1 %collective-permute-start.29 = (bf16[144,512]{1,0:T(8,128)(2,1)S(1)}, bf16[144,512]{1,0:T(8,128)(2,1)S(1)}, u32[]{:S(2)}, u32[]{:S(2)}) collective-permute-start(bf16[144,512]{1,0:T(8,128)(2,1)S(1)} %collective-permute-done.28.refs_5_), channel_id=1, source_target_pairs={{0,32},{32,64},{64,96},{96,128},{128,160},{160,192},{192,224},{224... | collective-permute-start | bytes 442376 | tf_op jit(solution)/shard_map/ppermute | solution.py:400
  120.4 6.4 %collective-permute-start.20 = (bf16[144,512]{1,0:T(8,128)(2,1)S(1)}, bf16[144,512]{1,0:T(8,128)(2,1)S(1)}, u32[]{:S(2)}, u32[]{:S(2)}) collective-permute-start(bf16[144,512]{1,0:T(8,128)(2,1)S(1)} %collective-permute-done.19.refs_0_), channel_id=1, source_target_pairs={{0,224},{32,0},{64,32},{96,64},{128,96},{160,128},{192,160},{224,1... | collective-permute-start | bytes 442376 | tf_op jit(solution)/shard_map/ppermute | solution.py:399
  123.1 7.1 %collective-permute-start.23 = (bf16[144,512]{1,0:T(8,128)(2,1)S(1)}, bf16[144,512]{1,0:T(8,128)(2,1)S(1)}, u32[]{:S(2)}, u32[]{:S(2)}) collective-permute-start(bf16[144,512]{1,0:T(8,128)(2,1)S(1)} %collective-permute-done.22.refs_1_), channel_id=1, source_target_pairs={{0,224},{32,0},{64,32},{96,64},{128,96},{160,128},{192,160},{224,1... | collective-permute-start | bytes 442376 | tf_op jit(solution)/shard_map/ppermute | solution.py:402
  124.7 7.9 %collective-permute-start.26 = (bf16[144,512]{1,0:T(8,128)(2,1)S(1)}, bf16[144,512]{1,0:T(8,128)(2,1)S(1)}, u32[]{:S(2)}, u32[]{:S(2)}) collective-permute-start(bf16[144,512]{1,0:T(8,128)(2,1)S(1)} %collective-permute-done.25.refs_4_), channel_id=1, source_target_pairs={{0,32},{32,64},{64,96},{96,128},{128,160},{160,192},{192,224},{224... | collective-permute-start | bytes 442376 | tf_op jit(solution)/shard_map/ppermute | solution.py:403
  126.5 6.6 %collective-permute-start.30 = (bf16[144,512]{1,0:T(8,128)(2,1)S(1)}, bf16[144,512]{1,0:T(8,128)(2,1)S(1)}, u32[]{:S(2)}, u32[]{:S(2)}) collective-permute-start(bf16[144,512]{1,0:T(8,128)(2,1)S(1)} %collective-permute-done.29.refs_7_), channel_id=1, source_target_pairs={{0,32},{32,64},{64,96},{96,128},{128,160},{160,192},{192,224},{224... | collective-permute-start | bytes 442376 | tf_op jit(solution)/shard_map/ppermute | solution.py:400
  126.8 7.0 %collective-permute-start.21 = (bf16[144,512]{1,0:T(8,128)(2,1)S(1)}, bf16[144,512]{1,0:T(8,128)(2,1)S(1)}, u32[]{:S(2)}, u32[]{:S(2)}) collective-permute-start(bf16[144,512]{1,0:T(8,128)(2,1)S(1)} %collective-permute-done.20.refs_2_), channel_id=1, source_target_pairs={{0,224},{32,0},{64,32},{96,64},{128,96},{160,128},{192,160},{224,1... | collective-permute-start | bytes 442376 | tf_op jit(solution)/shard_map/ppermute | solution.py:399
  130.2 18.8 %collective-permute-start.24 = (bf16[144,512]{1,0:T(8,128)(2,1)S(1)}, bf16[144,512]{1,0:T(8,128)(2,1)S(1)}, u32[]{:S(2)}, u32[]{:S(2)}) collective-permute-start(bf16[144,512]{1,0:T(8,128)(2,1)S(1)} %collective-permute-done.23.refs_3_), channel_id=1, source_target_pairs={{0,224},{32,0},{64,32},{96,64},{128,96},{160,128},{192,160},{224,1... | collective-permute-start | bytes 442376 | tf_op jit(solution)/shard_map/ppermute | solution.py:402
  132.6 16.4 %collective-permute-start.27 = (bf16[144,512]{1,0:T(8,128)(2,1)S(1)}, bf16[144,512]{1,0:T(8,128)(2,1)S(1)}, u32[]{:S(2)}, u32[]{:S(2)}) collective-permute-start(bf16[144,512]{1,0:T(8,128)(2,1)S(1)} %collective-permute-done.26.refs_6_), channel_id=1, source_target_pairs={{0,32},{32,64},{64,96},{96,128},{128,160},{160,192},{192,224},{224... | collective-permute-start | bytes 442376 | tf_op jit(solution)/shard_map/ppermute | solution.py:403
  133.1 15.9 %collective-permute-start.32 = (bf16[144,512]{1,0:T(8,128)(2,1)S(1)}, bf16[144,512]{1,0:T(8,128)(2,1)S(1)}, u32[]{:S(2)}, u32[]{:S(2)}) collective-permute-start(bf16[144,512]{1,0:T(8,128)(2,1)S(1)} %collective-permute-done.30.refs_5_), channel_id=1, source_target_pairs={{0,32},{32,64},{64,96},{96,128},{128,160},{160,192},{192,224},{224... | collective-permute-start | bytes 442376 | tf_op jit(solution)/shard_map/ppermute | solution.py:400
  133.8 15.2 %collective-permute-start.31 = (bf16[144,512]{1,0:T(8,128)(2,1)S(1)}, bf16[144,512]{1,0:T(8,128)(2,1)S(1)}, u32[]{:S(2)}, u32[]{:S(2)}) collective-permute-start(bf16[144,512]{1,0:T(8,128)(2,1)S(1)} %collective-permute-done.21.refs_0_), channel_id=1, source_target_pairs={{0,224},{32,0},{64,32},{96,64},{128,96},{160,128},{192,160},{224,1... | collective-permute-start | bytes 442376 | tf_op jit(solution)/shard_map/ppermute | solution.py:399
  139.7 12.5 %collective-permute-start.34 = (f32[2,144,896]{2,1,0:T(8,128)S(1)}, f32[2,144,896]{2,1,0:T(8,128)S(1)}, u32[]{:S(2)}, u32[]{:S(2)}) collective-permute-start(f32[2,144,896]{2,1,0:T(8,128)S(1)} %get-tuple-element.62), channel_id=1, source_target_pairs={{0,1},{1,0},{2,3},{3,2},{4,5},{5,4},{6,7},{7,6},{8,9},{9,8},{10,11... | collective-permute-start | bytes 3096584 | tf_op jit(solution)/shard_map/ppermute | solution.py:410
  151.5 2.9 %collective-permute-start.33 = (f32[2,144,896]{2,1,0:T(8,128)S(1)}, f32[2,144,896]{2,1,0:T(8,128)S(1)}, u32[]{:S(2)}, u32[]{:S(2)}) collective-permute-start(f32[2,144,896]{2,1,0:T(8,128)S(1)} %get-tuple-element.60), channel_id=1, source_target_pairs={{0,1},{1,0},{2,3},{3,2},{4,5},{5,4},{6,7},{7,6},{8,9},{9,8},{10,11... | collective-permute-start | bytes 3096584 | tf_op jit(solution)/shard_map/ppermute | solution.py:410
  173.9 10.4 %collective-permute-start.35 = (bf16[16,896]{1,0:T(8,128)(2,1)S(1)}, bf16[16,896]{1,0:T(8,128)(2,1)S(1)}, u32[]{:S(2)}, u32[]{:S(2)}) collective-permute-start(bf16[16,896]{1,0:T(8,128)(2,1)S(1)} %get-tuple-element.72), channel_id=1, source_target_pairs={{0,32},{1,225},{32,64},{33,1},{64,96},{65,33},{96,128},{97,65},{12... | collective-permute-start | bytes 86024 | tf_op jit(solution)/shard_map/ppermute | solution.py:417
  176.9 9.3 %collective-permute-start.38 = (bf16[16,896]{1,0:T(8,128)(2,1)S(1)}, bf16[16,896]{1,0:T(8,128)(2,1)S(1)}, u32[]{:S(2)}, u32[]{:S(2)}) collective-permute-start(bf16[16,896]{1,0:T(8,128)(2,1)S(1)} %get-tuple-element.69), channel_id=1, source_target_pairs={{0,0},{1,129},{32,32},{33,161},{64,64},{65,193},{96,96},{97,225},{... | collective-permute-start | bytes 86024 | tf_op jit(solution)/shard_map/ppermute | solution.py:417
  180.7 5.5 %collective-permute-start.37 = (bf16[16,896]{1,0:T(8,128)(2,1)S(1)}, bf16[16,896]{1,0:T(8,128)(2,1)S(1)}, u32[]{:S(2)}, u32[]{:S(2)}) collective-permute-start(bf16[16,896]{1,0:T(8,128)(2,1)S(1)} %get-tuple-element.70), channel_id=1, source_target_pairs={{0,96},{1,161},{32,128},{33,193},{64,160},{65,225},{96,192},{97,1}... | collective-permute-start | bytes 86024 | tf_op jit(solution)/shard_map/ppermute | solution.py:417
  181.6 4.5 %collective-permute-start.36 = (bf16[16,896]{1,0:T(8,128)(2,1)S(1)}, bf16[16,896]{1,0:T(8,128)(2,1)S(1)}, u32[]{:S(2)}, u32[]{:S(2)}) collective-permute-start(bf16[16,896]{1,0:T(8,128)(2,1)S(1)} %get-tuple-element.71), channel_id=1, source_target_pairs={{0,64},{1,193},{32,96},{33,225},{64,128},{65,1},{96,160},{97,33},{... | collective-permute-start | bytes 86024 | tf_op jit(solution)/shard_map/ppermute | solution.py:417
  186.2 1.4 collective-permute-start.39
where the time goes:
time: 189 us
  starting transfers between devices  67.3 us (36%)
  waiting for transfers between devices  46 us (24%)
  blocking collectives  39.1 us (21%)
  Pallas kernels  31.6 us (17%)
  local copies, waits for them, and re-layouts  2.84 us (2%)
    ppermute x14, waiting for transfers between devices, ring(): total = lax.ppermute(total.astype(LINK), 'dp', shifted(shift))  29.3 us
    pallas_call x2, Pallas kernels, up_dots(): pl.pallas_call(functools.partial(up_kernel, ks), grid=(FFH // NT,), out_s...  22.2 us
    all_to_all x1, blocking collectives, layer(): arrived = lax.all_to_all(packed, 'expert', 0, 0, tiled=True)  21.1 us
    all_to_all x1, blocking collectives, layer(): lax.all_to_all(rows[0], 'expert', 0, 0, tiled=True).reshape(4 * ROWS, BLOCK)  18 us
    ppermute x14, starting transfers between devices, ring(): total = lax.ppermute(total.astype(LINK), 'dp', shifted(shift))  16.1 us
    ppermute x4, starting transfers between devices, layer(): pd = lax.ppermute(pd, 'dp', shifted(-1))  12.1 us
    ppermute x4, starting transfers between devices, layer(): lax.ppermute(piece, ('dp', 'tensor'), paired(-j, -j) if j else paired(0, 4))  11.6 us
    ppermute x4, starting transfers between devices, layer(): lax.ppermute(mixed[i * PADT:(i + 1) * PADT], ('dp', 'tensor'), paired(to,...  10.4 us
  transfers between devices with their start and end apart: 40, of which 18 were waited for; matrix products, arithmetic and copies ran while one was open for 1% of the time, Pallas kernels for 10%

commit v1 on v0

--- a/solution.py
+++ b/solution.py
@@ -141,7 +141,7 @@
             side = 0 if k in HELD[0] else 1
             i = HELD[side].index(k)
             full, shared = sides[side]
-            x_ref[at] = full[i]
+            x_ref[at * ROWS : (at + 1) * ROWS] = full[i]
             s_ref[at * PADT : (at + 1) * PADT] = shared[i * PADT : (i + 1) * PADT]
 
     own, oth = (own_ref, so_ref), (oth_ref, st_ref)
@@ -157,14 +157,19 @@
 
     for w_ref, v_ref, o_refs in ((wg_ref, sg_ref, out_refs[:count]), (wu_ref, su_ref, out_refs[count:])):
         shared = fdot(s_ref[...], v_ref[...]) * SCALE
-
-        def chunk(i, carry):
-            full_ref[i] = fdot(x_ref[i], w_ref[0]) * SCALE
-            return carry
-
-        lax.fori_loop(0, count, chunk, 0)
+        if count == len(EARLY):
+            full_ref[...] = fdot(x_ref[...], w_ref[0]) * SCALE
+        else:
+            half = count * ROWS // 2
+
+            def part(i, carry):
+                rows = pl.ds(pl.multiple_of(i * half, half), half)
+                full_ref[rows, :] = fdot(x_ref[rows, :], w_ref[0]) * SCALE
+                return carry
+
+            lax.fori_loop(0, 2, part, 0)
         for i in range(count):
-            o_refs[i][:ROWS, :] = full_ref[i]
+            o_refs[i][:ROWS, :] = full_ref[i * ROWS : (i + 1) * ROWS]
             o_refs[i][ROWS:, :] = shared[i * PADT : (i + 1) * PADT]
 
 
@@ -188,9 +193,9 @@
         ],
         out_specs=(pl.BlockSpec((CHUNK, NT), lambda n: (0, n)),) * (2 * count),
         scratch_shapes=[
-            pltpu.VMEM((count, ROWS, BLOCK), jnp.bfloat16),
+            pltpu.VMEM((count * ROWS, BLOCK), jnp.bfloat16),
             pltpu.VMEM((count * PADT, BLOCK), jnp.bfloat16),
-            pltpu.VMEM((count, ROWS, NT), jnp.float32),
+            pltpu.VMEM((count * ROWS, NT), jnp.float32),
         ],
         compiler_params=PARAMS,
         cost_estimate=pl.CostEstimate(

time: 189 us -> 180 us (0.952)
  Pallas kernels: 31.6 us -> 22.9 us
    pallas_call x2, Pallas kernels: 22.2 us -> 13.5 us  [up_dots(): pl.pallas_call(functools.partial(up_kernel, ks), grid=(FFH // NT,), out_s...]
  transfers between devices with their start and end apart: 40 -> 40, of which waited for: 18 -> 18; matrix products, arithmetic and copies ran while one was open for 1% -> 1% of each run, Pallas kernels for 10% -> 8%
where the time goes in v1:
time: 180 us
  starting transfers between devices  67.3 us (37%)
  waiting for transfers between devices  46 us (26%)
  blocking collectives  39.2 us (22%)
  Pallas kernels  22.9 us (13%)
  local copies, waits for them, and re-layouts  2.84 us (2%)
    ppermute x14, waiting for transfers between devices, ring(): total = lax.ppermute(total.astype(LINK), 'dp', shifted(shift))  29.3 us
    all_to_all x1, blocking collectives, layer(): arrived = lax.all_to_all(packed, 'expert', 0, 0, tiled=True)  21.1 us
    all_to_all x1, blocking collectives, layer(): lax.all_to_all(rows[0], 'expert', 0, 0, tiled=True).reshape(4 * ROWS, BLOCK)  18 us
    ppermute x14, starting transfers between devices, ring(): total = lax.ppermute(total.astype(LINK), 'dp', shifted(shift))  16 us
    pallas_call x2, Pallas kernels, up_dots(): pl.pallas_call(functools.partial(up_kernel, ks), grid=(FFH // NT,), out_s...  13.5 us
    ppermute x4, starting transfers between devices, layer(): pd = lax.ppermute(pd, 'dp', shifted(-1))  12.1 us
    ppermute x4, starting transfers between devices, layer(): lax.ppermute(piece, ('dp', 'tensor'), paired(-j, -j) if j else paired(0, 4))  11.6 us
    ppermute x4, starting transfers between devices, layer(): lax.ppermute(mixed[i * PADT:(i + 1) * PADT], ('dp', 'tensor'), paired(to,...  10.4 us
  transfers between devices with their start and end apart: 40, of which 18 were waited for; matrix products, arithmetic and copies ran while one was open for 1% of the time, Pallas kernels for 8%

profile of v1, /device:TPU:1, one launch (start us, length us, event | category | flops | bytes accessed | tf_op | source)
XLA Modules:
  0.0 180.2 jit_solution(2934860764729199543)
XLA Ops:
  0.1 0.9 copy-done.6
  1.0 0.7 copy-done.7
  1.7 0.7 copy-done.8
  2.4 1.1 prep.1
  3.5 9.6 %collective-permute-start = (bf16[16,1024]{1,0:T(8,128)(2,1)S(1)}, bf16[16,1024]{1,0:T(8,128)(2,1)S(1)}, u32[]{:S(2)}, u32[]{:S(2)}) collective-permute-start(bf16[16,1024]{1,0:T(8,128)(2,1)S(1)} %get-tuple-element.36), channel_id=1, source_target_pairs={{0,0},{1,129},{32,32},{33,161},{64,64},{65,193},{96,96},{97,225},{... | collective-permute-start | bytes 98312 | tf_op jit(solution)/shard_map/ppermute | solution.py:378
  13.1 0.8 collective-permute-start.1
  13.9 1.2 collective-permute-start.2
  15.1 2.0 %collective-permute-done.1.refs_1_ = bf16[16,1024]{1,0:T(8,128)(2,1)S(1)} collective-permute-done((bf16[16,1024]{1,0:T(8,128)(2,1)S(1)}, bf16[16,1024]{1,0:T(8,128)(2,1)S(1)}, u32[]{:S(2)}, u32[]{:S(2)}) %collective-permute-start.1) | collective-permute-done | bytes 32800 | tf_op jit(solution)/shard_map/ppermute | solution.py:378
  17.2 1.7 collective-permute-done.2.refs_2_
  18.8 2.1 %collective-permute-done.3.refs_3_ = bf16[16,1024]{1,0:T(8,128)(2,1)S(1)} collective-permute-done((bf16[16,1024]{1,0:T(8,128)(2,1)S(1)}, bf16[16,1024]{1,0:T(8,128)(2,1)S(1)}, u32[]{:S(2)}, u32[]{:S(2)}) %collective-permute-start.3) | collective-permute-done | bytes 32800 | tf_op jit(solution)/shard_map/ppermute | solution.py:378
  20.9 0.6 pack.1
  21.5 21.1 %all_to_all.10 = bf16[16,32,896]{2,1,0:T(8,128)(2,1)S(1)} all-to-all(bf16[16,32,896]{2,1,0:T(8,128)(2,1)S(1)} %get-tuple-element.41), channel_id=1, replica_groups=mesh['dp'=8,'expert'=16,'tensor'=2] {'expert'}, dimensions={0} | all-to-all | bytes 1835008 | tf_op jit(solution)/shard_map/all_to_all | solution.py:380
  43.0 2.5 %collective-permute-done.4 = bf16[576,896]{1,0:T(8,128)(2,1)S(1)} collective-permute-done((bf16[576,896]{1,0:T(8,128)(2,1)S(1)}, bf16[576,896]{1,0:T(8,128)(2,1)S(1)}, u32[]{:S(2)}, u32[]{:S(2)}) %collective-permute-start.4) | collective-permute-done | bytes 1032224 | tf_op jit(solution)/shard_map/ppermute | solution.py:382
  45.7 0.2 copy-done.3
  45.9 4.2 %shard_map.92 = (f32[144,1024]{1,0:T(8,128)S(1)}, f32[144,1024]{1,0:T(8,128)S(1)}, f32[144,1024]{1,0:T(8,128)S(1)}, f32[144,1024]{1,0:T(8,128)S(1)}, f32[144,1024]{1,0:T(8,128)S(1)}, /*index=5*/f32[144,1024]{1,0:T(8,128)S(1)}) custom-call(s32[1]{0:T(128)} %bitcast.1.c_ref, bf16[4,128,896]{2,1,0:T(8,128)(2,1)S(1)} %copy_bitcast_fusion.1.own_ref, ...), custom_call_target="tpu_custom_call" | custom-call | flops 1585446912 | bytes 7340032 | tf_op jit(solution)/shard_map/pallas_call | solution.py:179
  50.2 1.9 %collective-permute-start.15 = (f16[144,1024]{1,0:T(8,128)(2,1)S(1)}, f16[144,1024]{1,0:T(8,128)(2,1)S(1)}, u32[]{:S(2)}, u32[]{:S(2)}) collective-permute-start(f16[144,1024]{1,0:T(8,128)(2,1)S(1)} %convert_element_type.107), channel_id=1, source_target_pairs={{0,32},{32,64},{64,96},{96,128},{128,160},{160,192},{192,224},{224... | collective-permute-start | bytes 884744 | tf_op jit(solution)/shard_map/ppermute | solution.py:367
  52.1 0.9 collective-permute-start.5
  53.0 9.3 %shard_map.91 = (f32[144,1024]{1,0:T(8,128)S(1)}, f32[144,1024]{1,0:T(8,128)S(1)}, f32[144,1024]{1,0:T(8,128)S(1)}, f32[144,1024]{1,0:T(8,128)S(1)}, f32[144,102...) custom-call(s32[1]{0:T(128)} %bitcast.1.c_ref, ...), custom_call_target="tpu_custom_call" | custom-call | flops 2642411520 | bytes 7340032 | tf_op jit(solution)/shard_map/pallas_call | solution.py:179
  62.4 1.1 collective-permute-start.12
  63.5 0.4 collective-permute-start.9
  64.1 0.7 collective-permute-start.16
  64.9 2.1 %collective-permute-start.6 = (f16[144,1024]{1,0:T(8,128)(2,1)S(1)}, f16[144,1024]{1,0:T(8,128)(2,1)S(1)}, u32[]{:S(2)}, u32[]{:S(2)}) collective-permute-start(f16[144,1024]{1,0:T(8,128)(2,1)S(1)} %add_convert_fusion.9), channel_id=1, source_target_pairs={{0,224},{32,0},{64,32},{96,64},{128,96},{160,128},{192,160},{224,1... | collective-permute-start | bytes 884744 | tf_op jit(solution)/shard_map/ppermute | solution.py:367
  67.0 5.1 %collective-permute-done.9 = f16[144,1024]{1,0:T(8,128)(2,1)S(1)} collective-permute-done((f16[144,1024]{1,0:T(8,128)(2,1)S(1)}, f16[144,1024]{1,0:T(8,128)(2,1)S(1)}, u32[]{:S(2)}, u32[]{:S(2)}) %collective-permute-start.9) | collective-permute-done | bytes 294944 | tf_op jit(solution)/shard_map/ppermute | solution.py:367
  72.2 0.3 collective-permute-start.10
  72.6 2.7 %collective-permute-start.13 = (f16[144,1024]{1,0:T(8,128)(2,1)S(1)}, f16[144,1024]{1,0:T(8,128)(2,1)S(1)}, u32[]{:S(2)}, u32[]{:S(2)}) collective-permute-start(f16[144,1024]{1,0:T(8,128)(2,1)S(1)} %add_convert_fusion.4), channel_id=1, source_target_pairs={{0,224},{32,0},{64,32},{96,64},{128,96},{160,128},{192,160},{224,1... | collective-permute-start | bytes 884744 | tf_op jit(solution)/shard_map/ppermute | solution.py:367
  75.3 1.4 collective-permute-done.6
  76.8 2.1 %collective-permute-start.7 = (f16[144,1024]{1,0:T(8,128)(2,1)S(1)}, f16[144,1024]{1,0:T(8,128)(2,1)S(1)}, u32[]{:S(2)}, u32[]{:S(2)}) collective-permute-start(f16[144,1024]{1,0:T(8,128)(2,1)S(1)} %add_convert_fusion.8), channel_id=1, source_target_pairs={{0,224},{32,0},{64,32},{96,64},{128,96},{160,128},{192,160},{224,1... | collective-permute-start | bytes 884744 | tf_op jit(solution)/shard_map/ppermute | solution.py:367
  78.9 5.9 %collective-permute-done.10 = f16[144,1024]{1,0:T(8,128)(2,1)S(1)} collective-permute-done((f16[144,1024]{1,0:T(8,128)(2,1)S(1)}, f16[144,1024]{1,0:T(8,128)(2,1)S(1)}, u32[]{:S(2)}, u32[]{:S(2)}) %collective-permute-start.10) | collective-permute-done | bytes 294944 | tf_op jit(solution)/shard_map/ppermute | solution.py:367
  85.3 2.7 %collective-permute-start.14 = (f16[144,1024]{1,0:T(8,128)(2,1)S(1)}, f16[144,1024]{1,0:T(8,128)(2,1)S(1)}, u32[]{:S(2)}, u32[]{:S(2)}) collective-permute-start(f16[144,1024]{1,0:T(8,128)(2,1)S(1)} %add_convert_fusion.3), channel_id=1, source_target_pairs={{0,224},{32,0},{64,32},{96,64},{128,96},{160,128},{192,160},{224,1... | collective-permute-start | bytes 884744 | tf_op jit(solution)/shard_map/ppermute | solution.py:367
  88.0 0.8 collective-permute-done.7
  88.8 0.8 collective-permute-start.8
  89.6 9.4 %collective-permute-done.17 = f16[144,1024]{1,0:T(8,128)(2,1)S(1)} collective-permute-done((f16[144,1024]{1,0:T(8,128)(2,1)S(1)}, f16[144,1024]{1,0:T(8,128)(2,1)S(1)}, u32[]{:S(2)}, u32[]{:S(2)}) %collective-permute-start.17) | collective-permute-done | bytes 294944 | tf_op jit(solution)/shard_map/ppermute | solution.py:367
  99.2 2.2 %collective-permute-done.8 = f16[144,1024]{1,0:T(8,128)(2,1)S(1)} collective-permute-done((f16[144,1024]{1,0:T(8,128)(2,1)S(1)}, f16[144,1024]{1,0:T(8,128)(2,1)S(1)}, u32[]{:S(2)}, u32[]{:S(2)}) %collective-permute-start.8) | collective-permute-done | bytes 294944 | tf_op jit(solution)/shard_map/ppermute | solution.py:367
  101.4 4.6 %collective-permute-done.18 = f16[144,1024]{1,0:T(8,128)(2,1)S(1)} collective-permute-done((f16[144,1024]{1,0:T(8,128)(2,1)S(1)}, f16[144,1024]{1,0:T(8,128)(2,1)S(1)}, u32[]{:S(2)}, u32[]{:S(2)}) %collective-permute-start.18) | collective-permute-done | bytes 294944 | tf_op jit(solution)/shard_map/ppermute | solution.py:367
  106.0 0.4 multiply_convert_fusion
  106.5 2.7 %collective-permute-start.19 = (bf16[144,512]{1,0:T(8,128)(2,1)S(1)}, bf16[144,512]{1,0:T(8,128)(2,1)S(1)}, u32[]{:S(2)}, u32[]{:S(2)}) collective-permute-start(bf16[144,512]{1,0:T(8,128)(2,1)S(1)} %get-tuple-element.68.refs_2_), channel_id=1, source_target_pairs={{0,224},{32,0},{64,32},{96,64},{128,96},{160,128},{192,160},{224,1... | collective-permute-start | bytes 442376 | tf_op jit(solution)/shard_map/ppermute | solution.py:404
  109.1 1.4 collective-permute-start.25
  110.6 1.1 collective-permute-done.28.refs_5_
  111.7 2.7 %collective-permute-start.20 = (bf16[144,512]{1,0:T(8,128)(2,1)S(1)}, bf16[144,512]{1,0:T(8,128)(2,1)S(1)}, u32[]{:S(2)}, u32[]{:S(2)}) collective-permute-start(bf16[144,512]{1,0:T(8,128)(2,1)S(1)} %collective-permute-done.19.refs_0_), channel_id=1, source_target_pairs={{0,224},{32,0},{64,32},{96,64},{128,96},{160,128},{192,160},{224,1... | collective-permute-start | bytes 442376 | tf_op jit(solution)/shard_map/ppermute | solution.py:404
  114.3 1.6 collective-permute-start.23
  115.9 0.5 collective-permute-start.26
  116.4 1.4 collective-permute-done.29.refs_7_
  117.7 0.3 collective-permute-start.30
  118.0 3.4 %collective-permute-start.21 = (bf16[144,512]{1,0:T(8,128)(2,1)S(1)}, bf16[144,512]{1,0:T(8,128)(2,1)S(1)}, u32[]{:S(2)}, u32[]{:S(2)}) collective-permute-start(bf16[144,512]{1,0:T(8,128)(2,1)S(1)} %collective-permute-done.20.refs_2_), channel_id=1, source_target_pairs={{0,224},{32,0},{64,32},{96,64},{128,96},{160,128},{192,160},{224,1... | collective-permute-start | bytes 442376 | tf_op jit(solution)/shard_map/ppermute | solution.py:404
  121.4 2.4 %collective-permute-start.24 = (bf16[144,512]{1,0:T(8,128)(2,1)S(1)}, bf16[144,512]{1,0:T(8,128)(2,1)S(1)}, u32[]{:S(2)}, u32[]{:S(2)}) collective-permute-start(bf16[144,512]{1,0:T(8,128)(2,1)S(1)} %collective-permute-done.23.refs_3_), channel_id=1, source_target_pairs={{0,224},{32,0},{64,32},{96,64},{128,96},{160,128},{192,160},{224,1... | collective-permute-start | bytes 442376 | tf_op jit(solution)/shard_map/ppermute | solution.py:407
  123.9 0.5 collective-permute-done.30.refs_5_
  124.4 0.6 collective-permute-start.32
  125.1 3.4 %collective-permute-start.31 = (bf16[144,512]{1,0:T(8,128)(2,1)S(1)}, bf16[144,512]{1,0:T(8,128)(2,1)S(1)}, u32[]{:S(2)}, u32[]{:S(2)}) collective-permute-start(bf16[144,512]{1,0:T(8,128)(2,1)S(1)} %collective-permute-done.21.refs_0_), channel_id=1, source_target_pairs={{0,224},{32,0},{64,32},{96,64},{128,96},{160,128},{192,160},{224,1... | collective-permute-start | bytes 442376 | tf_op jit(solution)/shard_map/ppermute | solution.py:404
  128.5 2.4 %down_dots.3 = (f32[2,144,896]{2,1,0:T(8,128)S(1)}, f32[2,144,896]{2,1,0:T(8,128)S(1)}) custom-call(s32[1]{0:T(128)} %bitcast.1.c_ref, bf16[144,512]{1,0:T(8,128)(2,1)S(1)} %collective-permute-done.19.refs_0_, bf16[144,512]{1,0:T(8,128)(2,1)S(1)} %collective-permute-done.22.refs_1_, bf16[144,512]{1,0:T(8,128)(2,1)S(1)} %collective-permute-done.20.refs_2_, ...), custom_call_target="tpu_custom_call" | custom-call | flops 1056964608 | bytes 3670016 | tf_op jit(solution)/shard_map/down_dots/pallas_call | solution.py:231
  130.9 9.3 %collective-permute-start.34 = (f32[2,144,896]{2,1,0:T(8,128)S(1)}, f32[2,144,896]{2,1,0:T(8,128)S(1)}, u32[]{:S(2)}, u32[]{:S(2)}) collective-permute-start(f32[2,144,896]{2,1,0:T(8,128)S(1)} %get-tuple-element.62), channel_id=1, source_target_pairs={{0,1},{1,0},{2,3},{3,2},{4,5},{5,4},{6,7},{7,6},{8,9},{9,8},{10,11... | collective-permute-start | bytes 3096584 | tf_op jit(solution)/shard_map/ppermute | solution.py:415
  140.3 2.4 %down_dots.2 = (f32[2,144,896]{2,1,0:T(8,128)S(1)}, f32[2,144,896]{2,1,0:T(8,128)S(1)}) custom-call(s32[1]{0:T(128)} %bitcast.1.c_ref, bf16[144,512]{1,0:T(8,128)(2,1)S(1)} %collective-permute-done.21.refs_0_, bf16[144,512]{1,0:T(8,128)(2,1)S(1)} %collective-permute-done.24.refs_1_, bf16[144,512]{1,0:T(8,128)(2,1)S(1)} %get-tuple-element.68.refs_2_, ...), custom_call_target="tpu_custom_call" | custom-call | flops 1056964608 | bytes 3670016 | tf_op jit(solution)/shard_map/down_dots/pallas_call | solution.py:231
  142.7 0.6 collective-permute-start.33
  143.4 0.1 settle.2
  143.5 2.2 %collective-permute-done.33.came_ref = f32[2,144,896]{2,1,0:T(8,128)S(1)} collective-permute-done((f32[2,144,896]{2,1,0:T(8,128)S(1)}, f32[2,144,896]{2,1,0:T(8,128)S(1)}, u32[]{:S(2)}, u32[]{:S(2)}) %collective-permute-start.33) | collective-permute-done | bytes 1032224 | tf_op jit(solution)/shard_map/ppermute | solution.py:415
  145.6 0.1 settle.3
  145.8 18.0 %all_to_all.11 = bf16[16,32,896]{2,1,0:T(8,128)(2,1)S(1)} all-to-all(bf16[16,32,896]{2,1,0:T(8,128)(2,1)S(1)} %get-tuple-element.64), channel_id=1, replica_groups=mesh['dp'=8,'expert'=16,'tensor'=2] {'expert'}, dimensions={0} | all-to-all | bytes 1835008 | tf_op jit(solution)/shard_map/all_to_all | solution.py:418
  163.8 1.3 combine.1
  165.2 3.0 %collective-permute-start.35 = (bf16[16,896]{1,0:T(8,128)(2,1)S(1)}, bf16[16,896]{1,0:T(8,128)(2,1)S(1)}, u32[]{:S(2)}, u32[]{:S(2)}) collective-permute-start(bf16[16,896]{1,0:T(8,128)(2,1)S(1)} %get-tuple-element.72), channel_id=1, source_target_pairs={{0,32},{1,225},{32,64},{33,1},{64,96},{65,33},{96,128},{97,65},{12... | collective-permute-start | bytes 86024 | tf_op jit(solution)/shard_map/ppermute | solution.py:422
  168.2 3.8 %collective-permute-start.38 = (bf16[16,896]{1,0:T(8,128)(2,1)S(1)}, bf16[16,896]{1,0:T(8,128)(2,1)S(1)}, u32[]{:S(2)}, u32[]{:S(2)}) collective-permute-start(bf16[16,896]{1,0:T(8,128)(2,1)S(1)} %get-tuple-element.69), channel_id=1, source_target_pairs={{0,0},{1,129},{32,32},{33,161},{64,64},{65,193},{96,96},{97,225},{... | collective-permute-start | bytes 86024 | tf_op jit(solution)/shard_map/ppermute | solution.py:422
  172.0 0.9 collective-permute-start.37
  172.9 2.7 %collective-permute-start.36 = (bf16[16,896]{1,0:T(8,128)(2,1)S(1)}, bf16[16,896]{1,0:T(8,128)(2,1)S(1)}, u32[]{:S(2)}, u32[]{:S(2)}) collective-permute-start(bf16[16,896]{1,0:T(8,128)(2,1)S(1)} %get-tuple-element.71), channel_id=1, source_target_pairs={{0,64},{1,193},{32,96},{33,225},{64,128},{65,1},{96,160},{97,33},{... | collective-permute-start | bytes 86024 | tf_op jit(solution)/shard_map/ppermute | solution.py:422
  175.6 1.8 %collective-permute-done.36 = bf16[16,896]{1,0:T(8,128)(2,1)S(1)} collective-permute-done((bf16[16,896]{1,0:T(8,128)(2,1)S(1)}, bf16[16,896]{1,0:T(8,128)(2,1)S(1)}, u32[]{:S(2)}, u32[]{:S(2)}) %collective-permute-start.36) | collective-permute-done | bytes 28704 | tf_op jit(solution)/shard_map/ppermute | solution.py:422
  177.6 1.3 collective-permute-done.39.refs_1_
  178.9 1.3 assemble.1
  (73 shorter events, 2.2 us)
Async XLA Ops:
  0.1 0.9 copy-start.6
  1.0 0.7 copy-start.7
  1.7 0.7 copy-start.8
  3.5 11.7 %collective-permute-start = (bf16[16,1024]{1,0:T(8,128)(2,1)S(1)}, bf16[16,1024]{1,0:T(8,128)(2,1)S(1)}, u32[]{:S(2)}, u32[]{:S(2)}) collective-permute-start(bf16[16,1024]{1,0:T(8,128)(2,1)S(1)} %get-tuple-element.36), channel_id=1, source_target_pairs={{0,0},{1,129},{32,32},{33,161},{64,64},{65,193},{96,96},{97,225},{... | collective-permute-start | bytes 98312 | tf_op jit(solution)/shard_map/ppermute | solution.py:378
  13.1 4.1 %collective-permute-start.1 = (bf16[16,1024]{1,0:T(8,128)(2,1)S(1)}, bf16[16,1024]{1,0:T(8,128)(2,1)S(1)}, u32[]{:S(2)}, u32[]{:S(2)}) collective-permute-start(bf16[16,1024]{1,0:T(8,128)(2,1)S(1)} %get-tuple-element.37), channel_id=1, source_target_pairs={{0,224},{1,33},{32,0},{33,65},{64,32},{65,97},{96,64},{97,129},{12... | collective-permute-start | bytes 98312 | tf_op jit(solution)/shard_map/ppermute | solution.py:378
  13.9 4.9 %collective-permute-start.2 = (bf16[16,1024]{1,0:T(8,128)(2,1)S(1)}, bf16[16,1024]{1,0:T(8,128)(2,1)S(1)}, u32[]{:S(2)}, u32[]{:S(2)}) collective-permute-start(bf16[16,1024]{1,0:T(8,128)(2,1)S(1)} %get-tuple-element.38), channel_id=1, source_target_pairs={{0,192},{1,65},{32,224},{33,97},{64,0},{65,129},{96,32},{97,161},{... | collective-permute-start | bytes 98312 | tf_op jit(solution)/shard_map/ppermute | solution.py:378
  15.1 5.8 %collective-permute-start.3 = (bf16[16,1024]{1,0:T(8,128)(2,1)S(1)}, bf16[16,1024]{1,0:T(8,128)(2,1)S(1)}, u32[]{:S(2)}, u32[]{:S(2)}) collective-permute-start(bf16[16,1024]{1,0:T(8,128)(2,1)S(1)} %get-tuple-element.39), channel_id=1, source_target_pairs={{0,160},{1,97},{32,192},{33,129},{64,224},{65,161},{96,0},{97,193}... | collective-permute-start | bytes 98312 | tf_op jit(solution)/shard_map/ppermute | solution.py:378
  42.6 3.0 %copy-start.5 = (bf16[896,1024]{1,0:T(8,128)(2,1)S(1)}, bf16[896,1024]{1,0:T(8,128)(2,1)}, u32[]{:S(2)}) copy-start(bf16[896,1024]{1,0:T(8,128)(2,1)} %su_ref.3) | copy-start | bytes 5505028
  42.7 2.7 %collective-permute-start.4 = (bf16[576,896]{1,0:T(8,128)(2,1)S(1)}, bf16[576,896]{1,0:T(8,128)(2,1)S(1)}, u32[]{:S(2)}, u32[]{:S(2)}) collective-permute-start(bf16[576,896]{1,0:T(8,128)(2,1)S(1)} %pad_maximum_fusion), channel_id=1, source_target_pairs={{0,1},{1,0},{2,3},{3,2},{4,5},{5,4},{6,7},{7,6},{8,9},{9,8},{10,11... | collective-permute-start | bytes 3096584 | tf_op jit(solution)/shard_map/ppermute | solution.py:382
  42.8 2.8 %copy-start.4 = (bf16[896,1024]{1,0:T(8,128)(2,1)S(1)}, bf16[896,1024]{1,0:T(8,128)(2,1)}, u32[]{:S(2)}) copy-start(bf16[896,1024]{1,0:T(8,128)(2,1)} %sg_ref.3) | copy-start | bytes 5505028
  42.9 2.7 %copy-start.2 = (bf16[1,896,1024]{2,1,0:T(8,128)(2,1)S(1)}, bf16[1,896,1024]{2,1,0:T(8,128)(2,1)}, u32[]{:S(2)}) copy-start(bf16[1,896,1024]{2,1,0:T(8,128)(2,1)} %wg_ref.3) | copy-start | bytes 5505028
  42.9 2.9 %copy-start.3 = (bf16[1,896,1024]{2,1,0:T(8,128)(2,1)S(1)}, bf16[1,896,1024]{2,1,0:T(8,128)(2,1)}, u32[]{:S(2)}) copy-start(bf16[1,896,1024]{2,1,0:T(8,128)(2,1)} %wu_ref.3) | copy-start | bytes 5505028
  50.2 13.8 %collective-permute-start.15 = (f16[144,1024]{1,0:T(8,128)(2,1)S(1)}, f16[144,1024]{1,0:T(8,128)(2,1)S(1)}, u32[]{:S(2)}, u32[]{:S(2)}) collective-permute-start(f16[144,1024]{1,0:T(8,128)(2,1)S(1)} %convert_element_type.107), channel_id=1, source_target_pairs={{0,32},{32,64},{64,96},{96,128},{128,160},{160,192},{192,224},{224... | collective-permute-start | bytes 884744 | tf_op jit(solution)/shard_map/ppermute | solution.py:367
  52.1 12.6 %collective-permute-start.5 = (f16[144,1024]{1,0:T(8,128)(2,1)S(1)}, f16[144,1024]{1,0:T(8,128)(2,1)S(1)}, u32[]{:S(2)}, u32[]{:S(2)}) collective-permute-start(f16[144,1024]{1,0:T(8,128)(2,1)S(1)} %convert_element_type.87), channel_id=1, source_target_pairs={{0,224},{32,0},{64,32},{96,64},{128,96},{160,128},{192,160},{224,1... | collective-permute-start | bytes 884744 | tf_op jit(solution)/shard_map/ppermute | solution.py:367
  62.4 10.1 %collective-permute-start.12 = (f16[144,1024]{1,0:T(8,128)(2,1)S(1)}, f16[144,1024]{1,0:T(8,128)(2,1)S(1)}, u32[]{:S(2)}, u32[]{:S(2)}) collective-permute-start(f16[144,1024]{1,0:T(8,128)(2,1)S(1)} %convert_element_type.101), channel_id=1, source_target_pairs={{0,224},{32,0},{64,32},{96,64},{128,96},{160,128},{192,160},{224,1... | collective-permute-start | bytes 884744 | tf_op jit(solution)/shard_map/ppermute | solution.py:367
  63.5 8.6 %collective-permute-start.9 = (f16[144,1024]{1,0:T(8,128)(2,1)S(1)}, f16[144,1024]{1,0:T(8,128)(2,1)S(1)}, u32[]{:S(2)}, u32[]{:S(2)}) collective-permute-start(f16[144,1024]{1,0:T(8,128)(2,1)S(1)} %convert_element_type.95), channel_id=1, source_target_pairs={{0,32},{32,64},{64,96},{96,128},{128,160},{160,192},{192,224},{224... | collective-permute-start | bytes 884744 | tf_op jit(solution)/shard_map/ppermute | solution.py:367
  64.1 20.9 %collective-permute-start.16 = (f16[144,1024]{1,0:T(8,128)(2,1)S(1)}, f16[144,1024]{1,0:T(8,128)(2,1)S(1)}, u32[]{:S(2)}, u32[]{:S(2)}) collective-permute-start(f16[144,1024]{1,0:T(8,128)(2,1)S(1)} %add_convert_fusion.2), channel_id=1, source_target_pairs={{0,32},{32,64},{64,96},{96,128},{128,160},{160,192},{192,224},{224... | collective-permute-start | bytes 884744 | tf_op jit(solution)/shard_map/ppermute | solution.py:367
  64.9 11.8 %collective-permute-start.6 = (f16[144,1024]{1,0:T(8,128)(2,1)S(1)}, f16[144,1024]{1,0:T(8,128)(2,1)S(1)}, u32[]{:S(2)}, u32[]{:S(2)}) collective-permute-start(f16[144,1024]{1,0:T(8,128)(2,1)S(1)} %add_convert_fusion.9), channel_id=1, source_target_pairs={{0,224},{32,0},{64,32},{96,64},{128,96},{160,128},{192,160},{224,1... | collective-permute-start | bytes 884744 | tf_op jit(solution)/shard_map/ppermute | solution.py:367
  72.2 12.5 %collective-permute-start.10 = (f16[144,1024]{1,0:T(8,128)(2,1)S(1)}, f16[144,1024]{1,0:T(8,128)(2,1)S(1)}, u32[]{:S(2)}, u32[]{:S(2)}) collective-permute-start(f16[144,1024]{1,0:T(8,128)(2,1)S(1)} %add_convert_fusion.6), channel_id=1, source_target_pairs={{0,32},{32,64},{64,96},{96,128},{128,160},{160,192},{192,224},{224... | collective-permute-start | bytes 884744 | tf_op jit(solution)/shard_map/ppermute | solution.py:367
  72.6 12.6 %collective-permute-start.13 = (f16[144,1024]{1,0:T(8,128)(2,1)S(1)}, f16[144,1024]{1,0:T(8,128)(2,1)S(1)}, u32[]{:S(2)}, u32[]{:S(2)}) collective-permute-start(f16[144,1024]{1,0:T(8,128)(2,1)S(1)} %add_convert_fusion.4), channel_id=1, source_target_pairs={{0,224},{32,0},{64,32},{96,64},{128,96},{160,128},{192,160},{224,1... | collective-permute-start | bytes 884744 | tf_op jit(solution)/shard_map/ppermute | solution.py:367
  76.8 12.0 %collective-permute-start.7 = (f16[144,1024]{1,0:T(8,128)(2,1)S(1)}, f16[144,1024]{1,0:T(8,128)(2,1)S(1)}, u32[]{:S(2)}, u32[]{:S(2)}) collective-permute-start(f16[144,1024]{1,0:T(8,128)(2,1)S(1)} %add_convert_fusion.8), channel_id=1, source_target_pairs={{0,224},{32,0},{64,32},{96,64},{128,96},{160,128},{192,160},{224,1... | collective-permute-start | bytes 884744 | tf_op jit(solution)/shard_map/ppermute | solution.py:367
  84.9 14.3 %collective-permute-start.11 = (f16[144,1024]{1,0:T(8,128)(2,1)S(1)}, f16[144,1024]{1,0:T(8,128)(2,1)S(1)}, u32[]{:S(2)}, u32[]{:S(2)}) collective-permute-start(f16[144,1024]{1,0:T(8,128)(2,1)S(1)} %add_convert_fusion.5), channel_id=1, source_target_pairs={{0,32},{32,64},{64,96},{96,128},{128,160},{160,192},{192,224},{224... | collective-permute-start | bytes 884744 | tf_op jit(solution)/shard_map/ppermute | solution.py:367
  85.1 13.9 %collective-permute-start.17 = (f16[144,1024]{1,0:T(8,128)(2,1)S(1)}, f16[144,1024]{1,0:T(8,128)(2,1)S(1)}, u32[]{:S(2)}, u32[]{:S(2)}) collective-permute-start(f16[144,1024]{1,0:T(8,128)(2,1)S(1)} %add_convert_fusion.1), channel_id=1, source_target_pairs={{0,32},{32,64},{64,96},{96,128},{128,160},{160,192},{192,224},{224... | collective-permute-start | bytes 884744 | tf_op jit(solution)/shard_map/ppermute | solution.py:367
  85.3 14.0 %collective-permute-start.14 = (f16[144,1024]{1,0:T(8,128)(2,1)S(1)}, f16[144,1024]{1,0:T(8,128)(2,1)S(1)}, u32[]{:S(2)}, u32[]{:S(2)}) collective-permute-start(f16[144,1024]{1,0:T(8,128)(2,1)S(1)} %add_convert_fusion.3), channel_id=1, source_target_pairs={{0,224},{32,0},{64,32},{96,64},{128,96},{160,128},{192,160},{224,1... | collective-permute-start | bytes 884744 | tf_op jit(solution)/shard_map/ppermute | solution.py:367
  88.8 12.5 %collective-permute-start.8 = (f16[144,1024]{1,0:T(8,128)(2,1)S(1)}, f16[144,1024]{1,0:T(8,128)(2,1)S(1)}, u32[]{:S(2)}, u32[]{:S(2)}) collective-permute-start(f16[144,1024]{1,0:T(8,128)(2,1)S(1)} %add_convert_fusion.7), channel_id=1, source_target_pairs={{0,224},{32,0},{64,32},{96,64},{128,96},{160,128},{192,160},{224,1... | collective-permute-start | bytes 884744 | tf_op jit(solution)/shard_map/ppermute | solution.py:367
  99.0 29.5 %copy-start.1 = (bf16[1024,896]{1,0:T(8,128)(2,1)S(1)}, bf16[1024,896]{1,0:T(8,128)(2,1)}, u32[]{:S(2)}) copy-start(bf16[1024,896]{1,0:T(8,128)(2,1)} %refs_9_.3) | copy-start | bytes 5505028
  99.1 29.4 %copy-start = (bf16[1,1024,896]{2,1,0:T(8,128)(2,1)S(1)}, bf16[1,1024,896]{2,1,0:T(8,128)(2,1)}, u32[]{:S(2)}) copy-start(bf16[1,1024,896]{2,1,0:T(8,128)(2,1)} %refs_8_.3) | copy-start | bytes 5505028
  99.1 6.9 %collective-permute-start.18 = (f16[144,1024]{1,0:T(8,128)(2,1)S(1)}, f16[144,1024]{1,0:T(8,128)(2,1)S(1)}, u32[]{:S(2)}, u32[]{:S(2)}) collective-permute-start(f16[144,1024]{1,0:T(8,128)(2,1)S(1)} %add_convert_fusion), channel_id=1, source_target_pairs={{0,32},{32,64},{64,96},{96,128},{128,160},{160,192},{192,224},{224... | collective-permute-start | bytes 884744 | tf_op jit(solution)/shard_map/ppermute | solution.py:367
  106.4 5.3 %collective-permute-start.28 = (bf16[144,512]{1,0:T(8,128)(2,1)S(1)}, bf16[144,512]{1,0:T(8,128)(2,1)S(1)}, u32[]{:S(2)}, u32[]{:S(2)}) collective-permute-start(bf16[144,512]{1,0:T(8,128)(2,1)S(1)} %get-tuple-element.67.refs_3_), channel_id=1, source_target_pairs={{0,32},{32,64},{64,96},{96,128},{128,160},{160,192},{192,224},{224... | collective-permute-start | bytes 442376 | tf_op jit(solution)/shard_map/ppermute | solution.py:405
  106.5 5.2 %collective-permute-start.19 = (bf16[144,512]{1,0:T(8,128)(2,1)S(1)}, bf16[144,512]{1,0:T(8,128)(2,1)S(1)}, u32[]{:S(2)}, u32[]{:S(2)}) collective-permute-start(bf16[144,512]{1,0:T(8,128)(2,1)S(1)} %get-tuple-element.68.refs_2_), channel_id=1, source_target_pairs={{0,224},{32,0},{64,32},{96,64},{128,96},{160,128},{192,160},{224,1... | collective-permute-start | bytes 442376 | tf_op jit(solution)/shard_map/ppermute | solution.py:404
  109.1 5.2 %collective-permute-start.22 = (bf16[144,512]{1,0:T(8,128)(2,1)S(1)}, bf16[144,512]{1,0:T(8,128)(2,1)S(1)}, u32[]{:S(2)}, u32[]{:S(2)}) collective-permute-start(bf16[144,512]{1,0:T(8,128)(2,1)S(1)} %get-tuple-element.67.refs_3_), channel_id=1, source_target_pairs={{0,224},{32,0},{64,32},{96,64},{128,96},{160,128},{192,160},{224,1... | collective-permute-start | bytes 442376 | tf_op jit(solution)/shard_map/ppermute | solution.py:407
  109.1 6.8 %collective-permute-start.25 = (bf16[144,512]{1,0:T(8,128)(2,1)S(1)}, bf16[144,512]{1,0:T(8,128)(2,1)S(1)}, u32[]{:S(2)}, u32[]{:S(2)}) collective-permute-start(bf16[144,512]{1,0:T(8,128)(2,1)S(1)} %get-tuple-element.68.refs_2_), channel_id=1, source_target_pairs={{0,32},{32,64},{64,96},{96,128},{128,160},{160,192},{192,224},{224... | collective-permute-start | bytes 442376 | tf_op jit(solution)/shard_map/ppermute | solution.py:408
  111.6 6.1 %collective-permute-start.29 = (bf16[144,512]{1,0:T(8,128)(2,1)S(1)}, bf16[144,512]{1,0:T(8,128)(2,1)S(1)}, u32[]{:S(2)}, u32[]{:S(2)}) collective-permute-start(bf16[144,512]{1,0:T(8,128)(2,1)S(1)} %collective-permute-done.28.refs_5_), channel_id=1, source_target_pairs={{0,32},{32,64},{64,96},{96,128},{128,160},{160,192},{192,224},{224... | collective-permute-start | bytes 442376 | tf_op jit(solution)/shard_map/ppermute | solution.py:405
  111.7 6.4 %collective-permute-start.20 = (bf16[144,512]{1,0:T(8,128)(2,1)S(1)}, bf16[144,512]{1,0:T(8,128)(2,1)S(1)}, u32[]{:S(2)}, u32[]{:S(2)}) collective-permute-start(bf16[144,512]{1,0:T(8,128)(2,1)S(1)} %collective-permute-done.19.refs_0_), channel_id=1, source_target_pairs={{0,224},{32,0},{64,32},{96,64},{128,96},{160,128},{192,160},{224,1... | collective-permute-start | bytes 442376 | tf_op jit(solution)/shard_map/ppermute | solution.py:404
  114.3 7.1 %collective-permute-start.23 = (bf16[144,512]{1,0:T(8,128)(2,1)S(1)}, bf16[144,512]{1,0:T(8,128)(2,1)S(1)}, u32[]{:S(2)}, u32[]{:S(2)}) collective-permute-start(bf16[144,512]{1,0:T(8,128)(2,1)S(1)} %collective-permute-done.22.refs_1_), channel_id=1, source_target_pairs={{0,224},{32,0},{64,32},{96,64},{128,96},{160,128},{192,160},{224,1... | collective-permute-start | bytes 442376 | tf_op jit(solution)/shard_map/ppermute | solution.py:407
  115.9 8.0 %collective-permute-start.26 = (bf16[144,512]{1,0:T(8,128)(2,1)S(1)}, bf16[144,512]{1,0:T(8,128)(2,1)S(1)}, u32[]{:S(2)}, u32[]{:S(2)}) collective-permute-start(bf16[144,512]{1,0:T(8,128)(2,1)S(1)} %collective-permute-done.25.refs_4_), channel_id=1, source_target_pairs={{0,32},{32,64},{64,96},{96,128},{128,160},{160,192},{192,224},{224... | collective-permute-start | bytes 442376 | tf_op jit(solution)/shard_map/ppermute | solution.py:408
  117.7 6.6 %collective-permute-start.30 = (bf16[144,512]{1,0:T(8,128)(2,1)S(1)}, bf16[144,512]{1,0:T(8,128)(2,1)S(1)}, u32[]{:S(2)}, u32[]{:S(2)}) collective-permute-start(bf16[144,512]{1,0:T(8,128)(2,1)S(1)} %collective-permute-done.29.refs_7_), channel_id=1, source_target_pairs={{0,32},{32,64},{64,96},{96,128},{128,160},{160,192},{192,224},{224... | collective-permute-start | bytes 442376 | tf_op jit(solution)/shard_map/ppermute | solution.py:405
  118.0 7.0 %collective-permute-start.21 = (bf16[144,512]{1,0:T(8,128)(2,1)S(1)}, bf16[144,512]{1,0:T(8,128)(2,1)S(1)}, u32[]{:S(2)}, u32[]{:S(2)}) collective-permute-start(bf16[144,512]{1,0:T(8,128)(2,1)S(1)} %collective-permute-done.20.refs_2_), channel_id=1, source_target_pairs={{0,224},{32,0},{64,32},{96,64},{128,96},{160,128},{192,160},{224,1... | collective-permute-start | bytes 442376 | tf_op jit(solution)/shard_map/ppermute | solution.py:404
  121.4 18.9 %collective-permute-start.24 = (bf16[144,512]{1,0:T(8,128)(2,1)S(1)}, bf16[144,512]{1,0:T(8,128)(2,1)S(1)}, u32[]{:S(2)}, u32[]{:S(2)}) collective-permute-start(bf16[144,512]{1,0:T(8,128)(2,1)S(1)} %collective-permute-done.23.refs_3_), channel_id=1, source_target_pairs={{0,224},{32,0},{64,32},{96,64},{128,96},{160,128},{192,160},{224,1... | collective-permute-start | bytes 442376 | tf_op jit(solution)/shard_map/ppermute | solution.py:407
  123.9 16.4 %collective-permute-start.27 = (bf16[144,512]{1,0:T(8,128)(2,1)S(1)}, bf16[144,512]{1,0:T(8,128)(2,1)S(1)}, u32[]{:S(2)}, u32[]{:S(2)}) collective-permute-start(bf16[144,512]{1,0:T(8,128)(2,1)S(1)} %collective-permute-done.26.refs_6_), channel_id=1, source_target_pairs={{0,32},{32,64},{64,96},{96,128},{128,160},{160,192},{192,224},{224... | collective-permute-start | bytes 442376 | tf_op jit(solution)/shard_map/ppermute | solution.py:408
  124.4 15.9 %collective-permute-start.32 = (bf16[144,512]{1,0:T(8,128)(2,1)S(1)}, bf16[144,512]{1,0:T(8,128)(2,1)S(1)}, u32[]{:S(2)}, u32[]{:S(2)}) collective-permute-start(bf16[144,512]{1,0:T(8,128)(2,1)S(1)} %collective-permute-done.30.refs_5_), channel_id=1, source_target_pairs={{0,32},{32,64},{64,96},{96,128},{128,160},{160,192},{192,224},{224... | collective-permute-start | bytes 442376 | tf_op jit(solution)/shard_map/ppermute | solution.py:405
  125.1 15.2 %collective-permute-start.31 = (bf16[144,512]{1,0:T(8,128)(2,1)S(1)}, bf16[144,512]{1,0:T(8,128)(2,1)S(1)}, u32[]{:S(2)}, u32[]{:S(2)}) collective-permute-start(bf16[144,512]{1,0:T(8,128)(2,1)S(1)} %collective-permute-done.21.refs_0_), channel_id=1, source_target_pairs={{0,224},{32,0},{64,32},{96,64},{128,96},{160,128},{192,160},{224,1... | collective-permute-start | bytes 442376 | tf_op jit(solution)/shard_map/ppermute | solution.py:404
  130.9 12.5 %collective-permute-start.34 = (f32[2,144,896]{2,1,0:T(8,128)S(1)}, f32[2,144,896]{2,1,0:T(8,128)S(1)}, u32[]{:S(2)}, u32[]{:S(2)}) collective-permute-start(f32[2,144,896]{2,1,0:T(8,128)S(1)} %get-tuple-element.62), channel_id=1, source_target_pairs={{0,1},{1,0},{2,3},{3,2},{4,5},{5,4},{6,7},{7,6},{8,9},{9,8},{10,11... | collective-permute-start | bytes 3096584 | tf_op jit(solution)/shard_map/ppermute | solution.py:415
  142.7 2.9 %collective-permute-start.33 = (f32[2,144,896]{2,1,0:T(8,128)S(1)}, f32[2,144,896]{2,1,0:T(8,128)S(1)}, u32[]{:S(2)}, u32[]{:S(2)}) collective-permute-start(f32[2,144,896]{2,1,0:T(8,128)S(1)} %get-tuple-element.60), channel_id=1, source_target_pairs={{0,1},{1,0},{2,3},{3,2},{4,5},{5,4},{6,7},{7,6},{8,9},{9,8},{10,11... | collective-permute-start | bytes 3096584 | tf_op jit(solution)/shard_map/ppermute | solution.py:415
  165.2 10.4 %collective-permute-start.35 = (bf16[16,896]{1,0:T(8,128)(2,1)S(1)}, bf16[16,896]{1,0:T(8,128)(2,1)S(1)}, u32[]{:S(2)}, u32[]{:S(2)}) collective-permute-start(bf16[16,896]{1,0:T(8,128)(2,1)S(1)} %get-tuple-element.72), channel_id=1, source_target_pairs={{0,32},{1,225},{32,64},{33,1},{64,96},{65,33},{96,128},{97,65},{12... | collective-permute-start | bytes 86024 | tf_op jit(solution)/shard_map/ppermute | solution.py:422
  168.2 9.3 %collective-permute-start.38 = (bf16[16,896]{1,0:T(8,128)(2,1)S(1)}, bf16[16,896]{1,0:T(8,128)(2,1)S(1)}, u32[]{:S(2)}, u32[]{:S(2)}) collective-permute-start(bf16[16,896]{1,0:T(8,128)(2,1)S(1)} %get-tuple-element.69), channel_id=1, source_target_pairs={{0,0},{1,129},{32,32},{33,161},{64,64},{65,193},{96,96},{97,225},{... | collective-permute-start | bytes 86024 | tf_op jit(solution)/shard_map/ppermute | solution.py:422
  172.0 5.5 %collective-permute-start.37 = (bf16[16,896]{1,0:T(8,128)(2,1)S(1)}, bf16[16,896]{1,0:T(8,128)(2,1)S(1)}, u32[]{:S(2)}, u32[]{:S(2)}) collective-permute-start(bf16[16,896]{1,0:T(8,128)(2,1)S(1)} %get-tuple-element.70), channel_id=1, source_target_pairs={{0,96},{1,161},{32,128},{33,193},{64,160},{65,225},{96,192},{97,1}... | collective-permute-start | bytes 86024 | tf_op jit(solution)/shard_map/ppermute | solution.py:422
  172.9 4.5 %collective-permute-start.36 = (bf16[16,896]{1,0:T(8,128)(2,1)S(1)}, bf16[16,896]{1,0:T(8,128)(2,1)S(1)}, u32[]{:S(2)}, u32[]{:S(2)}) collective-permute-start(bf16[16,896]{1,0:T(8,128)(2,1)S(1)} %get-tuple-element.71), channel_id=1, source_target_pairs={{0,64},{1,193},{32,96},{33,225},{64,128},{65,1},{96,160},{97,33},{... | collective-permute-start | bytes 86024 | tf_op jit(solution)/shard_map/ppermute | solution.py:422
  177.5 1.4 collective-permute-start.39

commit v2 on v1

--- a/solution.py
+++ b/solution.py
@@ -157,17 +157,7 @@
 
     for w_ref, v_ref, o_refs in ((wg_ref, sg_ref, out_refs[:count]), (wu_ref, su_ref, out_refs[count:])):
         shared = fdot(s_ref[...], v_ref[...]) * SCALE
-        if count == len(EARLY):
-            full_ref[...] = fdot(x_ref[...], w_ref[0]) * SCALE
-        else:
-            half = count * ROWS // 2
-
-            def part(i, carry):
-                rows = pl.ds(pl.multiple_of(i * half, half), half)
-                full_ref[rows, :] = fdot(x_ref[rows, :], w_ref[0]) * SCALE
-                return carry
-
-            lax.fori_loop(0, 2, part, 0)
+        full_ref[...] = fdot(x_ref[...], w_ref[0]) * SCALE
         for i in range(count):
             o_refs[i][:ROWS, :] = full_ref[i * ROWS : (i + 1) * ROWS]
             o_refs[i][ROWS:, :] = shared[i * PADT : (i + 1) * PADT]
@@ -249,33 +239,29 @@
     )(c, *xs, wd, sd)
 
 
-def settle_kernel(keep_ref, came_ref, *refs):
-    before, (rows_ref, shared_ref) = refs[:-2], refs[-2:]
-    at = 0
-    if before:
-        at = 2 * CAP
-        rows_ref[:, :at, :] = before[0][...]
-    for i in range(2):
-        total = keep_ref[i, :ROWS] + came_ref[i, :ROWS]
-        rows_ref[:, at + i * CAP : at + (i + 1) * CAP, :] = total.reshape(EXPERTS, CAP, BLOCK).astype(jnp.bfloat16)
-        shared_ref[i * PADT : (i + 1) * PADT] = keep_ref[i, ROWS:] + came_ref[i, ROWS:]
-
-
-def settle(keep, came, *before):
+def settle_kernel(near_ref, far_ref, came_ref, rows_ref, shared_ref):
+    for i in range(4):
+        keep = (near_ref, far_ref)[i // 2]
+        total = keep[i % 2, :ROWS] + came_ref[i, :ROWS]
+        rows_ref[:, i * CAP : (i + 1) * CAP, :] = total.reshape(EXPERTS, CAP, BLOCK).astype(jnp.bfloat16)
+        shared_ref[i * PADT : (i + 1) * PADT] = keep[i % 2, ROWS:] + came_ref[i, ROWS:]
+
+
+def settle(near, far, came):
     return pl.pallas_call(
         settle_kernel,
         out_shape=(
-            jax.ShapeDtypeStruct((EXPERTS, (2 + 2 * len(before)) * CAP, BLOCK), jnp.bfloat16),
-            jax.ShapeDtypeStruct((2 * PADT, BLOCK), jnp.float32),
+            jax.ShapeDtypeStruct((EXPERTS, 4 * CAP, BLOCK), jnp.bfloat16),
+            jax.ShapeDtypeStruct((4 * PADT, BLOCK), jnp.float32),
         ),
-        in_specs=[VMEM] * (2 + len(before)),
+        in_specs=[VMEM] * 3,
         out_specs=(VMEM, VMEM),
         compiler_params=PARAMS,
         name="settle",
-    )(keep, came, *before)
-
-
-def combine_kernel(ext_ref, back_ref, near_ref, far_ref, out_ref, terms_ref, total_ref):
+    )(near, far, came)
+
+
+def combine_kernel(ext_ref, back_ref, shared_ref, out_ref, terms_ref, total_ref):
     rows = 4 * PADT
     cols = 4 * ROWS
     ext = jnp.concatenate([ext_ref[PADT:], ext_ref[:PADT]], axis=0).astype(jnp.float32)
@@ -302,8 +288,7 @@
     low = (rest - mid.astype(jnp.float32)).astype(jnp.bfloat16)
     for i, term in enumerate((low, mid, hi)):
         terms_ref[i] = term
-    total_ref[: 2 * PADT] = near_ref[...]
-    total_ref[2 * PADT :] = far_ref[...]
+    total_ref[...] = shared_ref[...]
 
     def add(i, carry):
         total_ref[...] += fdot(terms_ref[i], back_ref[...])
@@ -313,11 +298,11 @@
     out_ref[...] = total_ref[...].astype(jnp.bfloat16)
 
 
-def combine(ext, back, near, far):
+def combine(ext, back, shared):
     return pl.pallas_call(
         combine_kernel,
         out_shape=jax.ShapeDtypeStruct((4 * PADT, BLOCK), jnp.bfloat16),
-        in_specs=[VMEM, VMEM, VMEM, VMEM],
+        in_specs=[VMEM, VMEM, VMEM],
         out_specs=VMEM,
         scratch_shapes=[
             pltpu.VMEM((3, 4 * PADT, 4 * ROWS), jnp.bfloat16),
@@ -325,7 +310,7 @@
         ],
         compiler_params=PARAMS,
         name="combine",
-    )(ext, back, near, far)
+    )(ext, back, shared)
 
 
 def assemble_kernel(s_ref, *refs):
@@ -409,14 +394,15 @@
             got[ZN - j], got[j] = (pd, qd), (pu, qu)
         else:
             got[4] = (pd, qu)
-    rows, shares = (), []
+    keeps, sends = [], []
     for a, b in (((7, 6), (1, 2)), ((5, 0), (3, 4))):
         keep, send = down_dots(c1, [p for k in a + b for p in got[k]], wd, sd)
-        came = lax.ppermute(send, "tensor", SWAP)
-        *rows, shared = settle(keep, came, *rows)
-        shares.append(shared)
-    back = lax.all_to_all(rows[0], "expert", 0, 0, tiled=True).reshape(4 * ROWS, BLOCK)
-    mixed = combine(ext, back, *shares)
+        keeps.append(keep)
+        sends.append(send)
+    crossed = lax.ppermute(jnp.concatenate(sends), "tensor", SWAP)
+    rows, shared = settle(*keeps, crossed)
+    back = lax.all_to_all(rows, "expert", 0, 0, tiled=True).reshape(4 * ROWS, BLOCK)
+    mixed = combine(ext, back, shared)
     held = []
     for i, (to, fro) in enumerate(((1, 1), (2, 2), (3, 3), (0, 4))):
         held.append(lax.ppermute(mixed[i * PADT : (i + 1) * PADT], ("dp", "tensor"), paired(to, fro)))

time: 180 us -> 179 us (level)
  waiting for transfers between devices: 46 us -> 49.7 us
  Pallas kernels: 22.9 us -> 19.2 us
  starting transfers between devices: 67.3 us -> 65.2 us
    pallas_call x2, Pallas kernels: 13.5 us -> 9.88 us  [up_dots(): pl.pallas_call(functools.partial(up_kernel, ks), grid=(FFH // NT,), out_s...]
    ppermute x4, waiting for transfers between devices: 2.94 us -> 5.12 us  [layer(): qu = lax.ppermute(qu, 'dp', shifted(1))]
    ppermute x2 -> x1, starting transfers between devices: 9.99 us -> 7.87 us  [layer(): crossed = lax.ppermute(jnp.concatenate(sends), 'tensor', SWAP)]
    ppermute x2 -> x1, waiting for transfers between devices: 2.16 us -> 3.74 us  [layer(): crossed = lax.ppermute(jnp.concatenate(sends), 'tensor', SWAP)]
  transfers between devices with their start and end apart: 40 -> 39, of which waited for: 18 -> 19; matrix products, arithmetic and copies ran while one was open for 1% -> 1% of each run, Pallas kernels for 8% -> 5%
where the time goes in v2:
time: 179 us; the launch traced here: 178 us
  starting transfers between devices  65.2 us (36%)
  waiting for transfers between devices  49.7 us (28%)
  blocking collectives  39.2 us (22%)
  Pallas kernels  19.2 us (11%)
  local copies, waits for them, and re-layouts  2.84 us (2%)
    ppermute x14, waiting for transfers between devices, ring(): total = lax.ppermute(total.astype(LINK), 'dp', shifted(shift))  29.3 us
    all_to_all x1, blocking collectives, layer(): arrived = lax.all_to_all(packed, 'expert', 0, 0, tiled=True)  21.1 us
    all_to_all x1, blocking collectives, layer(): lax.all_to_all(rows, 'expert', 0, 0, tiled=True).reshape(4 * ROWS, BLOCK)  18.1 us
    ppermute x14, starting transfers between devices, ring(): total = lax.ppermute(total.astype(LINK), 'dp', shifted(shift))  16.1 us
    ppermute x4, starting transfers between devices, layer(): pd = lax.ppermute(pd, 'dp', shifted(-1))  12.1 us
    ppermute x4, starting transfers between devices, layer(): lax.ppermute(piece, ('dp', 'tensor'), paired(-j, -j) if j else paired(0, 4))  11.6 us
    ppermute x4, starting transfers between devices, layer(): lax.ppermute(mixed[i * PADT:(i + 1) * PADT], ('dp', 'tensor'), paired(to,...  10.4 us
    pallas_call x2, Pallas kernels, up_dots(): pl.pallas_call(functools.partial(up_kernel, ks), grid=(FFH // NT,), out_s...  9.88 us
  transfers between devices with their start and end apart: 39, of which 19 were waited for; matrix products, arithmetic and copies ran while one was open for 1% of the time, Pallas kernels for 5%

profile of v2, /device:TPU:1, one launch (start us, length us, event | category | flops | bytes accessed | tf_op | source)
XLA Modules:
  0.0 178.2 jit_solution(15009849328626334420)
XLA Ops:
  0.1 0.9 copy-done.6
  1.0 0.7 copy-done.7
  1.7 0.7 copy-done.8
  2.4 1.1 prep.1
  3.5 9.6 %collective-permute-start = (bf16[16,1024]{1,0:T(8,128)(2,1)S(1)}, bf16[16,1024]{1,0:T(8,128)(2,1)S(1)}, u32[]{:S(2)}, u32[]{:S(2)}) collective-permute-start(bf16[16,1024]{1,0:T(8,128)(2,1)S(1)} %get-tuple-element.34), channel_id=1, source_target_pairs={{0,0},{1,129},{32,32},{33,161},{64,64},{65,193},{96,96},{97,225},{... | collective-permute-start | bytes 98312 | tf_op jit(solution)/shard_map/ppermute | solution.py:363
  13.1 0.8 collective-permute-start.1
  13.9 1.2 collective-permute-start.2
  15.1 2.0 %collective-permute-done.1.refs_1_ = bf16[16,1024]{1,0:T(8,128)(2,1)S(1)} collective-permute-done((bf16[16,1024]{1,0:T(8,128)(2,1)S(1)}, bf16[16,1024]{1,0:T(8,128)(2,1)S(1)}, u32[]{:S(2)}, u32[]{:S(2)}) %collective-permute-start.1) | collective-permute-done | bytes 32800 | tf_op jit(solution)/shard_map/ppermute | solution.py:363
  17.2 1.7 collective-permute-done.2.refs_2_
  18.8 2.1 %collective-permute-done.3.refs_3_ = bf16[16,1024]{1,0:T(8,128)(2,1)S(1)} collective-permute-done((bf16[16,1024]{1,0:T(8,128)(2,1)S(1)}, bf16[16,1024]{1,0:T(8,128)(2,1)S(1)}, u32[]{:S(2)}, u32[]{:S(2)}) %collective-permute-start.3) | collective-permute-done | bytes 32800 | tf_op jit(solution)/shard_map/ppermute | solution.py:363
  20.9 0.6 pack.1
  21.5 21.1 %all_to_all.10 = bf16[16,32,896]{2,1,0:T(8,128)(2,1)S(1)} all-to-all(bf16[16,32,896]{2,1,0:T(8,128)(2,1)S(1)} %get-tuple-element.39), channel_id=1, replica_groups=mesh['dp'=8,'expert'=16,'tensor'=2] {'expert'}, dimensions={0} | all-to-all | bytes 1835008 | tf_op jit(solution)/shard_map/all_to_all | solution.py:365
  43.0 2.5 %collective-permute-done.4 = bf16[576,896]{1,0:T(8,128)(2,1)S(1)} collective-permute-done((bf16[576,896]{1,0:T(8,128)(2,1)S(1)}, bf16[576,896]{1,0:T(8,128)(2,1)S(1)}, u32[]{:S(2)}, u32[]{:S(2)}) %collective-permute-start.4) | collective-permute-done | bytes 1032224 | tf_op jit(solution)/shard_map/ppermute | solution.py:367
  45.7 0.2 copy-done.3
  45.9 4.2 %shard_map.92 = (f32[144,1024]{1,0:T(8,128)S(1)}, f32[144,1024]{1,0:T(8,128)S(1)}, f32[144,1024]{1,0:T(8,128)S(1)}, f32[144,1024]{1,0:T(8,128)S(1)}, f32[144,1024]{1,0:T(8,128)S(1)}, /*index=5*/f32[144,1024]{1,0:T(8,128)S(1)}) custom-call(s32[1]{0:T(128)} %bitcast.1.c_ref, bf16[4,128,896]{2,1,0:T(8,128)(2,1)S(1)} %copy_bitcast_fusion.1.own_ref, ...), custom_call_target="tpu_custom_call" | custom-call | flops 1585446912 | bytes 7340032 | tf_op jit(solution)/shard_map/pallas_call | solution.py:169
  50.2 1.9 %collective-permute-start.15 = (f16[144,1024]{1,0:T(8,128)(2,1)S(1)}, f16[144,1024]{1,0:T(8,128)(2,1)S(1)}, u32[]{:S(2)}, u32[]{:S(2)}) collective-permute-start(f16[144,1024]{1,0:T(8,128)(2,1)S(1)} %convert_element_type.107), channel_id=1, source_target_pairs={{0,32},{32,64},{64,96},{96,128},{128,160},{160,192},{192,224},{224... | collective-permute-start | bytes 884744 | tf_op jit(solution)/shard_map/ppermute | solution.py:352
  52.1 0.9 collective-permute-start.5
  53.0 5.6 %shard_map.91 = (f32[144,1024]{1,0:T(8,128)S(1)}, f32[144,1024]{1,0:T(8,128)S(1)}, f32[144,1024]{1,0:T(8,128)S(1)}, f32[144,1024]{1,0:T(8,128)S(1)}, f32[144,102...) custom-call(s32[1]{0:T(128)} %bitcast.1.c_ref, ...), custom_call_target="tpu_custom_call" | custom-call | flops 2642411520 | bytes 7340032 | tf_op jit(solution)/shard_map/pallas_call | solution.py:169
  58.8 1.1 collective-permute-start.12
  59.9 0.4 collective-permute-start.9
  60.4 0.7 collective-permute-start.16
  61.2 2.1 %collective-permute-start.6 = (f16[144,1024]{1,0:T(8,128)(2,1)S(1)}, f16[144,1024]{1,0:T(8,128)(2,1)S(1)}, u32[]{:S(2)}, u32[]{:S(2)}) collective-permute-start(f16[144,1024]{1,0:T(8,128)(2,1)S(1)} %add_convert_fusion.9), channel_id=1, source_target_pairs={{0,224},{32,0},{64,32},{96,64},{128,96},{160,128},{192,160},{224,1... | collective-permute-start | bytes 884744 | tf_op jit(solution)/shard_map/ppermute | solution.py:352
  63.4 5.1 %collective-permute-done.9 = f16[144,1024]{1,0:T(8,128)(2,1)S(1)} collective-permute-done((f16[144,1024]{1,0:T(8,128)(2,1)S(1)}, f16[144,1024]{1,0:T(8,128)(2,1)S(1)}, u32[]{:S(2)}, u32[]{:S(2)}) %collective-permute-start.9) | collective-permute-done | bytes 294944 | tf_op jit(solution)/shard_map/ppermute | solution.py:352
  68.6 0.3 collective-permute-start.10
  69.0 2.7 %collective-permute-start.13 = (f16[144,1024]{1,0:T(8,128)(2,1)S(1)}, f16[144,1024]{1,0:T(8,128)(2,1)S(1)}, u32[]{:S(2)}, u32[]{:S(2)}) collective-permute-start(f16[144,1024]{1,0:T(8,128)(2,1)S(1)} %add_convert_fusion.4), channel_id=1, source_target_pairs={{0,224},{32,0},{64,32},{96,64},{128,96},{160,128},{192,160},{224,1... | collective-permute-start | bytes 884744 | tf_op jit(solution)/shard_map/ppermute | solution.py:352
  71.7 1.4 collective-permute-done.6
  73.1 2.1 %collective-permute-start.7 = (f16[144,1024]{1,0:T(8,128)(2,1)S(1)}, f16[144,1024]{1,0:T(8,128)(2,1)S(1)}, u32[]{:S(2)}, u32[]{:S(2)}) collective-permute-start(f16[144,1024]{1,0:T(8,128)(2,1)S(1)} %add_convert_fusion.8), channel_id=1, source_target_pairs={{0,224},{32,0},{64,32},{96,64},{128,96},{160,128},{192,160},{224,1... | collective-permute-start | bytes 884744 | tf_op jit(solution)/shard_map/ppermute | solution.py:352
  75.3 5.9 %collective-permute-done.10 = f16[144,1024]{1,0:T(8,128)(2,1)S(1)} collective-permute-done((f16[144,1024]{1,0:T(8,128)(2,1)S(1)}, f16[144,1024]{1,0:T(8,128)(2,1)S(1)}, u32[]{:S(2)}, u32[]{:S(2)}) %collective-permute-start.10) | collective-permute-done | bytes 294944 | tf_op jit(solution)/shard_map/ppermute | solution.py:352
  81.6 2.7 %collective-permute-start.14 = (f16[144,1024]{1,0:T(8,128)(2,1)S(1)}, f16[144,1024]{1,0:T(8,128)(2,1)S(1)}, u32[]{:S(2)}, u32[]{:S(2)}) collective-permute-start(f16[144,1024]{1,0:T(8,128)(2,1)S(1)} %add_convert_fusion.3), channel_id=1, source_target_pairs={{0,224},{32,0},{64,32},{96,64},{128,96},{160,128},{192,160},{224,1... | collective-permute-start | bytes 884744 | tf_op jit(solution)/shard_map/ppermute | solution.py:352
  84.4 0.8 collective-permute-done.7
  85.2 0.8 collective-permute-start.8
  86.0 9.4 %collective-permute-done.17 = f16[144,1024]{1,0:T(8,128)(2,1)S(1)} collective-permute-done((f16[144,1024]{1,0:T(8,128)(2,1)S(1)}, f16[144,1024]{1,0:T(8,128)(2,1)S(1)}, u32[]{:S(2)}, u32[]{:S(2)}) %collective-permute-start.17) | collective-permute-done | bytes 294944 | tf_op jit(solution)/shard_map/ppermute | solution.py:352
  95.6 2.2 %collective-permute-done.8 = f16[144,1024]{1,0:T(8,128)(2,1)S(1)} collective-permute-done((f16[144,1024]{1,0:T(8,128)(2,1)S(1)}, f16[144,1024]{1,0:T(8,128)(2,1)S(1)}, u32[]{:S(2)}, u32[]{:S(2)}) %collective-permute-start.8) | collective-permute-done | bytes 294944 | tf_op jit(solution)/shard_map/ppermute | solution.py:352
  97.8 4.5 %collective-permute-done.18 = f16[144,1024]{1,0:T(8,128)(2,1)S(1)} collective-permute-done((f16[144,1024]{1,0:T(8,128)(2,1)S(1)}, f16[144,1024]{1,0:T(8,128)(2,1)S(1)}, u32[]{:S(2)}, u32[]{:S(2)}) %collective-permute-start.18) | collective-permute-done | bytes 294944 | tf_op jit(solution)/shard_map/ppermute | solution.py:352
  102.3 0.4 multiply_convert_fusion
  102.8 2.7 %collective-permute-start.19 = (bf16[144,512]{1,0:T(8,128)(2,1)S(1)}, bf16[144,512]{1,0:T(8,128)(2,1)S(1)}, u32[]{:S(2)}, u32[]{:S(2)}) collective-permute-start(bf16[144,512]{1,0:T(8,128)(2,1)S(1)} %get-tuple-element.64.refs_2_), channel_id=1, source_target_pairs={{0,224},{32,0},{64,32},{96,64},{128,96},{160,128},{192,160},{224,1... | collective-permute-start | bytes 442376 | tf_op jit(solution)/shard_map/ppermute | solution.py:389
  105.5 1.4 collective-permute-start.23
  106.9 1.1 collective-permute-done.24.refs_5_
  108.0 2.7 %collective-permute-start.21 = (bf16[144,512]{1,0:T(8,128)(2,1)S(1)}, bf16[144,512]{1,0:T(8,128)(2,1)S(1)}, u32[]{:S(2)}, u32[]{:S(2)}) collective-permute-start(bf16[144,512]{1,0:T(8,128)(2,1)S(1)} %collective-permute-done.19.refs_0_), channel_id=1, source_target_pairs={{0,224},{32,0},{64,32},{96,64},{128,96},{160,128},{192,160},{224,1... | collective-permute-start | bytes 442376 | tf_op jit(solution)/shard_map/ppermute | solution.py:389
  110.7 1.6 collective-permute-start.22
  112.3 0.4 collective-permute-start.25
  112.7 1.4 collective-permute-done.26.refs_7_
  114.1 0.3 collective-permute-start.30
  114.4 3.4 %collective-permute-start.27 = (bf16[144,512]{1,0:T(8,128)(2,1)S(1)}, bf16[144,512]{1,0:T(8,128)(2,1)S(1)}, u32[]{:S(2)}, u32[]{:S(2)}) collective-permute-start(bf16[144,512]{1,0:T(8,128)(2,1)S(1)} %collective-permute-done.21.refs_2_), channel_id=1, source_target_pairs={{0,224},{32,0},{64,32},{96,64},{128,96},{160,128},{192,160},{224,1... | collective-permute-start | bytes 442376 | tf_op jit(solution)/shard_map/ppermute | solution.py:389
  117.8 2.5 %collective-permute-start.28 = (bf16[144,512]{1,0:T(8,128)(2,1)S(1)}, bf16[144,512]{1,0:T(8,128)(2,1)S(1)}, u32[]{:S(2)}, u32[]{:S(2)}) collective-permute-start(bf16[144,512]{1,0:T(8,128)(2,1)S(1)} %collective-permute-done.22.refs_3_), channel_id=1, source_target_pairs={{0,224},{32,0},{64,32},{96,64},{128,96},{160,128},{192,160},{224,1... | collective-permute-start | bytes 442376 | tf_op jit(solution)/shard_map/ppermute | solution.py:392
  120.2 0.5 collective-permute-done.30.refs_5_
  120.7 0.6 collective-permute-start.32
  121.4 3.4 %collective-permute-start.31 = (bf16[144,512]{1,0:T(8,128)(2,1)S(1)}, bf16[144,512]{1,0:T(8,128)(2,1)S(1)}, u32[]{:S(2)}, u32[]{:S(2)}) collective-permute-start(bf16[144,512]{1,0:T(8,128)(2,1)S(1)} %collective-permute-done.27.refs_0_), channel_id=1, source_target_pairs={{0,224},{32,0},{64,32},{96,64},{128,96},{160,128},{192,160},{224,1... | collective-permute-start | bytes 442376 | tf_op jit(solution)/shard_map/ppermute | solution.py:389
  124.8 2.4 %down_dots.2 = (f32[2,144,896]{2,1,0:T(8,128)S(1)}, f32[2,144,896]{2,1,0:T(8,128)S(1)}) custom-call(s32[1]{0:T(128)} %bitcast.1.c_ref, bf16[144,512]{1,0:T(8,128)(2,1)S(1)} %collective-permute-done.19.refs_0_, bf16[144,512]{1,0:T(8,128)(2,1)S(1)} %collective-permute-done.20.refs_1_, bf16[144,512]{1,0:T(8,128)(2,1)S(1)} %collective-permute-done.21.refs_2_, ...), custom_call_target="tpu_custom_call" | custom-call | flops 1056964608 | bytes 3670016 | tf_op jit(solution)/shard_map/down_dots/pallas_call | solution.py:221
  127.3 2.2 %collective-permute-done.32.refs_7_ = bf16[144,512]{1,0:T(8,128)(2,1)S(1)} collective-permute-done((bf16[144,512]{1,0:T(8,128)(2,1)S(1)}, bf16[144,512]{1,0:T(8,128)(2,1)S(1)}, u32[]{:S(2)}, u32[]{:S(2)}) %collective-permute-start.32) | collective-permute-done | bytes 147488 | tf_op jit(solution)/shard_map/ppermute | solution.py:390
  129.4 2.4 %down_dots.3 = (f32[2,144,896]{2,1,0:T(8,128)S(1)}, f32[2,144,896]{2,1,0:T(8,128)S(1)}) custom-call(s32[1]{0:T(128)} %bitcast.1.c_ref, bf16[144,512]{1,0:T(8,128)(2,1)S(1)} %collective-permute-done.27.refs_0_, bf16[144,512]{1,0:T(8,128)(2,1)S(1)} %collective-permute-done.28.refs_1_, bf16[144,512]{1,0:T(8,128)(2,1)S(1)} %get-tuple-element.64.refs_2_, ...), custom_call_target="tpu_custom_call" | custom-call | flops 1056964608 | bytes 3670016 | tf_op jit(solution)/shard_map/down_dots/pallas_call | solution.py:221
  131.9 0.1 pad_maximum_fusion
  132.0 7.9 %collective-permute-start.33 = (f32[4,144,896]{2,1,0:T(8,128)S(1)}, f32[4,144,896]{2,1,0:T(8,128)S(1)}, u32[]{:S(2)}, u32[]{:S(2)}) collective-permute-start(f32[4,144,896]{2,1,0:T(8,128)S(1)} %pad_maximum_fusion), channel_id=1, source_target_pairs={{0,1},{1,0},{2,3},{3,2},{4,5},{5,4},{6,7},{7,6},{8,9},{9,8},{10,11... | collective-permute-start | bytes 6193160 | tf_op jit(solution)/shard_map/ppermute | solution.py:402
  139.9 3.7 %collective-permute-done.33.came_ref = f32[4,144,896]{2,1,0:T(8,128)S(1)} collective-permute-done((f32[4,144,896]{2,1,0:T(8,128)S(1)}, f32[4,144,896]{2,1,0:T(8,128)S(1)}, u32[]{:S(2)}, u32[]{:S(2)}) %collective-permute-start.33) | collective-permute-done | bytes 2064416 | tf_op jit(solution)/shard_map/ppermute | solution.py:402
  143.6 0.2 settle.1
  143.8 18.1 %all_to_all.11 = bf16[16,32,896]{2,1,0:T(8,128)(2,1)S(1)} all-to-all(bf16[16,32,896]{2,1,0:T(8,128)(2,1)S(1)} %get-tuple-element.61), channel_id=1, replica_groups=mesh['dp'=8,'expert'=16,'tensor'=2] {'expert'}, dimensions={0} | all-to-all | bytes 1835008 | tf_op jit(solution)/shard_map/all_to_all | solution.py:404
  161.9 1.3 combine.1
  163.2 3.0 %collective-permute-start.34 = (bf16[16,896]{1,0:T(8,128)(2,1)S(1)}, bf16[16,896]{1,0:T(8,128)(2,1)S(1)}, u32[]{:S(2)}, u32[]{:S(2)}) collective-permute-start(bf16[16,896]{1,0:T(8,128)(2,1)S(1)} %get-tuple-element.68), channel_id=1, source_target_pairs={{0,32},{1,225},{32,64},{33,1},{64,96},{65,33},{96,128},{97,65},{12... | collective-permute-start | bytes 86024 | tf_op jit(solution)/shard_map/ppermute | solution.py:408
  166.3 3.8 %collective-permute-start.37 = (bf16[16,896]{1,0:T(8,128)(2,1)S(1)}, bf16[16,896]{1,0:T(8,128)(2,1)S(1)}, u32[]{:S(2)}, u32[]{:S(2)}) collective-permute-start(bf16[16,896]{1,0:T(8,128)(2,1)S(1)} %get-tuple-element.65), channel_id=1, source_target_pairs={{0,0},{1,129},{32,32},{33,161},{64,64},{65,193},{96,96},{97,225},{... | collective-permute-start | bytes 86024 | tf_op jit(solution)/shard_map/ppermute | solution.py:408
  170.0 0.9 collective-permute-start.36
  171.0 2.7 %collective-permute-start.35 = (bf16[16,896]{1,0:T(8,128)(2,1)S(1)}, bf16[16,896]{1,0:T(8,128)(2,1)S(1)}, u32[]{:S(2)}, u32[]{:S(2)}) collective-permute-start(bf16[16,896]{1,0:T(8,128)(2,1)S(1)} %get-tuple-element.67), channel_id=1, source_target_pairs={{0,64},{1,193},{32,96},{33,225},{64,128},{65,1},{96,160},{97,33},{... | collective-permute-start | bytes 86024 | tf_op jit(solution)/shard_map/ppermute | solution.py:408
  173.7 1.8 %collective-permute-done.35 = bf16[16,896]{1,0:T(8,128)(2,1)S(1)} collective-permute-done((bf16[16,896]{1,0:T(8,128)(2,1)S(1)}, bf16[16,896]{1,0:T(8,128)(2,1)S(1)}, u32[]{:S(2)}, u32[]{:S(2)}) %collective-permute-start.35) | collective-permute-done | bytes 28704 | tf_op jit(solution)/shard_map/ppermute | solution.py:408
  175.7 1.3 collective-permute-done.38.refs_1_
  177.0 1.3 assemble.1
  (71 shorter events, 2.2 us)
Async XLA Ops:
  0.1 0.9 copy-start.6
  1.0 0.7 copy-start.7
  1.7 0.7 copy-start.8
  3.5 11.7 %collective-permute-start = (bf16[16,1024]{1,0:T(8,128)(2,1)S(1)}, bf16[16,1024]{1,0:T(8,128)(2,1)S(1)}, u32[]{:S(2)}, u32[]{:S(2)}) collective-permute-start(bf16[16,1024]{1,0:T(8,128)(2,1)S(1)} %get-tuple-element.34), channel_id=1, source_target_pairs={{0,0},{1,129},{32,32},{33,161},{64,64},{65,193},{96,96},{97,225},{... | collective-permute-start | bytes 98312 | tf_op jit(solution)/shard_map/ppermute | solution.py:363
  13.1 4.1 %collective-permute-start.1 = (bf16[16,1024]{1,0:T(8,128)(2,1)S(1)}, bf16[16,1024]{1,0:T(8,128)(2,1)S(1)}, u32[]{:S(2)}, u32[]{:S(2)}) collective-permute-start(bf16[16,1024]{1,0:T(8,128)(2,1)S(1)} %get-tuple-element.35), channel_id=1, source_target_pairs={{0,224},{1,33},{32,0},{33,65},{64,32},{65,97},{96,64},{97,129},{12... | collective-permute-start | bytes 98312 | tf_op jit(solution)/shard_map/ppermute | solution.py:363
  13.9 4.9 %collective-permute-start.2 = (bf16[16,1024]{1,0:T(8,128)(2,1)S(1)}, bf16[16,1024]{1,0:T(8,128)(2,1)S(1)}, u32[]{:S(2)}, u32[]{:S(2)}) collective-permute-start(bf16[16,1024]{1,0:T(8,128)(2,1)S(1)} %get-tuple-element.36), channel_id=1, source_target_pairs={{0,192},{1,65},{32,224},{33,97},{64,0},{65,129},{96,32},{97,161},{... | collective-permute-start | bytes 98312 | tf_op jit(solution)/shard_map/ppermute | solution.py:363
  15.1 5.8 %collective-permute-start.3 = (bf16[16,1024]{1,0:T(8,128)(2,1)S(1)}, bf16[16,1024]{1,0:T(8,128)(2,1)S(1)}, u32[]{:S(2)}, u32[]{:S(2)}) collective-permute-start(bf16[16,1024]{1,0:T(8,128)(2,1)S(1)} %get-tuple-element.37), channel_id=1, source_target_pairs={{0,160},{1,97},{32,192},{33,129},{64,224},{65,161},{96,0},{97,193}... | collective-permute-start | bytes 98312 | tf_op jit(solution)/shard_map/ppermute | solution.py:363
  42.6 3.0 %copy-start.5 = (bf16[896,1024]{1,0:T(8,128)(2,1)S(1)}, bf16[896,1024]{1,0:T(8,128)(2,1)}, u32[]{:S(2)}) copy-start(bf16[896,1024]{1,0:T(8,128)(2,1)} %su_ref.3) | copy-start | bytes 5505028
  42.7 2.7 %collective-permute-start.4 = (bf16[576,896]{1,0:T(8,128)(2,1)S(1)}, bf16[576,896]{1,0:T(8,128)(2,1)S(1)}, u32[]{:S(2)}, u32[]{:S(2)}) collective-permute-start(bf16[576,896]{1,0:T(8,128)(2,1)S(1)} %pad_maximum_fusion.1), channel_id=1, source_target_pairs={{0,1},{1,0},{2,3},{3,2},{4,5},{5,4},{6,7},{7,6},{8,9},{9,8},{10,11... | collective-permute-start | bytes 3096584 | tf_op jit(solution)/shard_map/ppermute | solution.py:367
  42.8 2.8 %copy-start.4 = (bf16[896,1024]{1,0:T(8,128)(2,1)S(1)}, bf16[896,1024]{1,0:T(8,128)(2,1)}, u32[]{:S(2)}) copy-start(bf16[896,1024]{1,0:T(8,128)(2,1)} %sg_ref.3) | copy-start | bytes 5505028
  42.9 2.7 %copy-start.2 = (bf16[1,896,1024]{2,1,0:T(8,128)(2,1)S(1)}, bf16[1,896,1024]{2,1,0:T(8,128)(2,1)}, u32[]{:S(2)}) copy-start(bf16[1,896,1024]{2,1,0:T(8,128)(2,1)} %wg_ref.3) | copy-start | bytes 5505028
  42.9 2.9 %copy-start.3 = (bf16[1,896,1024]{2,1,0:T(8,128)(2,1)S(1)}, bf16[1,896,1024]{2,1,0:T(8,128)(2,1)}, u32[]{:S(2)}) copy-start(bf16[1,896,1024]{2,1,0:T(8,128)(2,1)} %wu_ref.3) | copy-start | bytes 5505028
  50.2 10.2 %collective-permute-start.15 = (f16[144,1024]{1,0:T(8,128)(2,1)S(1)}, f16[144,1024]{1,0:T(8,128)(2,1)S(1)}, u32[]{:S(2)}, u32[]{:S(2)}) collective-permute-start(f16[144,1024]{1,0:T(8,128)(2,1)S(1)} %convert_element_type.107), channel_id=1, source_target_pairs={{0,32},{32,64},{64,96},{96,128},{128,160},{160,192},{192,224},{224... | collective-permute-start | bytes 884744 | tf_op jit(solution)/shard_map/ppermute | solution.py:352
  52.1 9.0 %collective-permute-start.5 = (f16[144,1024]{1,0:T(8,128)(2,1)S(1)}, f16[144,1024]{1,0:T(8,128)(2,1)S(1)}, u32[]{:S(2)}, u32[]{:S(2)}) collective-permute-start(f16[144,1024]{1,0:T(8,128)(2,1)S(1)} %convert_element_type.87), channel_id=1, source_target_pairs={{0,224},{32,0},{64,32},{96,64},{128,96},{160,128},{192,160},{224,1... | collective-permute-start | bytes 884744 | tf_op jit(solution)/shard_map/ppermute | solution.py:352
  58.8 10.1 %collective-permute-start.12 = (f16[144,1024]{1,0:T(8,128)(2,1)S(1)}, f16[144,1024]{1,0:T(8,128)(2,1)S(1)}, u32[]{:S(2)}, u32[]{:S(2)}) collective-permute-start(f16[144,1024]{1,0:T(8,128)(2,1)S(1)} %convert_element_type.101), channel_id=1, source_target_pairs={{0,224},{32,0},{64,32},{96,64},{128,96},{160,128},{192,160},{224,1... | collective-permute-start | bytes 884744 | tf_op jit(solution)/shard_map/ppermute | solution.py:352
  59.9 8.6 %collective-permute-start.9 = (f16[144,1024]{1,0:T(8,128)(2,1)S(1)}, f16[144,1024]{1,0:T(8,128)(2,1)S(1)}, u32[]{:S(2)}, u32[]{:S(2)}) collective-permute-start(f16[144,1024]{1,0:T(8,128)(2,1)S(1)} %convert_element_type.95), channel_id=1, source_target_pairs={{0,32},{32,64},{64,96},{96,128},{128,160},{160,192},{192,224},{224... | collective-permute-start | bytes 884744 | tf_op jit(solution)/shard_map/ppermute | solution.py:352
  60.4 20.9 %collective-permute-start.16 = (f16[144,1024]{1,0:T(8,128)(2,1)S(1)}, f16[144,1024]{1,0:T(8,128)(2,1)S(1)}, u32[]{:S(2)}, u32[]{:S(2)}) collective-permute-start(f16[144,1024]{1,0:T(8,128)(2,1)S(1)} %add_convert_fusion.2), channel_id=1, source_target_pairs={{0,32},{32,64},{64,96},{96,128},{128,160},{160,192},{192,224},{224... | collective-permute-start | bytes 884744 | tf_op jit(solution)/shard_map/ppermute | solution.py:352
  61.2 11.8 %collective-permute-start.6 = (f16[144,1024]{1,0:T(8,128)(2,1)S(1)}, f16[144,1024]{1,0:T(8,128)(2,1)S(1)}, u32[]{:S(2)}, u32[]{:S(2)}) collective-permute-start(f16[144,1024]{1,0:T(8,128)(2,1)S(1)} %add_convert_fusion.9), channel_id=1, source_target_pairs={{0,224},{32,0},{64,32},{96,64},{128,96},{160,128},{192,160},{224,1... | collective-permute-start | bytes 884744 | tf_op jit(solution)/shard_map/ppermute | solution.py:352
  68.6 12.6 %collective-permute-start.10 = (f16[144,1024]{1,0:T(8,128)(2,1)S(1)}, f16[144,1024]{1,0:T(8,128)(2,1)S(1)}, u32[]{:S(2)}, u32[]{:S(2)}) collective-permute-start(f16[144,1024]{1,0:T(8,128)(2,1)S(1)} %add_convert_fusion.6), channel_id=1, source_target_pairs={{0,32},{32,64},{64,96},{96,128},{128,160},{160,192},{192,224},{224... | collective-permute-start | bytes 884744 | tf_op jit(solution)/shard_map/ppermute | solution.py:352
  69.0 12.6 %collective-permute-start.13 = (f16[144,1024]{1,0:T(8,128)(2,1)S(1)}, f16[144,1024]{1,0:T(8,128)(2,1)S(1)}, u32[]{:S(2)}, u32[]{:S(2)}) collective-permute-start(f16[144,1024]{1,0:T(8,128)(2,1)S(1)} %add_convert_fusion.4), channel_id=1, source_target_pairs={{0,224},{32,0},{64,32},{96,64},{128,96},{160,128},{192,160},{224,1... | collective-permute-start | bytes 884744 | tf_op jit(solution)/shard_map/ppermute | solution.py:352
  73.1 12.0 %collective-permute-start.7 = (f16[144,1024]{1,0:T(8,128)(2,1)S(1)}, f16[144,1024]{1,0:T(8,128)(2,1)S(1)}, u32[]{:S(2)}, u32[]{:S(2)}) collective-permute-start(f16[144,1024]{1,0:T(8,128)(2,1)S(1)} %add_convert_fusion.8), channel_id=1, source_target_pairs={{0,224},{32,0},{64,32},{96,64},{128,96},{160,128},{192,160},{224,1... | collective-permute-start | bytes 884744 | tf_op jit(solution)/shard_map/ppermute | solution.py:352
  81.2 14.3 %collective-permute-start.11 = (f16[144,1024]{1,0:T(8,128)(2,1)S(1)}, f16[144,1024]{1,0:T(8,128)(2,1)S(1)}, u32[]{:S(2)}, u32[]{:S(2)}) collective-permute-start(f16[144,1024]{1,0:T(8,128)(2,1)S(1)} %add_convert_fusion.5), channel_id=1, source_target_pairs={{0,32},{32,64},{64,96},{96,128},{128,160},{160,192},{192,224},{224... | collective-permute-start | bytes 884744 | tf_op jit(solution)/shard_map/ppermute | solution.py:352
  81.4 13.9 %collective-permute-start.17 = (f16[144,1024]{1,0:T(8,128)(2,1)S(1)}, f16[144,1024]{1,0:T(8,128)(2,1)S(1)}, u32[]{:S(2)}, u32[]{:S(2)}) collective-permute-start(f16[144,1024]{1,0:T(8,128)(2,1)S(1)} %add_convert_fusion.1), channel_id=1, source_target_pairs={{0,32},{32,64},{64,96},{96,128},{128,160},{160,192},{192,224},{224... | collective-permute-start | bytes 884744 | tf_op jit(solution)/shard_map/ppermute | solution.py:352
  81.6 13.9 %collective-permute-start.14 = (f16[144,1024]{1,0:T(8,128)(2,1)S(1)}, f16[144,1024]{1,0:T(8,128)(2,1)S(1)}, u32[]{:S(2)}, u32[]{:S(2)}) collective-permute-start(f16[144,1024]{1,0:T(8,128)(2,1)S(1)} %add_convert_fusion.3), channel_id=1, source_target_pairs={{0,224},{32,0},{64,32},{96,64},{128,96},{160,128},{192,160},{224,1... | collective-permute-start | bytes 884744 | tf_op jit(solution)/shard_map/ppermute | solution.py:352
  85.2 12.5 %collective-permute-start.8 = (f16[144,1024]{1,0:T(8,128)(2,1)S(1)}, f16[144,1024]{1,0:T(8,128)(2,1)S(1)}, u32[]{:S(2)}, u32[]{:S(2)}) collective-permute-start(f16[144,1024]{1,0:T(8,128)(2,1)S(1)} %add_convert_fusion.7), channel_id=1, source_target_pairs={{0,224},{32,0},{64,32},{96,64},{128,96},{160,128},{192,160},{224,1... | collective-permute-start | bytes 884744 | tf_op jit(solution)/shard_map/ppermute | solution.py:352
  95.4 29.4 %copy-start = (bf16[1,1024,896]{2,1,0:T(8,128)(2,1)S(1)}, bf16[1,1024,896]{2,1,0:T(8,128)(2,1)}, u32[]{:S(2)}) copy-start(bf16[1,1024,896]{2,1,0:T(8,128)(2,1)} %refs_8_.3) | copy-start | bytes 5505028
  95.4 29.4 %copy-start.1 = (bf16[1024,896]{1,0:T(8,128)(2,1)S(1)}, bf16[1024,896]{1,0:T(8,128)(2,1)}, u32[]{:S(2)}) copy-start(bf16[1024,896]{1,0:T(8,128)(2,1)} %refs_9_.3) | copy-start | bytes 5505028
  95.4 6.9 %collective-permute-start.18 = (f16[144,1024]{1,0:T(8,128)(2,1)S(1)}, f16[144,1024]{1,0:T(8,128)(2,1)S(1)}, u32[]{:S(2)}, u32[]{:S(2)}) collective-permute-start(f16[144,1024]{1,0:T(8,128)(2,1)S(1)} %add_convert_fusion), channel_id=1, source_target_pairs={{0,32},{32,64},{64,96},{96,128},{128,160},{160,192},{192,224},{224... | collective-permute-start | bytes 884744 | tf_op jit(solution)/shard_map/ppermute | solution.py:352
  102.7 5.3 %collective-permute-start.24 = (bf16[144,512]{1,0:T(8,128)(2,1)S(1)}, bf16[144,512]{1,0:T(8,128)(2,1)S(1)}, u32[]{:S(2)}, u32[]{:S(2)}) collective-permute-start(bf16[144,512]{1,0:T(8,128)(2,1)S(1)} %get-tuple-element.63.refs_3_), channel_id=1, source_target_pairs={{0,32},{32,64},{64,96},{96,128},{128,160},{160,192},{192,224},{224... | collective-permute-start | bytes 442376 | tf_op jit(solution)/shard_map/ppermute | solution.py:390
  102.8 5.2 %collective-permute-start.19 = (bf16[144,512]{1,0:T(8,128)(2,1)S(1)}, bf16[144,512]{1,0:T(8,128)(2,1)S(1)}, u32[]{:S(2)}, u32[]{:S(2)}) collective-permute-start(bf16[144,512]{1,0:T(8,128)(2,1)S(1)} %get-tuple-element.64.refs_2_), channel_id=1, source_target_pairs={{0,224},{32,0},{64,32},{96,64},{128,96},{160,128},{192,160},{224,1... | collective-permute-start | bytes 442376 | tf_op jit(solution)/shard_map/ppermute | solution.py:389
  105.5 5.2 %collective-permute-start.20 = (bf16[144,512]{1,0:T(8,128)(2,1)S(1)}, bf16[144,512]{1,0:T(8,128)(2,1)S(1)}, u32[]{:S(2)}, u32[]{:S(2)}) collective-permute-start(bf16[144,512]{1,0:T(8,128)(2,1)S(1)} %get-tuple-element.63.refs_3_), channel_id=1, source_target_pairs={{0,224},{32,0},{64,32},{96,64},{128,96},{160,128},{192,160},{224,1... | collective-permute-start | bytes 442376 | tf_op jit(solution)/shard_map/ppermute | solution.py:392
  105.5 6.8 %collective-permute-start.23 = (bf16[144,512]{1,0:T(8,128)(2,1)S(1)}, bf16[144,512]{1,0:T(8,128)(2,1)S(1)}, u32[]{:S(2)}, u32[]{:S(2)}) collective-permute-start(bf16[144,512]{1,0:T(8,128)(2,1)S(1)} %get-tuple-element.64.refs_2_), channel_id=1, source_target_pairs={{0,32},{32,64},{64,96},{96,128},{128,160},{160,192},{192,224},{224... | collective-permute-start | bytes 442376 | tf_op jit(solution)/shard_map/ppermute | solution.py:393
  108.0 6.1 %collective-permute-start.26 = (bf16[144,512]{1,0:T(8,128)(2,1)S(1)}, bf16[144,512]{1,0:T(8,128)(2,1)S(1)}, u32[]{:S(2)}, u32[]{:S(2)}) collective-permute-start(bf16[144,512]{1,0:T(8,128)(2,1)S(1)} %collective-permute-done.24.refs_5_), channel_id=1, source_target_pairs={{0,32},{32,64},{64,96},{96,128},{128,160},{160,192},{192,224},{224... | collective-permute-start | bytes 442376 | tf_op jit(solution)/shard_map/ppermute | solution.py:390
  108.0 6.4 %collective-permute-start.21 = (bf16[144,512]{1,0:T(8,128)(2,1)S(1)}, bf16[144,512]{1,0:T(8,128)(2,1)S(1)}, u32[]{:S(2)}, u32[]{:S(2)}) collective-permute-start(bf16[144,512]{1,0:T(8,128)(2,1)S(1)} %collective-permute-done.19.refs_0_), channel_id=1, source_target_pairs={{0,224},{32,0},{64,32},{96,64},{128,96},{160,128},{192,160},{224,1... | collective-permute-start | bytes 442376 | tf_op jit(solution)/shard_map/ppermute | solution.py:389
  110.7 7.1 %collective-permute-start.22 = (bf16[144,512]{1,0:T(8,128)(2,1)S(1)}, bf16[144,512]{1,0:T(8,128)(2,1)S(1)}, u32[]{:S(2)}, u32[]{:S(2)}) collective-permute-start(bf16[144,512]{1,0:T(8,128)(2,1)S(1)} %collective-permute-done.20.refs_1_), channel_id=1, source_target_pairs={{0,224},{32,0},{64,32},{96,64},{128,96},{160,128},{192,160},{224,1... | collective-permute-start | bytes 442376 | tf_op jit(solution)/shard_map/ppermute | solution.py:392
  112.3 8.0 %collective-permute-start.25 = (bf16[144,512]{1,0:T(8,128)(2,1)S(1)}, bf16[144,512]{1,0:T(8,128)(2,1)S(1)}, u32[]{:S(2)}, u32[]{:S(2)}) collective-permute-start(bf16[144,512]{1,0:T(8,128)(2,1)S(1)} %collective-permute-done.23.refs_4_), channel_id=1, source_target_pairs={{0,32},{32,64},{64,96},{96,128},{128,160},{160,192},{192,224},{224... | collective-permute-start | bytes 442376 | tf_op jit(solution)/shard_map/ppermute | solution.py:393
  114.1 6.6 %collective-permute-start.30 = (bf16[144,512]{1,0:T(8,128)(2,1)S(1)}, bf16[144,512]{1,0:T(8,128)(2,1)S(1)}, u32[]{:S(2)}, u32[]{:S(2)}) collective-permute-start(bf16[144,512]{1,0:T(8,128)(2,1)S(1)} %collective-permute-done.26.refs_7_), channel_id=1, source_target_pairs={{0,32},{32,64},{64,96},{96,128},{128,160},{160,192},{192,224},{224... | collective-permute-start | bytes 442376 | tf_op jit(solution)/shard_map/ppermute | solution.py:390
  114.4 7.0 %collective-permute-start.27 = (bf16[144,512]{1,0:T(8,128)(2,1)S(1)}, bf16[144,512]{1,0:T(8,128)(2,1)S(1)}, u32[]{:S(2)}, u32[]{:S(2)}) collective-permute-start(bf16[144,512]{1,0:T(8,128)(2,1)S(1)} %collective-permute-done.21.refs_2_), channel_id=1, source_target_pairs={{0,224},{32,0},{64,32},{96,64},{128,96},{160,128},{192,160},{224,1... | collective-permute-start | bytes 442376 | tf_op jit(solution)/shard_map/ppermute | solution.py:389
  117.8 9.5 %collective-permute-start.28 = (bf16[144,512]{1,0:T(8,128)(2,1)S(1)}, bf16[144,512]{1,0:T(8,128)(2,1)S(1)}, u32[]{:S(2)}, u32[]{:S(2)}) collective-permute-start(bf16[144,512]{1,0:T(8,128)(2,1)S(1)} %collective-permute-done.22.refs_3_), channel_id=1, source_target_pairs={{0,224},{32,0},{64,32},{96,64},{128,96},{160,128},{192,160},{224,1... | collective-permute-start | bytes 442376 | tf_op jit(solution)/shard_map/ppermute | solution.py:392
  120.2 7.0 %collective-permute-start.29 = (bf16[144,512]{1,0:T(8,128)(2,1)S(1)}, bf16[144,512]{1,0:T(8,128)(2,1)S(1)}, u32[]{:S(2)}, u32[]{:S(2)}) collective-permute-start(bf16[144,512]{1,0:T(8,128)(2,1)S(1)} %collective-permute-done.25.refs_6_), channel_id=1, source_target_pairs={{0,32},{32,64},{64,96},{96,128},{128,160},{160,192},{192,224},{224... | collective-permute-start | bytes 442376 | tf_op jit(solution)/shard_map/ppermute | solution.py:393
  120.7 8.7 %collective-permute-start.32 = (bf16[144,512]{1,0:T(8,128)(2,1)S(1)}, bf16[144,512]{1,0:T(8,128)(2,1)S(1)}, u32[]{:S(2)}, u32[]{:S(2)}) collective-permute-start(bf16[144,512]{1,0:T(8,128)(2,1)S(1)} %collective-permute-done.30.refs_5_), channel_id=1, source_target_pairs={{0,32},{32,64},{64,96},{96,128},{128,160},{160,192},{192,224},{224... | collective-permute-start | bytes 442376 | tf_op jit(solution)/shard_map/ppermute | solution.py:390
  121.4 8.1 %collective-permute-start.31 = (bf16[144,512]{1,0:T(8,128)(2,1)S(1)}, bf16[144,512]{1,0:T(8,128)(2,1)S(1)}, u32[]{:S(2)}, u32[]{:S(2)}) collective-permute-start(bf16[144,512]{1,0:T(8,128)(2,1)S(1)} %collective-permute-done.27.refs_0_), channel_id=1, source_target_pairs={{0,224},{32,0},{64,32},{96,64},{128,96},{160,128},{192,160},{224,1... | collective-permute-start | bytes 442376 | tf_op jit(solution)/shard_map/ppermute | solution.py:389
  132.0 11.6 %collective-permute-start.33 = (f32[4,144,896]{2,1,0:T(8,128)S(1)}, f32[4,144,896]{2,1,0:T(8,128)S(1)}, u32[]{:S(2)}, u32[]{:S(2)}) collective-permute-start(f32[4,144,896]{2,1,0:T(8,128)S(1)} %pad_maximum_fusion), channel_id=1, source_target_pairs={{0,1},{1,0},{2,3},{3,2},{4,5},{5,4},{6,7},{7,6},{8,9},{9,8},{10,11... | collective-permute-start | bytes 6193160 | tf_op jit(solution)/shard_map/ppermute | solution.py:402
  163.2 10.4 %collective-permute-start.34 = (bf16[16,896]{1,0:T(8,128)(2,1)S(1)}, bf16[16,896]{1,0:T(8,128)(2,1)S(1)}, u32[]{:S(2)}, u32[]{:S(2)}) collective-permute-start(bf16[16,896]{1,0:T(8,128)(2,1)S(1)} %get-tuple-element.68), channel_id=1, source_target_pairs={{0,32},{1,225},{32,64},{33,1},{64,96},{65,33},{96,128},{97,65},{12... | collective-permute-start | bytes 86024 | tf_op jit(solution)/shard_map/ppermute | solution.py:408
  166.3 9.3 %collective-permute-start.37 = (bf16[16,896]{1,0:T(8,128)(2,1)S(1)}, bf16[16,896]{1,0:T(8,128)(2,1)S(1)}, u32[]{:S(2)}, u32[]{:S(2)}) collective-permute-start(bf16[16,896]{1,0:T(8,128)(2,1)S(1)} %get-tuple-element.65), channel_id=1, source_target_pairs={{0,0},{1,129},{32,32},{33,161},{64,64},{65,193},{96,96},{97,225},{... | collective-permute-start | bytes 86024 | tf_op jit(solution)/shard_map/ppermute | solution.py:408
  170.0 5.5 %collective-permute-start.36 = (bf16[16,896]{1,0:T(8,128)(2,1)S(1)}, bf16[16,896]{1,0:T(8,128)(2,1)S(1)}, u32[]{:S(2)}, u32[]{:S(2)}) collective-permute-start(bf16[16,896]{1,0:T(8,128)(2,1)S(1)} %get-tuple-element.66), channel_id=1, source_target_pairs={{0,96},{1,161},{32,128},{33,193},{64,160},{65,225},{96,192},{97,1}... | collective-permute-start | bytes 86024 | tf_op jit(solution)/shard_map/ppermute | solution.py:408
  171.0 4.5 %collective-permute-start.35 = (bf16[16,896]{1,0:T(8,128)(2,1)S(1)}, bf16[16,896]{1,0:T(8,128)(2,1)S(1)}, u32[]{:S(2)}, u32[]{:S(2)}) collective-permute-start(bf16[16,896]{1,0:T(8,128)(2,1)S(1)} %get-tuple-element.67), channel_id=1, source_target_pairs={{0,64},{1,193},{32,96},{33,225},{64,128},{65,1},{96,160},{97,33},{... | collective-permute-start | bytes 86024 | tf_op jit(solution)/shard_map/ppermute | solution.py:408
  175.6 1.4 collective-permute-start.38

commit v3 on v2

--- a/solution.py
+++ b/solution.py
@@ -213,7 +213,7 @@
     c = c_ref[0]
     for i in range(n):
         keep_ref[i] = full_ref[c * n + i]
-        send_ref[i] = full_ref[(1 - c) * n + i]
+        send_ref[i] = full_ref[(1 - c) * n + i].astype(jnp.bfloat16)
 
 
 def down_dots(c, xs, wd, sd):
@@ -222,7 +222,7 @@
         down_kernel,
         out_shape=(
             jax.ShapeDtypeStruct((n, CHUNK, BLOCK), jnp.float32),
-            jax.ShapeDtypeStruct((n, CHUNK, BLOCK), jnp.float32),
+            jax.ShapeDtypeStruct((n, CHUNK, BLOCK), jnp.bfloat16),
         ),
         in_specs=[SMEM] + [VMEM] * (len(xs) + 2),
         out_specs=(VMEM, VMEM),
@@ -242,9 +242,9 @@
 def settle_kernel(near_ref, far_ref, came_ref, rows_ref, shared_ref):
     for i in range(4):
         keep = (near_ref, far_ref)[i // 2]
-        total = keep[i % 2, :ROWS] + came_ref[i, :ROWS]
+        total = keep[i % 2, :ROWS] + came_ref[i, :ROWS].astype(jnp.float32)
         rows_ref[:, i * CAP : (i + 1) * CAP, :] = total.reshape(EXPERTS, CAP, BLOCK).astype(jnp.bfloat16)
-        shared_ref[i * PADT : (i + 1) * PADT] = keep[i % 2, ROWS:] + came_ref[i, ROWS:]
+        shared_ref[i * PADT : (i + 1) * PADT] = keep[i % 2, ROWS:] + came_ref[i, ROWS:].astype(jnp.float32)
 
 
 def settle(near, far, came):
@@ -261,7 +261,7 @@
     )(near, far, came)
 
 
-def combine_kernel(ext_ref, back_ref, shared_ref, out_ref, terms_ref, total_ref):
+def terms_kernel(ext_ref, terms_ref):
     rows = 4 * PADT
     cols = 4 * ROWS
     ext = jnp.concatenate([ext_ref[PADT:], ext_ref[:PADT]], axis=0).astype(jnp.float32)
@@ -288,6 +288,20 @@
     low = (rest - mid.astype(jnp.float32)).astype(jnp.bfloat16)
     for i, term in enumerate((low, mid, hi)):
         terms_ref[i] = term
+
+
+def terms(ext):
+    return pl.pallas_call(
+        terms_kernel,
+        out_shape=jax.ShapeDtypeStruct((3, 4 * PADT, 4 * ROWS), jnp.bfloat16),
+        in_specs=[VMEM],
+        out_specs=VMEM,
+        compiler_params=PARAMS,
+        name="terms",
+    )(ext)
+
+
+def combine_kernel(terms_ref, back_ref, shared_ref, out_ref, total_ref):
     total_ref[...] = shared_ref[...]
 
     def add(i, carry):
@@ -298,19 +312,18 @@
     out_ref[...] = total_ref[...].astype(jnp.bfloat16)
 
 
-def combine(ext, back, shared):
+def combine(scales, back, shared):
     return pl.pallas_call(
         combine_kernel,
         out_shape=jax.ShapeDtypeStruct((4 * PADT, BLOCK), jnp.bfloat16),
         in_specs=[VMEM, VMEM, VMEM],
         out_specs=VMEM,
         scratch_shapes=[
-            pltpu.VMEM((3, 4 * PADT, 4 * ROWS), jnp.bfloat16),
             pltpu.VMEM((4 * PADT, BLOCK), jnp.float32),
         ],
         compiler_params=PARAMS,
         name="combine",
-    )(ext, back, shared)
+    )(scales, back, shared)
 
 
 def assemble_kernel(s_ref, *refs):
@@ -357,7 +370,8 @@
     z = lax.axis_index("dp")
     c = lax.axis_index("tensor")
     c1, zc = c.reshape(1), jnp.stack([z, c])
-    sent = prep(zc, tokens, ids.T, weights.T)
+    held_out = [pltpu.with_memory_space_constraint(a, pltpu.HBM) for a in (tokens, ids.T, weights.T)]
+    sent = prep(zc, *held_out)
     came = []
     for j, piece in enumerate(sent):
         came.append(lax.ppermute(piece, ("dp", "tensor"), paired(-j, -j) if j else paired(0, 4)))
@@ -394,6 +408,7 @@
             got[ZN - j], got[j] = (pd, qd), (pu, qu)
         else:
             got[4] = (pd, qu)
+    scales = terms(ext)
     keeps, sends = [], []
     for a, b in (((7, 6), (1, 2)), ((5, 0), (3, 4))):
         keep, send = down_dots(c1, [p for k in a + b for p in got[k]], wd, sd)
@@ -402,7 +417,7 @@
     crossed = lax.ppermute(jnp.concatenate(sends), "tensor", SWAP)
     rows, shared = settle(*keeps, crossed)
     back = lax.all_to_all(rows, "expert", 0, 0, tiled=True).reshape(4 * ROWS, BLOCK)
-    mixed = combine(ext, back, shared)
+    mixed = combine(scales, back, shared)
     held = []
     for i, (to, fro) in enumerate(((1, 1), (2, 2), (3, 3), (0, 4))):
         held.append(lax.ppermute(mixed[i * PADT : (i + 1) * PADT], ("dp", "tensor"), paired(to, fro)))

time: 179 us -> 176 us (0.983)
  blocking collectives: 39.2 us -> 21.1 us
  waiting for transfers between devices: 49.7 us -> 62.7 us
  starting transfers between devices: 65.2 us -> 68.8 us
  local copies, waits for them, and re-layouts: 2.84 us -> 0.53 us
    all_to_all x1 -> x0, blocking collectives: 18.1 us -> none  [layer(): lax.all_to_all(rows, 'expert', 0, 0, tiled=True).reshape(4 * ROWS, BLOCK)]
    all_to_all x0 -> x1, waiting for transfers between devices: none -> 14.7 us  [layer(): lax.all_to_all(rows, 'expert', 0, 0, tiled=True).reshape(4 * ROWS, BLOCK)]
    all_to_all x0 -> x1, starting transfers between devices: none -> 3.63 us  [layer(): lax.all_to_all(rows, 'expert', 0, 0, tiled=True).reshape(4 * ROWS, BLOCK)]
    unnamed x21 -> x15, local copies, waits for them, and re-layouts: 2.56 us -> 0.25 us
  transfers between devices with their start and end apart: 39 -> 40, of which waited for: 19 -> 21; matrix products, arithmetic and copies ran while one was open for 1% -> 1% of each run, Pallas kernels for 5% -> 5%
where the time goes in v3:
time: 176 us
  starting transfers between devices  68.8 us (39%)
  waiting for transfers between devices  62.7 us (36%)
  blocking collectives  21.1 us (12%)
  Pallas kernels  20.8 us (12%)
    ppermute x14, waiting for transfers between devices, ring(): total = lax.ppermute(total.astype(LINK), 'dp', shifted(shift))  29.4 us
    all_to_all x1, blocking collectives, layer(): arrived = lax.all_to_all(packed, 'expert', 0, 0, tiled=True)  21.1 us
    ppermute x14, starting transfers between devices, ring(): total = lax.ppermute(total.astype(LINK), 'dp', shifted(shift))  16 us
    all_to_all x1, waiting for transfers between devices, layer(): lax.all_to_all(rows, 'expert', 0, 0, tiled=True).reshape(4 * ROWS, BLOCK)  14.7 us
    ppermute x4, starting transfers between devices, layer(): pd = lax.ppermute(pd, 'dp', shifted(-1))  12.1 us
    ppermute x4, starting transfers between devices, layer(): lax.ppermute(piece, ('dp', 'tensor'), paired(-j, -j) if j else paired(0, 4))  11.6 us
    ppermute x4, starting transfers between devices, layer(): lax.ppermute(mixed[i * PADT:(i + 1) * PADT], ('dp', 'tensor'), paired(to,...  10.4 us
    pallas_call x2, Pallas kernels, up_dots(): pl.pallas_call(functools.partial(up_kernel, ks), grid=(FFH // NT,), out_s...  9.89 us
  transfers between devices with their start and end apart: 40, of which 21 were waited for; matrix products, arithmetic and copies ran while one was open for 1% of the time, Pallas kernels for 5%

profile of v3, /device:TPU:1, one launch (start us, length us, event | category | flops | bytes accessed | tf_op | source)
XLA Modules:
  0.0 176.0 jit_solution(8991985375881813489)
XLA Ops:
  0.1 1.7 prep.1
  1.8 9.6 %collective-permute-start = (bf16[16,1024]{1,0:T(8,128)(2,1)S(1)}, bf16[16,1024]{1,0:T(8,128)(2,1)S(1)}, u32[]{:S(2)}, u32[]{:S(2)}) collective-permute-start(bf16[16,1024]{1,0:T(8,128)(2,1)S(1)} %get-tuple-element.34), channel_id=1, source_target_pairs={{0,0},{1,129},{32,32},{33,161},{64,64},{65,193},{96,96},{97,225},{... | collective-permute-start | bytes 98312 | tf_op jit(solution)/shard_map/ppermute | solution.py:377
  11.4 0.8 collective-permute-start.1
  12.3 1.2 collective-permute-start.2
  13.5 2.0 %collective-permute-done.1.refs_1_ = bf16[16,1024]{1,0:T(8,128)(2,1)S(1)} collective-permute-done((bf16[16,1024]{1,0:T(8,128)(2,1)S(1)}, bf16[16,1024]{1,0:T(8,128)(2,1)S(1)}, u32[]{:S(2)}, u32[]{:S(2)}) %collective-permute-start.1) | collective-permute-done | bytes 32800 | tf_op jit(solution)/shard_map/ppermute | solution.py:377
  15.5 1.7 collective-permute-done.2.refs_2_
  17.2 2.1 %collective-permute-done.3.refs_3_ = bf16[16,1024]{1,0:T(8,128)(2,1)S(1)} collective-permute-done((bf16[16,1024]{1,0:T(8,128)(2,1)S(1)}, bf16[16,1024]{1,0:T(8,128)(2,1)S(1)}, u32[]{:S(2)}, u32[]{:S(2)}) %collective-permute-start.3) | collective-permute-done | bytes 32800 | tf_op jit(solution)/shard_map/ppermute | solution.py:377
  19.2 0.6 pack.1
  19.8 21.1 %all_to_all.10 = bf16[16,32,896]{2,1,0:T(8,128)(2,1)S(1)} all-to-all(bf16[16,32,896]{2,1,0:T(8,128)(2,1)S(1)} %get-tuple-element.39), channel_id=1, replica_groups=mesh['dp'=8,'expert'=16,'tensor'=2] {'expert'}, dimensions={0} | all-to-all | bytes 1835008 | tf_op jit(solution)/shard_map/all_to_all | solution.py:379
  41.3 2.5 %collective-permute-done.4 = bf16[576,896]{1,0:T(8,128)(2,1)S(1)} collective-permute-done((bf16[576,896]{1,0:T(8,128)(2,1)S(1)}, bf16[576,896]{1,0:T(8,128)(2,1)S(1)}, u32[]{:S(2)}, u32[]{:S(2)}) %collective-permute-start.4) | collective-permute-done | bytes 1032224 | tf_op jit(solution)/shard_map/ppermute | solution.py:381
  44.0 0.2 copy-done.3
  44.2 4.2 %shard_map.92 = (f32[144,1024]{1,0:T(8,128)S(1)}, f32[144,1024]{1,0:T(8,128)S(1)}, f32[144,1024]{1,0:T(8,128)S(1)}, f32[144,1024]{1,0:T(8,128)S(1)}, f32[144,1024]{1,0:T(8,128)S(1)}, /*index=5*/f32[144,1024]{1,0:T(8,128)S(1)}) custom-call(s32[1]{0:T(128)} %bitcast.1.c_ref, bf16[4,128,896]{2,1,0:T(8,128)(2,1)S(1)} %copy_bitcast_fusion.1.own_ref, ...), custom_call_target="tpu_custom_call" | custom-call | flops 1585446912 | bytes 7340032 | tf_op jit(solution)/shard_map/pallas_call | solution.py:169
  48.5 1.9 %collective-permute-start.15 = (f16[144,1024]{1,0:T(8,128)(2,1)S(1)}, f16[144,1024]{1,0:T(8,128)(2,1)S(1)}, u32[]{:S(2)}, u32[]{:S(2)}) collective-permute-start(f16[144,1024]{1,0:T(8,128)(2,1)S(1)} %convert_element_type.107), channel_id=1, source_target_pairs={{0,32},{32,64},{64,96},{96,128},{128,160},{160,192},{192,224},{224... | collective-permute-start | bytes 884744 | tf_op jit(solution)/shard_map/ppermute | solution.py:365
  50.5 0.9 collective-permute-start.5
  51.4 5.7 %shard_map.91 = (f32[144,1024]{1,0:T(8,128)S(1)}, f32[144,1024]{1,0:T(8,128)S(1)}, f32[144,1024]{1,0:T(8,128)S(1)}, f32[144,1024]{1,0:T(8,128)S(1)}, f32[144,102...) custom-call(s32[1]{0:T(128)} %bitcast.1.c_ref, ...), custom_call_target="tpu_custom_call" | custom-call | flops 2642411520 | bytes 7340032 | tf_op jit(solution)/shard_map/pallas_call | solution.py:169
  57.1 1.1 collective-permute-start.12
  58.3 0.4 collective-permute-start.9
  58.8 0.7 collective-permute-start.16
  59.6 2.1 %collective-permute-start.6 = (f16[144,1024]{1,0:T(8,128)(2,1)S(1)}, f16[144,1024]{1,0:T(8,128)(2,1)S(1)}, u32[]{:S(2)}, u32[]{:S(2)}) collective-permute-start(f16[144,1024]{1,0:T(8,128)(2,1)S(1)} %add_convert_fusion.9), channel_id=1, source_target_pairs={{0,224},{32,0},{64,32},{96,64},{128,96},{160,128},{192,160},{224,1... | collective-permute-start | bytes 884744 | tf_op jit(solution)/shard_map/ppermute | solution.py:365
  61.7 5.2 %collective-permute-done.9 = f16[144,1024]{1,0:T(8,128)(2,1)S(1)} collective-permute-done((f16[144,1024]{1,0:T(8,128)(2,1)S(1)}, f16[144,1024]{1,0:T(8,128)(2,1)S(1)}, u32[]{:S(2)}, u32[]{:S(2)}) %collective-permute-start.9) | collective-permute-done | bytes 294944 | tf_op jit(solution)/shard_map/ppermute | solution.py:365
  67.0 0.3 collective-permute-start.10
  67.3 2.7 %collective-permute-start.13 = (f16[144,1024]{1,0:T(8,128)(2,1)S(1)}, f16[144,1024]{1,0:T(8,128)(2,1)S(1)}, u32[]{:S(2)}, u32[]{:S(2)}) collective-permute-start(f16[144,1024]{1,0:T(8,128)(2,1)S(1)} %add_convert_fusion.4), channel_id=1, source_target_pairs={{0,224},{32,0},{64,32},{96,64},{128,96},{160,128},{192,160},{224,1... | collective-permute-start | bytes 884744 | tf_op jit(solution)/shard_map/ppermute | solution.py:365
  70.1 1.4 collective-permute-done.6
  71.5 2.1 %collective-permute-start.7 = (f16[144,1024]{1,0:T(8,128)(2,1)S(1)}, f16[144,1024]{1,0:T(8,128)(2,1)S(1)}, u32[]{:S(2)}, u32[]{:S(2)}) collective-permute-start(f16[144,1024]{1,0:T(8,128)(2,1)S(1)} %add_convert_fusion.8), channel_id=1, source_target_pairs={{0,224},{32,0},{64,32},{96,64},{128,96},{160,128},{192,160},{224,1... | collective-permute-start | bytes 884744 | tf_op jit(solution)/shard_map/ppermute | solution.py:365
  73.6 5.9 %collective-permute-done.10 = f16[144,1024]{1,0:T(8,128)(2,1)S(1)} collective-permute-done((f16[144,1024]{1,0:T(8,128)(2,1)S(1)}, f16[144,1024]{1,0:T(8,128)(2,1)S(1)}, u32[]{:S(2)}, u32[]{:S(2)}) %collective-permute-start.10) | collective-permute-done | bytes 294944 | tf_op jit(solution)/shard_map/ppermute | solution.py:365
  80.0 2.7 %collective-permute-start.14 = (f16[144,1024]{1,0:T(8,128)(2,1)S(1)}, f16[144,1024]{1,0:T(8,128)(2,1)S(1)}, u32[]{:S(2)}, u32[]{:S(2)}) collective-permute-start(f16[144,1024]{1,0:T(8,128)(2,1)S(1)} %add_convert_fusion.3), channel_id=1, source_target_pairs={{0,224},{32,0},{64,32},{96,64},{128,96},{160,128},{192,160},{224,1... | collective-permute-start | bytes 884744 | tf_op jit(solution)/shard_map/ppermute | solution.py:365
  82.7 0.8 collective-permute-done.7
  83.6 0.7 collective-permute-start.8
  84.3 9.4 %collective-permute-done.17 = f16[144,1024]{1,0:T(8,128)(2,1)S(1)} collective-permute-done((f16[144,1024]{1,0:T(8,128)(2,1)S(1)}, f16[144,1024]{1,0:T(8,128)(2,1)S(1)}, u32[]{:S(2)}, u32[]{:S(2)}) %collective-permute-start.17) | collective-permute-done | bytes 294944 | tf_op jit(solution)/shard_map/ppermute | solution.py:365
  93.9 2.2 %collective-permute-done.8 = f16[144,1024]{1,0:T(8,128)(2,1)S(1)} collective-permute-done((f16[144,1024]{1,0:T(8,128)(2,1)S(1)}, f16[144,1024]{1,0:T(8,128)(2,1)S(1)}, u32[]{:S(2)}, u32[]{:S(2)}) %collective-permute-start.8) | collective-permute-done | bytes 294944 | tf_op jit(solution)/shard_map/ppermute | solution.py:365
  96.1 4.6 %collective-permute-done.18 = f16[144,1024]{1,0:T(8,128)(2,1)S(1)} collective-permute-done((f16[144,1024]{1,0:T(8,128)(2,1)S(1)}, f16[144,1024]{1,0:T(8,128)(2,1)S(1)}, u32[]{:S(2)}, u32[]{:S(2)}) %collective-permute-start.18) | collective-permute-done | bytes 294944 | tf_op jit(solution)/shard_map/ppermute | solution.py:365
  100.7 0.4 multiply_convert_fusion
  101.2 2.7 %collective-permute-start.19 = (bf16[144,512]{1,0:T(8,128)(2,1)S(1)}, bf16[144,512]{1,0:T(8,128)(2,1)S(1)}, u32[]{:S(2)}, u32[]{:S(2)}) collective-permute-start(bf16[144,512]{1,0:T(8,128)(2,1)S(1)} %get-tuple-element.64.refs_2_), channel_id=1, source_target_pairs={{0,224},{32,0},{64,32},{96,64},{128,96},{160,128},{192,160},{224,1... | collective-permute-start | bytes 442376 | tf_op jit(solution)/shard_map/ppermute | solution.py:403
  103.9 1.4 collective-permute-start.23
  105.3 1.1 collective-permute-done.24.refs_5_
  106.4 2.7 %collective-permute-start.21 = (bf16[144,512]{1,0:T(8,128)(2,1)S(1)}, bf16[144,512]{1,0:T(8,128)(2,1)S(1)}, u32[]{:S(2)}, u32[]{:S(2)}) collective-permute-start(bf16[144,512]{1,0:T(8,128)(2,1)S(1)} %collective-permute-done.19.refs_0_), channel_id=1, source_target_pairs={{0,224},{32,0},{64,32},{96,64},{128,96},{160,128},{192,160},{224,1... | collective-permute-start | bytes 442376 | tf_op jit(solution)/shard_map/ppermute | solution.py:403
  109.1 1.6 collective-permute-start.22
  110.6 0.4 collective-permute-start.25
  111.1 1.4 collective-permute-done.26.refs_7_
  112.5 0.3 collective-permute-start.30
  112.8 3.4 %collective-permute-start.27 = (bf16[144,512]{1,0:T(8,128)(2,1)S(1)}, bf16[144,512]{1,0:T(8,128)(2,1)S(1)}, u32[]{:S(2)}, u32[]{:S(2)}) collective-permute-start(bf16[144,512]{1,0:T(8,128)(2,1)S(1)} %collective-permute-done.21.refs_2_), channel_id=1, source_target_pairs={{0,224},{32,0},{64,32},{96,64},{128,96},{160,128},{192,160},{224,1... | collective-permute-start | bytes 442376 | tf_op jit(solution)/shard_map/ppermute | solution.py:403
  116.1 2.5 %collective-permute-start.28 = (bf16[144,512]{1,0:T(8,128)(2,1)S(1)}, bf16[144,512]{1,0:T(8,128)(2,1)S(1)}, u32[]{:S(2)}, u32[]{:S(2)}) collective-permute-start(bf16[144,512]{1,0:T(8,128)(2,1)S(1)} %collective-permute-done.22.refs_3_), channel_id=1, source_target_pairs={{0,224},{32,0},{64,32},{96,64},{128,96},{160,128},{192,160},{224,1... | collective-permute-start | bytes 442376 | tf_op jit(solution)/shard_map/ppermute | solution.py:406
  118.6 0.5 collective-permute-done.30.refs_5_
  119.1 0.6 collective-permute-start.32
  119.8 3.4 %collective-permute-start.31 = (bf16[144,512]{1,0:T(8,128)(2,1)S(1)}, bf16[144,512]{1,0:T(8,128)(2,1)S(1)}, u32[]{:S(2)}, u32[]{:S(2)}) collective-permute-start(bf16[144,512]{1,0:T(8,128)(2,1)S(1)} %collective-permute-done.27.refs_0_), channel_id=1, source_target_pairs={{0,224},{32,0},{64,32},{96,64},{128,96},{160,128},{192,160},{224,1... | collective-permute-start | bytes 442376 | tf_op jit(solution)/shard_map/ppermute | solution.py:403
  123.2 2.4 %down_dots.2 = (f32[2,144,896]{2,1,0:T(8,128)S(1)}, bf16[2,144,896]{2,1,0:T(8,128)(2,1)S(1)}) custom-call(s32[1]{0:T(128)} %bitcast.1.c_ref, bf16[144,512]{1,0:T(8,128)(2,1)S(1)} %collective-permute-done.19.refs_0_, bf16[144,512]{1,0:T(8,128)(2,1)S(1)} %collective-permute-done.20.refs_1_, bf16[144,512]{1,0:T(8,128)(2,1)S(1)} %collective-permute-done.21.refs_2_, ...), custom_call_target="tpu_custom_call" | custom-call | flops 1056964608 | bytes 3670016 | tf_op jit(solution)/shard_map/down_dots/pallas_call | solution.py:221
  125.6 2.2 %collective-permute-done.32.refs_7_ = bf16[144,512]{1,0:T(8,128)(2,1)S(1)} collective-permute-done((bf16[144,512]{1,0:T(8,128)(2,1)S(1)}, bf16[144,512]{1,0:T(8,128)(2,1)S(1)}, u32[]{:S(2)}, u32[]{:S(2)}) %collective-permute-start.32) | collective-permute-done | bytes 147488 | tf_op jit(solution)/shard_map/ppermute | solution.py:404
  127.8 2.4 %down_dots.3 = (f32[2,144,896]{2,1,0:T(8,128)S(1)}, bf16[2,144,896]{2,1,0:T(8,128)(2,1)S(1)}) custom-call(s32[1]{0:T(128)} %bitcast.1.c_ref, bf16[144,512]{1,0:T(8,128)(2,1)S(1)} %collective-permute-done.27.refs_0_, bf16[144,512]{1,0:T(8,128)(2,1)S(1)} %collective-permute-done.28.refs_1_, bf16[144,512]{1,0:T(8,128)(2,1)S(1)} %get-tuple-element.64.refs_2_, ...), custom_call_target="tpu_custom_call" | custom-call | flops 1056964608 | bytes 3670016 | tf_op jit(solution)/shard_map/down_dots/pallas_call | solution.py:221
  130.2 0.1 pad_maximum_fusion.1
  130.4 7.9 %collective-permute-start.33 = (bf16[4,144,896]{2,1,0:T(8,128)(2,1)S(1)}, bf16[4,144,896]{2,1,0:T(8,128)(2,1)S(1)}, u32[]{:S(2)}, u32[]{:S(2)}) collective-permute-start(bf16[4,144,896]{2,1,0:T(8,128)(2,1)S(1)} %pad_maximum_fusion.1), channel_id=1, source_target_pairs={{0,1},{1,0},{2,3},{3,2},{4,5},{5,4},{6,7},{7,6},{8,9},{9,8},{10,11... | collective-permute-start | bytes 3096584 | tf_op jit(solution)/shard_map/ppermute | solution.py:417
  138.2 2.3 %collective-permute-done.33.came_ref = bf16[4,144,896]{2,1,0:T(8,128)(2,1)S(1)} collective-permute-done((bf16[4,144,896]{2,1,0:T(8,128)(2,1)S(1)}, bf16[4,144,896]{2,1,0:T(8,128)(2,1)S(1)}, u32[]{:S(2)}, u32[]{:S(2)}) %collective-permute-start.33) | collective-permute-done | bytes 1032224 | tf_op jit(solution)/shard_map/ppermute | solution.py:417
  140.5 1.2 settle.1
  141.7 3.6 %all-to-all-start.1 = ((bf16[16,32,896]{2,1,0:T(8,128)(2,1)}), bf16[16,32,896]{2,1,0:T(8,128)(2,1)S(1)}, u32[]{:S(2)}, u32[]{:S(2)}) async-start(bf16[16,32,896]{2,1,0:T(8,128)(2,1)} %get-tuple-element.61), calls=%async_computation.1 | async-start | bytes 1835008 | tf_op jit(solution)/shard_map/all_to_all | solution.py:419
  145.3 0.4 terms.1.terms_ref
  145.7 14.7 %all-to-all-done.1 = bf16[16,32,896]{2,1,0:T(8,128)(2,1)S(1)} async-done(((bf16[16,32,896]{2,1,0:T(8,128)(2,1)}), bf16[16,32,896]{2,1,0:T(8,128)(2,1)S(1)}, u32[]{:S(2)}, u32[]{:S(2)}) %all-to-all-start.1) | async-done | bytes 917536 | tf_op jit(solution)/shard_map/all_to_all | solution.py:419
  160.4 0.9 combine.1
  161.4 3.0 %collective-permute-start.34 = (bf16[16,896]{1,0:T(8,128)(2,1)S(1)}, bf16[16,896]{1,0:T(8,128)(2,1)S(1)}, u32[]{:S(2)}, u32[]{:S(2)}) collective-permute-start(bf16[16,896]{1,0:T(8,128)(2,1)S(1)} %get-tuple-element.68), channel_id=1, source_target_pairs={{0,32},{1,225},{32,64},{33,1},{64,96},{65,33},{96,128},{97,65},{12... | collective-permute-start | bytes 86024 | tf_op jit(solution)/shard_map/ppermute | solution.py:423
  164.4 4.0 %collective-permute-start.37 = (bf16[16,896]{1,0:T(8,128)(2,1)S(1)}, bf16[16,896]{1,0:T(8,128)(2,1)S(1)}, u32[]{:S(2)}, u32[]{:S(2)}) collective-permute-start(bf16[16,896]{1,0:T(8,128)(2,1)S(1)} %get-tuple-element.65), channel_id=1, source_target_pairs={{0,0},{1,129},{32,32},{33,161},{64,64},{65,193},{96,96},{97,225},{... | collective-permute-start | bytes 86024 | tf_op jit(solution)/shard_map/ppermute | solution.py:423
  168.4 0.7 collective-permute-start.36
  169.1 2.7 %collective-permute-start.35 = (bf16[16,896]{1,0:T(8,128)(2,1)S(1)}, bf16[16,896]{1,0:T(8,128)(2,1)S(1)}, u32[]{:S(2)}, u32[]{:S(2)}) collective-permute-start(bf16[16,896]{1,0:T(8,128)(2,1)S(1)} %get-tuple-element.67), channel_id=1, source_target_pairs={{0,64},{1,193},{32,96},{33,225},{64,128},{65,1},{96,160},{97,33},{... | collective-permute-start | bytes 86024 | tf_op jit(solution)/shard_map/ppermute | solution.py:423
  171.8 1.0 collective-permute-done.35
  172.8 0.5 collective-permute-done.36
  173.4 1.3 collective-permute-done.38.refs_1_
  174.8 1.3 assemble.1
  (67 shorter events, 2.1 us)
Async XLA Ops:
  1.8 11.7 %collective-permute-start = (bf16[16,1024]{1,0:T(8,128)(2,1)S(1)}, bf16[16,1024]{1,0:T(8,128)(2,1)S(1)}, u32[]{:S(2)}, u32[]{:S(2)}) collective-permute-start(bf16[16,1024]{1,0:T(8,128)(2,1)S(1)} %get-tuple-element.34), channel_id=1, source_target_pairs={{0,0},{1,129},{32,32},{33,161},{64,64},{65,193},{96,96},{97,225},{... | collective-permute-start | bytes 98312 | tf_op jit(solution)/shard_map/ppermute | solution.py:377
  11.4 4.1 %collective-permute-start.1 = (bf16[16,1024]{1,0:T(8,128)(2,1)S(1)}, bf16[16,1024]{1,0:T(8,128)(2,1)S(1)}, u32[]{:S(2)}, u32[]{:S(2)}) collective-permute-start(bf16[16,1024]{1,0:T(8,128)(2,1)S(1)} %get-tuple-element.35), channel_id=1, source_target_pairs={{0,224},{1,33},{32,0},{33,65},{64,32},{65,97},{96,64},{97,129},{12... | collective-permute-start | bytes 98312 | tf_op jit(solution)/shard_map/ppermute | solution.py:377
  12.3 4.9 %collective-permute-start.2 = (bf16[16,1024]{1,0:T(8,128)(2,1)S(1)}, bf16[16,1024]{1,0:T(8,128)(2,1)S(1)}, u32[]{:S(2)}, u32[]{:S(2)}) collective-permute-start(bf16[16,1024]{1,0:T(8,128)(2,1)S(1)} %get-tuple-element.36), channel_id=1, source_target_pairs={{0,192},{1,65},{32,224},{33,97},{64,0},{65,129},{96,32},{97,161},{... | collective-permute-start | bytes 98312 | tf_op jit(solution)/shard_map/ppermute | solution.py:377
  13.5 5.8 %collective-permute-start.3 = (bf16[16,1024]{1,0:T(8,128)(2,1)S(1)}, bf16[16,1024]{1,0:T(8,128)(2,1)S(1)}, u32[]{:S(2)}, u32[]{:S(2)}) collective-permute-start(bf16[16,1024]{1,0:T(8,128)(2,1)S(1)} %get-tuple-element.37), channel_id=1, source_target_pairs={{0,160},{1,97},{32,192},{33,129},{64,224},{65,161},{96,0},{97,193}... | collective-permute-start | bytes 98312 | tf_op jit(solution)/shard_map/ppermute | solution.py:377
  41.0 3.0 %copy-start.5 = (bf16[896,1024]{1,0:T(8,128)(2,1)S(1)}, bf16[896,1024]{1,0:T(8,128)(2,1)}, u32[]{:S(2)}) copy-start(bf16[896,1024]{1,0:T(8,128)(2,1)} %su_ref.3) | copy-start | bytes 5505028
  41.1 2.7 %collective-permute-start.4 = (bf16[576,896]{1,0:T(8,128)(2,1)S(1)}, bf16[576,896]{1,0:T(8,128)(2,1)S(1)}, u32[]{:S(2)}, u32[]{:S(2)}) collective-permute-start(bf16[576,896]{1,0:T(8,128)(2,1)S(1)} %pad_maximum_fusion), channel_id=1, source_target_pairs={{0,1},{1,0},{2,3},{3,2},{4,5},{5,4},{6,7},{7,6},{8,9},{9,8},{10,11... | collective-permute-start | bytes 3096584 | tf_op jit(solution)/shard_map/ppermute | solution.py:381
  41.2 2.8 %copy-start.4 = (bf16[896,1024]{1,0:T(8,128)(2,1)S(1)}, bf16[896,1024]{1,0:T(8,128)(2,1)}, u32[]{:S(2)}) copy-start(bf16[896,1024]{1,0:T(8,128)(2,1)} %sg_ref.3) | copy-start | bytes 5505028
  41.3 2.7 %copy-start.2 = (bf16[1,896,1024]{2,1,0:T(8,128)(2,1)S(1)}, bf16[1,896,1024]{2,1,0:T(8,128)(2,1)}, u32[]{:S(2)}) copy-start(bf16[1,896,1024]{2,1,0:T(8,128)(2,1)} %wg_ref.3) | copy-start | bytes 5505028
  41.3 2.9 %copy-start.3 = (bf16[1,896,1024]{2,1,0:T(8,128)(2,1)S(1)}, bf16[1,896,1024]{2,1,0:T(8,128)(2,1)}, u32[]{:S(2)}) copy-start(bf16[1,896,1024]{2,1,0:T(8,128)(2,1)} %wu_ref.3) | copy-start | bytes 5505028
  48.5 10.2 %collective-permute-start.15 = (f16[144,1024]{1,0:T(8,128)(2,1)S(1)}, f16[144,1024]{1,0:T(8,128)(2,1)S(1)}, u32[]{:S(2)}, u32[]{:S(2)}) collective-permute-start(f16[144,1024]{1,0:T(8,128)(2,1)S(1)} %convert_element_type.107), channel_id=1, source_target_pairs={{0,32},{32,64},{64,96},{96,128},{128,160},{160,192},{192,224},{224... | collective-permute-start | bytes 884744 | tf_op jit(solution)/shard_map/ppermute | solution.py:365
  50.5 9.0 %collective-permute-start.5 = (f16[144,1024]{1,0:T(8,128)(2,1)S(1)}, f16[144,1024]{1,0:T(8,128)(2,1)S(1)}, u32[]{:S(2)}, u32[]{:S(2)}) collective-permute-start(f16[144,1024]{1,0:T(8,128)(2,1)S(1)} %convert_element_type.87), channel_id=1, source_target_pairs={{0,224},{32,0},{64,32},{96,64},{128,96},{160,128},{192,160},{224,1... | collective-permute-start | bytes 884744 | tf_op jit(solution)/shard_map/ppermute | solution.py:365
  57.1 10.1 %collective-permute-start.12 = (f16[144,1024]{1,0:T(8,128)(2,1)S(1)}, f16[144,1024]{1,0:T(8,128)(2,1)S(1)}, u32[]{:S(2)}, u32[]{:S(2)}) collective-permute-start(f16[144,1024]{1,0:T(8,128)(2,1)S(1)} %convert_element_type.101), channel_id=1, source_target_pairs={{0,224},{32,0},{64,32},{96,64},{128,96},{160,128},{192,160},{224,1... | collective-permute-start | bytes 884744 | tf_op jit(solution)/shard_map/ppermute | solution.py:365
  58.3 8.6 %collective-permute-start.9 = (f16[144,1024]{1,0:T(8,128)(2,1)S(1)}, f16[144,1024]{1,0:T(8,128)(2,1)S(1)}, u32[]{:S(2)}, u32[]{:S(2)}) collective-permute-start(f16[144,1024]{1,0:T(8,128)(2,1)S(1)} %convert_element_type.95), channel_id=1, source_target_pairs={{0,32},{32,64},{64,96},{96,128},{128,160},{160,192},{192,224},{224... | collective-permute-start | bytes 884744 | tf_op jit(solution)/shard_map/ppermute | solution.py:365
  58.8 20.9 %collective-permute-start.16 = (f16[144,1024]{1,0:T(8,128)(2,1)S(1)}, f16[144,1024]{1,0:T(8,128)(2,1)S(1)}, u32[]{:S(2)}, u32[]{:S(2)}) collective-permute-start(f16[144,1024]{1,0:T(8,128)(2,1)S(1)} %add_convert_fusion.2), channel_id=1, source_target_pairs={{0,32},{32,64},{64,96},{96,128},{128,160},{160,192},{192,224},{224... | collective-permute-start | bytes 884744 | tf_op jit(solution)/shard_map/ppermute | solution.py:365
  59.6 11.9 %collective-permute-start.6 = (f16[144,1024]{1,0:T(8,128)(2,1)S(1)}, f16[144,1024]{1,0:T(8,128)(2,1)S(1)}, u32[]{:S(2)}, u32[]{:S(2)}) collective-permute-start(f16[144,1024]{1,0:T(8,128)(2,1)S(1)} %add_convert_fusion.9), channel_id=1, source_target_pairs={{0,224},{32,0},{64,32},{96,64},{128,96},{160,128},{192,160},{224,1... | collective-permute-start | bytes 884744 | tf_op jit(solution)/shard_map/ppermute | solution.py:365
  67.0 12.6 %collective-permute-start.10 = (f16[144,1024]{1,0:T(8,128)(2,1)S(1)}, f16[144,1024]{1,0:T(8,128)(2,1)S(1)}, u32[]{:S(2)}, u32[]{:S(2)}) collective-permute-start(f16[144,1024]{1,0:T(8,128)(2,1)S(1)} %add_convert_fusion.6), channel_id=1, source_target_pairs={{0,32},{32,64},{64,96},{96,128},{128,160},{160,192},{192,224},{224... | collective-permute-start | bytes 884744 | tf_op jit(solution)/shard_map/ppermute | solution.py:365
  67.3 12.6 %collective-permute-start.13 = (f16[144,1024]{1,0:T(8,128)(2,1)S(1)}, f16[144,1024]{1,0:T(8,128)(2,1)S(1)}, u32[]{:S(2)}, u32[]{:S(2)}) collective-permute-start(f16[144,1024]{1,0:T(8,128)(2,1)S(1)} %add_convert_fusion.4), channel_id=1, source_target_pairs={{0,224},{32,0},{64,32},{96,64},{128,96},{160,128},{192,160},{224,1... | collective-permute-start | bytes 884744 | tf_op jit(solution)/shard_map/ppermute | solution.py:365
  71.5 12.0 %collective-permute-start.7 = (f16[144,1024]{1,0:T(8,128)(2,1)S(1)}, f16[144,1024]{1,0:T(8,128)(2,1)S(1)}, u32[]{:S(2)}, u32[]{:S(2)}) collective-permute-start(f16[144,1024]{1,0:T(8,128)(2,1)S(1)} %add_convert_fusion.8), channel_id=1, source_target_pairs={{0,224},{32,0},{64,32},{96,64},{128,96},{160,128},{192,160},{224,1... | collective-permute-start | bytes 884744 | tf_op jit(solution)/shard_map/ppermute | solution.py:365
  79.6 14.3 %collective-permute-start.11 = (f16[144,1024]{1,0:T(8,128)(2,1)S(1)}, f16[144,1024]{1,0:T(8,128)(2,1)S(1)}, u32[]{:S(2)}, u32[]{:S(2)}) collective-permute-start(f16[144,1024]{1,0:T(8,128)(2,1)S(1)} %add_convert_fusion.5), channel_id=1, source_target_pairs={{0,32},{32,64},{64,96},{96,128},{128,160},{160,192},{192,224},{224... | collective-permute-start | bytes 884744 | tf_op jit(solution)/shard_map/ppermute | solution.py:365
  79.8 13.9 %collective-permute-start.17 = (f16[144,1024]{1,0:T(8,128)(2,1)S(1)}, f16[144,1024]{1,0:T(8,128)(2,1)S(1)}, u32[]{:S(2)}, u32[]{:S(2)}) collective-permute-start(f16[144,1024]{1,0:T(8,128)(2,1)S(1)} %add_convert_fusion.1), channel_id=1, source_target_pairs={{0,32},{32,64},{64,96},{96,128},{128,160},{160,192},{192,224},{224... | collective-permute-start | bytes 884744 | tf_op jit(solution)/shard_map/ppermute | solution.py:365
  80.0 13.9 %collective-permute-start.14 = (f16[144,1024]{1,0:T(8,128)(2,1)S(1)}, f16[144,1024]{1,0:T(8,128)(2,1)S(1)}, u32[]{:S(2)}, u32[]{:S(2)}) collective-permute-start(f16[144,1024]{1,0:T(8,128)(2,1)S(1)} %add_convert_fusion.3), channel_id=1, source_target_pairs={{0,224},{32,0},{64,32},{96,64},{128,96},{160,128},{192,160},{224,1... | collective-permute-start | bytes 884744 | tf_op jit(solution)/shard_map/ppermute | solution.py:365
  83.6 12.6 %collective-permute-start.8 = (f16[144,1024]{1,0:T(8,128)(2,1)S(1)}, f16[144,1024]{1,0:T(8,128)(2,1)S(1)}, u32[]{:S(2)}, u32[]{:S(2)}) collective-permute-start(f16[144,1024]{1,0:T(8,128)(2,1)S(1)} %add_convert_fusion.7), channel_id=1, source_target_pairs={{0,224},{32,0},{64,32},{96,64},{128,96},{160,128},{192,160},{224,1... | collective-permute-start | bytes 884744 | tf_op jit(solution)/shard_map/ppermute | solution.py:365
  93.7 29.5 %copy-start.1 = (bf16[1024,896]{1,0:T(8,128)(2,1)S(1)}, bf16[1024,896]{1,0:T(8,128)(2,1)}, u32[]{:S(2)}) copy-start(bf16[1024,896]{1,0:T(8,128)(2,1)} %refs_9_.3) | copy-start | bytes 5505028
  93.8 29.4 %copy-start = (bf16[1,1024,896]{2,1,0:T(8,128)(2,1)S(1)}, bf16[1,1024,896]{2,1,0:T(8,128)(2,1)}, u32[]{:S(2)}) copy-start(bf16[1,1024,896]{2,1,0:T(8,128)(2,1)} %refs_8_.3) | copy-start | bytes 5505028
  93.8 6.9 %collective-permute-start.18 = (f16[144,1024]{1,0:T(8,128)(2,1)S(1)}, f16[144,1024]{1,0:T(8,128)(2,1)S(1)}, u32[]{:S(2)}, u32[]{:S(2)}) collective-permute-start(f16[144,1024]{1,0:T(8,128)(2,1)S(1)} %add_convert_fusion), channel_id=1, source_target_pairs={{0,32},{32,64},{64,96},{96,128},{128,160},{160,192},{192,224},{224... | collective-permute-start | bytes 884744 | tf_op jit(solution)/shard_map/ppermute | solution.py:365
  101.1 5.3 %collective-permute-start.24 = (bf16[144,512]{1,0:T(8,128)(2,1)S(1)}, bf16[144,512]{1,0:T(8,128)(2,1)S(1)}, u32[]{:S(2)}, u32[]{:S(2)}) collective-permute-start(bf16[144,512]{1,0:T(8,128)(2,1)S(1)} %get-tuple-element.63.refs_3_), channel_id=1, source_target_pairs={{0,32},{32,64},{64,96},{96,128},{128,160},{160,192},{192,224},{224... | collective-permute-start | bytes 442376 | tf_op jit(solution)/shard_map/ppermute | solution.py:404
  101.2 5.2 %collective-permute-start.19 = (bf16[144,512]{1,0:T(8,128)(2,1)S(1)}, bf16[144,512]{1,0:T(8,128)(2,1)S(1)}, u32[]{:S(2)}, u32[]{:S(2)}) collective-permute-start(bf16[144,512]{1,0:T(8,128)(2,1)S(1)} %get-tuple-element.64.refs_2_), channel_id=1, source_target_pairs={{0,224},{32,0},{64,32},{96,64},{128,96},{160,128},{192,160},{224,1... | collective-permute-start | bytes 442376 | tf_op jit(solution)/shard_map/ppermute | solution.py:403
  103.8 5.2 %collective-permute-start.20 = (bf16[144,512]{1,0:T(8,128)(2,1)S(1)}, bf16[144,512]{1,0:T(8,128)(2,1)S(1)}, u32[]{:S(2)}, u32[]{:S(2)}) collective-permute-start(bf16[144,512]{1,0:T(8,128)(2,1)S(1)} %get-tuple-element.63.refs_3_), channel_id=1, source_target_pairs={{0,224},{32,0},{64,32},{96,64},{128,96},{160,128},{192,160},{224,1... | collective-permute-start | bytes 442376 | tf_op jit(solution)/shard_map/ppermute | solution.py:406
  103.9 6.8 %collective-permute-start.23 = (bf16[144,512]{1,0:T(8,128)(2,1)S(1)}, bf16[144,512]{1,0:T(8,128)(2,1)S(1)}, u32[]{:S(2)}, u32[]{:S(2)}) collective-permute-start(bf16[144,512]{1,0:T(8,128)(2,1)S(1)} %get-tuple-element.64.refs_2_), channel_id=1, source_target_pairs={{0,32},{32,64},{64,96},{96,128},{128,160},{160,192},{192,224},{224... | collective-permute-start | bytes 442376 | tf_op jit(solution)/shard_map/ppermute | solution.py:407
  106.4 6.1 %collective-permute-start.26 = (bf16[144,512]{1,0:T(8,128)(2,1)S(1)}, bf16[144,512]{1,0:T(8,128)(2,1)S(1)}, u32[]{:S(2)}, u32[]{:S(2)}) collective-permute-start(bf16[144,512]{1,0:T(8,128)(2,1)S(1)} %collective-permute-done.24.refs_5_), channel_id=1, source_target_pairs={{0,32},{32,64},{64,96},{96,128},{128,160},{160,192},{192,224},{224... | collective-permute-start | bytes 442376 | tf_op jit(solution)/shard_map/ppermute | solution.py:404
  106.4 6.4 %collective-permute-start.21 = (bf16[144,512]{1,0:T(8,128)(2,1)S(1)}, bf16[144,512]{1,0:T(8,128)(2,1)S(1)}, u32[]{:S(2)}, u32[]{:S(2)}) collective-permute-start(bf16[144,512]{1,0:T(8,128)(2,1)S(1)} %collective-permute-done.19.refs_0_), channel_id=1, source_target_pairs={{0,224},{32,0},{64,32},{96,64},{128,96},{160,128},{192,160},{224,1... | collective-permute-start | bytes 442376 | tf_op jit(solution)/shard_map/ppermute | solution.py:403
  109.1 7.1 %collective-permute-start.22 = (bf16[144,512]{1,0:T(8,128)(2,1)S(1)}, bf16[144,512]{1,0:T(8,128)(2,1)S(1)}, u32[]{:S(2)}, u32[]{:S(2)}) collective-permute-start(bf16[144,512]{1,0:T(8,128)(2,1)S(1)} %collective-permute-done.20.refs_1_), channel_id=1, source_target_pairs={{0,224},{32,0},{64,32},{96,64},{128,96},{160,128},{192,160},{224,1... | collective-permute-start | bytes 442376 | tf_op jit(solution)/shard_map/ppermute | solution.py:406
  110.6 8.0 %collective-permute-start.25 = (bf16[144,512]{1,0:T(8,128)(2,1)S(1)}, bf16[144,512]{1,0:T(8,128)(2,1)S(1)}, u32[]{:S(2)}, u32[]{:S(2)}) collective-permute-start(bf16[144,512]{1,0:T(8,128)(2,1)S(1)} %collective-permute-done.23.refs_4_), channel_id=1, source_target_pairs={{0,32},{32,64},{64,96},{96,128},{128,160},{160,192},{192,224},{224... | collective-permute-start | bytes 442376 | tf_op jit(solution)/shard_map/ppermute | solution.py:407
  112.5 6.6 %collective-permute-start.30 = (bf16[144,512]{1,0:T(8,128)(2,1)S(1)}, bf16[144,512]{1,0:T(8,128)(2,1)S(1)}, u32[]{:S(2)}, u32[]{:S(2)}) collective-permute-start(bf16[144,512]{1,0:T(8,128)(2,1)S(1)} %collective-permute-done.26.refs_7_), channel_id=1, source_target_pairs={{0,32},{32,64},{64,96},{96,128},{128,160},{160,192},{192,224},{224... | collective-permute-start | bytes 442376 | tf_op jit(solution)/shard_map/ppermute | solution.py:404
  112.8 7.0 %collective-permute-start.27 = (bf16[144,512]{1,0:T(8,128)(2,1)S(1)}, bf16[144,512]{1,0:T(8,128)(2,1)S(1)}, u32[]{:S(2)}, u32[]{:S(2)}) collective-permute-start(bf16[144,512]{1,0:T(8,128)(2,1)S(1)} %collective-permute-done.21.refs_2_), channel_id=1, source_target_pairs={{0,224},{32,0},{64,32},{96,64},{128,96},{160,128},{192,160},{224,1... | collective-permute-start | bytes 442376 | tf_op jit(solution)/shard_map/ppermute | solution.py:403
  116.1 9.5 %collective-permute-start.28 = (bf16[144,512]{1,0:T(8,128)(2,1)S(1)}, bf16[144,512]{1,0:T(8,128)(2,1)S(1)}, u32[]{:S(2)}, u32[]{:S(2)}) collective-permute-start(bf16[144,512]{1,0:T(8,128)(2,1)S(1)} %collective-permute-done.22.refs_3_), channel_id=1, source_target_pairs={{0,224},{32,0},{64,32},{96,64},{128,96},{160,128},{192,160},{224,1... | collective-permute-start | bytes 442376 | tf_op jit(solution)/shard_map/ppermute | solution.py:406
  118.6 7.0 %collective-permute-start.29 = (bf16[144,512]{1,0:T(8,128)(2,1)S(1)}, bf16[144,512]{1,0:T(8,128)(2,1)S(1)}, u32[]{:S(2)}, u32[]{:S(2)}) collective-permute-start(bf16[144,512]{1,0:T(8,128)(2,1)S(1)} %collective-permute-done.25.refs_6_), channel_id=1, source_target_pairs={{0,32},{32,64},{64,96},{96,128},{128,160},{160,192},{192,224},{224... | collective-permute-start | bytes 442376 | tf_op jit(solution)/shard_map/ppermute | solution.py:407
  119.1 8.7 %collective-permute-start.32 = (bf16[144,512]{1,0:T(8,128)(2,1)S(1)}, bf16[144,512]{1,0:T(8,128)(2,1)S(1)}, u32[]{:S(2)}, u32[]{:S(2)}) collective-permute-start(bf16[144,512]{1,0:T(8,128)(2,1)S(1)} %collective-permute-done.30.refs_5_), channel_id=1, source_target_pairs={{0,32},{32,64},{64,96},{96,128},{128,160},{160,192},{192,224},{224... | collective-permute-start | bytes 442376 | tf_op jit(solution)/shard_map/ppermute | solution.py:404
  119.8 8.0 %collective-permute-start.31 = (bf16[144,512]{1,0:T(8,128)(2,1)S(1)}, bf16[144,512]{1,0:T(8,128)(2,1)S(1)}, u32[]{:S(2)}, u32[]{:S(2)}) collective-permute-start(bf16[144,512]{1,0:T(8,128)(2,1)S(1)} %collective-permute-done.27.refs_0_), channel_id=1, source_target_pairs={{0,224},{32,0},{64,32},{96,64},{128,96},{160,128},{192,160},{224,1... | collective-permute-start | bytes 442376 | tf_op jit(solution)/shard_map/ppermute | solution.py:403
  130.4 10.1 %collective-permute-start.33 = (bf16[4,144,896]{2,1,0:T(8,128)(2,1)S(1)}, bf16[4,144,896]{2,1,0:T(8,128)(2,1)S(1)}, u32[]{:S(2)}, u32[]{:S(2)}) collective-permute-start(bf16[4,144,896]{2,1,0:T(8,128)(2,1)S(1)} %pad_maximum_fusion.1), channel_id=1, source_target_pairs={{0,1},{1,0},{2,3},{3,2},{4,5},{5,4},{6,7},{7,6},{8,9},{9,8},{10,11... | collective-permute-start | bytes 3096584 | tf_op jit(solution)/shard_map/ppermute | solution.py:417
  141.7 18.8 %all-to-all-start.1 = ((bf16[16,32,896]{2,1,0:T(8,128)(2,1)}), bf16[16,32,896]{2,1,0:T(8,128)(2,1)S(1)}, u32[]{:S(2)}, u32[]{:S(2)}) async-start(bf16[16,32,896]{2,1,0:T(8,128)(2,1)} %get-tuple-element.61), calls=%async_computation.1 | async-start | bytes 1835008 | tf_op jit(solution)/shard_map/all_to_all | solution.py:419
  161.4 10.4 %collective-permute-start.34 = (bf16[16,896]{1,0:T(8,128)(2,1)S(1)}, bf16[16,896]{1,0:T(8,128)(2,1)S(1)}, u32[]{:S(2)}, u32[]{:S(2)}) collective-permute-start(bf16[16,896]{1,0:T(8,128)(2,1)S(1)} %get-tuple-element.68), channel_id=1, source_target_pairs={{0,32},{1,225},{32,64},{33,1},{64,96},{65,33},{96,128},{97,65},{12... | collective-permute-start | bytes 86024 | tf_op jit(solution)/shard_map/ppermute | solution.py:423
  164.4 8.9 %collective-permute-start.37 = (bf16[16,896]{1,0:T(8,128)(2,1)S(1)}, bf16[16,896]{1,0:T(8,128)(2,1)S(1)}, u32[]{:S(2)}, u32[]{:S(2)}) collective-permute-start(bf16[16,896]{1,0:T(8,128)(2,1)S(1)} %get-tuple-element.65), channel_id=1, source_target_pairs={{0,0},{1,129},{32,32},{33,161},{64,64},{65,193},{96,96},{97,225},{... | collective-permute-start | bytes 86024 | tf_op jit(solution)/shard_map/ppermute | solution.py:423
  168.4 4.9 %collective-permute-start.36 = (bf16[16,896]{1,0:T(8,128)(2,1)S(1)}, bf16[16,896]{1,0:T(8,128)(2,1)S(1)}, u32[]{:S(2)}, u32[]{:S(2)}) collective-permute-start(bf16[16,896]{1,0:T(8,128)(2,1)S(1)} %get-tuple-element.66), channel_id=1, source_target_pairs={{0,96},{1,161},{32,128},{33,193},{64,160},{65,225},{96,192},{97,1}... | collective-permute-start | bytes 86024 | tf_op jit(solution)/shard_map/ppermute | solution.py:423
  169.1 3.7 %collective-permute-start.35 = (bf16[16,896]{1,0:T(8,128)(2,1)S(1)}, bf16[16,896]{1,0:T(8,128)(2,1)S(1)}, u32[]{:S(2)}, u32[]{:S(2)}) collective-permute-start(bf16[16,896]{1,0:T(8,128)(2,1)S(1)} %get-tuple-element.67), channel_id=1, source_target_pairs={{0,64},{1,193},{32,96},{33,225},{64,128},{65,1},{96,160},{97,33},{... | collective-permute-start | bytes 86024 | tf_op jit(solution)/shard_map/ppermute | solution.py:423
  173.3 1.4 collective-permute-start.38
